TPU v7x, 32 devices: a whole 2x2x4 slice. The times are simulated.
32 devices in a mesh: gx: 2 (over core), gy: 4 (over y, x), gz: 4 (over z).
Axes of the slice: x: 2, y: 2, z: 4, core: 2. Of those that a mesh axis runs over, the one named last changes fastest.
Arguments:
- pressure_rhs: float32 [32, 128, 2048], P('gx', 'gy', 'gz'), may hold values from -6 to 6
- shift_diag: float32 [32, 128, 2048], P('gx', 'gy', 'gz'), may hold values from 0.02 to 0.3
- positions: float32 [3, 262144], P(None, ('gx', 'gy', 'gz')), may hold values from -6 to 6
- normals: float32 [3, 262144], P(None, ('gx', 'gy', 'gz')), may hold values from -6 to 6
- tension: float32 [262144], P(('gx', 'gy', 'gz')), may hold values from 0.3 to 3
- edge_weight: float32 [6, 262144], P(None, ('gx', 'gy', 'gz')), may hold values from 0.5 to 2
- owner_map: int32 [262144, 1], P(('gx', 'gy', 'gz')), may hold values from 0 to 31; in each aligned block of 8192 rows (0 to 8191, 8192 to 16383, ...) at most 1024 rows name the same one
- cell_map: int32 [262144], P(('gx', 'gy', 'gz')), may hold values from 0 to 262143
- connectivity: int32 [6, 262144], P(None, ('gx', 'gy', 'gz')), may hold values from 0 to 262143, as said below
Outputs:
- pressure: float32 [32, 128, 2048], P('gx', 'gy', 'gz')
- surface_force: float32 [3, 262144], P(None, ('gx', 'gy', 'gz'))
Inputs may be any that keep to these rules, and one draw needn't show every extreme that they name: `connectivity`: each neighbour index differs from the point's own index by 1 to 64, counted cyclically over 262144; the distance 64 occurs. `owner_map`: among the points of one device no owner is named more than 1024 times, a bound that some block reaches.
All inputs are finite; a program needn't handle non-finite values.
Results may differ from a plain program's by a relative error of at most 0.0003.
Values sent between devices are 32-bit elements; how exact they have to be, the bound alone decides.
A program may use at most 192 MiB of HBM per device.

v0:
```python
import functools

import jax
import jax.numpy as jnp
from jax import lax
from jax.experimental import pallas as pl
from jax.experimental.pallas import tpu as pltpu
from jax.sharding import PartitionSpec as P

HALO = 64
SMOOTH = 3
COARSE_SMOOTH = 4


centre = 1.125
spread = 0.875


def padded_2(cells, sides, closed):
    for axis, dim, width in sides:
        count = lax.axis_size(axis)
        ends = count if closed else count - 1
        head = lax.slice_in_dim(cells, 0, width, axis=dim)
        tail = lax.slice_in_dim(cells, cells.shape[dim] - width, cells.shape[dim], axis=dim)
        cells = jnp.concatenate(
            [
                lax.ppermute(tail, axis, [(i, (i + 1) % count) for i in range(ends)]),
                cells,
                lax.ppermute(head, axis, [((i + 1) % count, i) for i in range(ends)]),
            ],
            axis=dim,
        )
    return cells


def factors(sweeps):
    ratio = centre / spread
    fac = 1.0 / ratio
    pairs = [(0.0, 1.0 / centre)]
    for _ in range(1, sweeps):
        fac_new = 1.0 / (2.0 * ratio - fac)
        pairs.append((fac_new * fac, 2.0 * fac_new / spread))
        fac = fac_new
    return pairs


def beside(ref, x, cells):
    ny, nz = cells.shape
    total = ref[x - 1] + ref[x + 1]
    total = total + pltpu.roll(cells, 1, 0) + pltpu.roll(cells, ny - 1, 0)
    return total + pltpu.roll(cells, 1, 1) + pltpu.roll(cells, nz - 1, 1)


def sweep(rhs, inverse, src, dst, update, first, last, pair, keep=None):
    old, new = pair

    def slab(x, carry):
        cells = src[x]
        change = new * (inverse[x] * (rhs[x] + beside(src, x, cells)) - cells)
        if old:
            change = change + old * update[x]
        if keep is None:
            update[x] = change
            dst[x] = cells + change
        else:
            keep(x, cells + change)
        return carry

    lax.fori_loop(first, last, slab, 0)


def begin(rhs, inverse, dst, update, slabs):
    def slab(x, carry):
        change = inverse[x] * rhs[x] * (1.0 / centre)
        update[x] = change
        dst[x] = change
        return carry

    lax.fori_loop(0, slabs, slab, 0)


def down_kernel(wx, wy, wz, rhs, inverse, shift, smooth, remain, one, update):
    slabs = rhs.shape[0]
    ny, nz = remain.shape[1:]
    pairs = factors(SMOOTH)
    bufs = (one, smooth) if SMOOTH % 2 == 0 else (smooth, one)
    begin(rhs, inverse, bufs[0], update, slabs)
    for k in range(1, SMOOTH):
        sweep(
            rhs, inverse, bufs[(k - 1) % 2], bufs[k % 2], update, k, slabs - k, pairs[k]
        )

    def slab(x, carry):
        cells = smooth[x]
        near = rhs[x] + beside(smooth, x, cells)
        core = (slice(wy, wy + ny), slice(wz, wz + nz))
        remain[x - wx] = near[core] - (6.0 + shift[x - wx]) * cells[core]
        return carry

    lax.fori_loop(wx, slabs - wx, slab, 0)


def up_kernel(
    wx, wy, wz, cx, coarse, rhs, inverse, smooth, pressure,
    fix_a, fix_b, fix_update, one, two, update,
):
    crhs, cinverse = coarse.at[0], coarse.at[1]
    cslabs, cny, cnz = fix_a.shape
    slabs, fny, fnz = one.shape
    ny, nz = pressure.shape[1:]
    pairs = factors(COARSE_SMOOTH)
    bufs = (fix_a, fix_b)
    begin(crhs, cinverse, fix_a, fix_update, cslabs)
    for k in range(1, COARSE_SMOOTH):
        sweep(
            crhs, cinverse, bufs[(k - 1) % 2], bufs[k % 2], fix_update, k, cslabs - k, pairs[k]
        )
    fix = bufs[(COARSE_SMOOTH - 1) % 2]

    low = cx - (SMOOTH + 1) // 2
    count = cslabs - 2 * low
    flat = fix[low : low + count].reshape(count * cny, cnz)

    def onehot(shape, offset_f, offset_c, fine_dim, fine_per, coarse_per):
        f = lax.broadcasted_iota(jnp.int32, shape, fine_dim)
        c = lax.broadcasted_iota(jnp.int32, shape, 1 - fine_dim)
        block, inner = 0, f
        for g in range(1, shape[fine_dim] // fine_per):
            block = block + (f >= g * fine_per).astype(jnp.int32)
        inner = f - block * fine_per
        half = jnp.right_shift(inner - offset_f + 2 * offset_c, 1)
        return (c == half + block * coarse_per).astype(jnp.float32).astype(jnp.bfloat16)

    fan_y = onehot((count * fny, count * cny), wy, wy, 0, fny, cny)
    fan_z = onehot((cnz, fnz), wz, wz, 1, fnz, cnz)
    tall = sum(
        jnp.dot(fan_y, piece, preferred_element_type=jnp.float32) for piece in split3(flat)
    )
    full = sum(
        jnp.dot(piece, fan_z, preferred_element_type=jnp.float32) for piece in split3(tall)
    )
    for j in range(count):
        part = full[j * fny : (j + 1) * fny]
        for half in range(2):
            x = wx + 2 * (low + j - cx) + half
            if wx - SMOOTH <= x < slabs - wx + SMOOTH:
                one[x] = smooth[x] + part

    pairs = factors(SMOOTH)
    bufs = (one, two)

    def keep(x, cells):
        pressure[x - wx] = cells[wy : wy + ny, wz : wz + nz]

    edge = wx - SMOOTH
    for k in range(SMOOTH):
        sweep(
            rhs, inverse, bufs[k % 2], bufs[(k + 1) % 2], update,
            edge + k + 1, slabs - edge - k - 1, pairs[k], keep if k == SMOOTH - 1 else None,
        )


LANES = 2 * HALO
HIGH = lax.Precision.HIGHEST


def pair_matrix(rows, cols, offset=0):
    r = lax.broadcasted_iota(jnp.int32, (rows, cols), 0)
    c = lax.broadcasted_iota(jnp.int32, (rows, cols), 1)
    return (r == (c + offset) // 2).astype(jnp.float32)


def pool(field):
    nx, ny, nz = field.shape
    halves = jnp.sum(field.reshape(nx // 2, 2, ny, nz), axis=1)
    flat = halves.reshape(nx // 2 * ny, nz)
    along_z = jnp.dot(flat, pair_matrix(nz // 2, nz).T, precision=HIGH)
    along_y = jnp.dot(
        pair_matrix(nx // 2 * ny // 2, nx // 2 * ny), along_z, precision=HIGH
    )
    return along_y.reshape(nx // 2, ny // 2, nz // 2)


def split3(x):
    a = x.astype(jnp.bfloat16)
    rest = x - a.astype(jnp.float32)
    b = rest.astype(jnp.bfloat16)
    c = (rest - b.astype(jnp.float32)).astype(jnp.bfloat16)
    return a, b, c


def points_kernel(
    ndevice, capacity, pos_ref, nrm_ref, ten_ref, wgt_ref, con_ref, own_ref, cel_ref,
    force_ref, packed_ref, carry_ref,
):
    step = pl.program_id(0)
    chunk = ten_ref.shape[1]

    @pl.when(step == 0)
    def _():
        packed_ref[...] = jnp.zeros_like(packed_ref)
        carry_ref[...] = jnp.zeros_like(carry_ref)

    jumps = []
    for sub in range(chunk // LANES):
        here = pl.ds(sub * LANES, LANES)
        base = pl.multiple_of(step * chunk + sub * LANES, LANES)
        lower = pos_ref[:, pl.ds(base, LANES)]
        upper = pos_ref[:, pl.ds(base + LANES, LANES)]
        centre_pos = jnp.concatenate([lower[:, HALO:], upper[:, :HALO]], axis=1)
        total = jnp.zeros_like(lower)
        for which in range(con_ref.shape[0]):
            index = con_ref[which : which + 1, here] - base
            wide = jnp.broadcast_to(index, lower.shape)
            low = jnp.bitwise_and(wide, LANES - 1)
            near = jnp.take_along_axis(lower, low, axis=1, mode="promise_in_bounds")
            far = jnp.take_along_axis(upper, low, axis=1, mode="promise_in_bounds")
            picked = jnp.where(wide < LANES, near, far)
            total = total + wgt_ref[which : which + 1, here] * (picked - centre_pos)
        force = ten_ref[:, here] * total[:3]
        force_ref[:, here] = force
        jumps.append(jnp.sum(force * nrm_ref[:, here], axis=0, keepdims=True))
    jump = jnp.concatenate(jumps, axis=1)

    hot = (lax.broadcasted_iota(jnp.int32, (ndevice, chunk), 0) == own_ref[...]).astype(jnp.float32)
    hot_half = hot.astype(jnp.bfloat16)
    before = (
        lax.broadcasted_iota(jnp.int32, (chunk, chunk), 0)
        < lax.broadcasted_iota(jnp.int32, (chunk, chunk), 1)
    ).astype(jnp.bfloat16)
    earlier = jnp.dot(hot_half, before, preferred_element_type=jnp.float32) + carry_ref[...]
    rank = jnp.sum(hot * earlier, axis=0, keepdims=True).astype(jnp.int32)
    carry_ref[...] = carry_ref[...] + jnp.sum(hot, axis=1, keepdims=True)
    slots = (
        lax.broadcasted_iota(jnp.int32, (capacity, chunk), 0) == rank
    ).astype(jnp.float32).astype(jnp.bfloat16)
    cell = cel_ref[...]
    parts = [piece.astype(jnp.float32) for piece in split3(jump)]
    for bits in (0, 8, 16):
        piece = jnp.bitwise_and(jnp.right_shift(cell, bits), 255).astype(jnp.float32)
        parts.append(piece)
    left = jnp.concatenate([(hot * part).astype(jnp.bfloat16) for part in parts], axis=0)
    packed = lax.dot_general(
        left, slots, (((1,), (1,)), ((), ())), preferred_element_type=jnp.float32
    )
    n = ndevice
    values = packed[0:n] + packed[n : 2 * n] + packed[2 * n : 3 * n]
    cells = packed[3 * n : 4 * n] + 256.0 * packed[4 * n : 5 * n] + 65536.0 * packed[5 * n :]
    packed_ref[:, :capacity] += values
    packed_ref[:, capacity:] += cells


def points(padded, normals, tension, edge_weight, relative, owner_ids, cell_map, ndevice, capacity):
    npoint = tension.shape[0]
    chunk = 4 * LANES if npoint % (4 * LANES) == 0 else LANES
    padded = jnp.concatenate([padded, jnp.zeros((5, padded.shape[1]), jnp.float32)], axis=0)
    neigh = relative.shape[0]

    def rows(count):
        return pl.BlockSpec((count, chunk), lambda i: (0, i))

    return pl.pallas_call(
        functools.partial(points_kernel, ndevice, capacity),
        grid=(npoint // chunk,),
        in_specs=[
            pl.BlockSpec(padded.shape, lambda i: (0, 0)),
            rows(3), rows(1), rows(neigh), rows(neigh), rows(1), rows(1),
        ],
        out_specs=[rows(3), pl.BlockSpec((ndevice, 2 * capacity), lambda i: (0, 0))],
        out_shape=[
            jax.ShapeDtypeStruct((3, npoint), jnp.float32),
            jax.ShapeDtypeStruct((ndevice, 2 * capacity), jnp.float32),
        ],
        scratch_shapes=[pltpu.VMEM((ndevice, 1), jnp.float32)],
        cost_estimate=pl.CostEstimate(
            flops=2 * npoint * capacity * 6 * ndevice, bytes_accessed=40000000, transcendentals=0
        ),
    )(
        padded, normals, tension[None], edge_weight, relative, owner_ids[None], cell_map[None]
    )


def scatter_kernel(rhs_ref, val_ref, row_ref, col_ref, out_ref):
    @pl.when(pl.program_id(0) == 0)
    def _():
        out_ref[...] = rhs_ref[...]

    nrow, ncol = out_ref.shape
    count = val_ref.shape[2]
    value = val_ref[0]
    first = value.astype(jnp.bfloat16)
    second = (value - first.astype(jnp.float32)).astype(jnp.bfloat16)
    by_row = (
        (lax.broadcasted_iota(jnp.int32, (nrow, count), 0) == row_ref[0])
        .astype(jnp.float32)
        .astype(jnp.bfloat16)
    )
    same = lax.broadcasted_iota(jnp.int32, (ncol, count), 0) == col_ref[0]
    total = out_ref[...]
    for piece in (first, second):
        by_col = jnp.where(same, piece.astype(jnp.float32), 0.0).astype(jnp.bfloat16)
        total = total + lax.dot_general(
            by_row, by_col, (((1,), (1,)), ((), ())), preferred_element_type=jnp.float32
        )
    out_ref[...] = total


def scatter(rhs, values, cells):
    nx, ny, nz = rhs.shape
    nrow = nx * ny
    sources, count = values.shape
    rows = cells // nz
    cols = cells - rows * nz
    one = pl.BlockSpec((1, 1, count), lambda i: (i, 0, 0))
    whole = pl.BlockSpec((nrow, nz), lambda i: (0, 0))
    out = pl.pallas_call(
        scatter_kernel,
        grid=(sources,),
        in_specs=[whole, one, one, one],
        out_specs=whole,
        out_shape=jax.ShapeDtypeStruct((nrow, nz), jnp.float32),
        cost_estimate=pl.CostEstimate(
            flops=4 * nrow * nz * sources * count, bytes_accessed=4000000, transcendentals=0
        ),
    )(rhs.reshape(nrow, nz), values[:, None], rows[:, None], cols[:, None])
    return out.reshape(nx, ny, nz)


def body(
    pressure_rhs,
    shift_diag,
    positions,
    normals,
    tension,
    edge_weight,
    owner_map,
    cell_map,
    connectivity,
):
    npoint = positions.shape[1]
    ndevice = lax.axis_size(("gx", "gy", "gz"))
    total = npoint * ndevice
    begin = lax.axis_index(("gx", "gy", "gz")) * npoint
    padded = padded_2(positions, ((("gx", "gy", "gz"), 1, HALO),), True)
    relative = (connectivity - begin + HALO + total) % total
    capacity = 4 * npoint // ndevice
    surface_force, packed = points(
        padded, normals, tension, edge_weight, relative, owner_map[:, 0], cell_map,
        ndevice, capacity,
    )
    got = lax.all_to_all(packed, ("gx", "gy", "gz"), split_axis=0, concat_axis=0, tiled=True)
    forcing = scatter(pressure_rhs, got[:, :capacity], got[:, capacity:].astype(jnp.int32))

    nx, ny, nz = pressure_rhs.shape
    wx, wy, wz = 2 * SMOOTH - 1, 8, 128
    cx = COARSE_SMOOTH - 1 + (SMOOTH + 1) // 2
    sides = (("gz", 2, wz), ("gy", 1, wy), ("gx", 0, wx))
    coarse_sides = (("gz", 3, wz), ("gy", 2, wy), ("gx", 1, cx))
    coarse_shift = 0.5 * pool(shift_diag)
    inverse = padded_2(1.0 / (6.0 + shift_diag), sides, False)
    rhs = padded_2(forcing, sides, False)
    wide = jax.ShapeDtypeStruct(rhs.shape, jnp.float32)
    core = jax.ShapeDtypeStruct(pressure_rhs.shape, jnp.float32)
    vmem = pl.BlockSpec(memory_space=pltpu.VMEM)
    wide_buf = pltpu.VMEM(rhs.shape, jnp.float32)
    smooth, remain = pl.pallas_call(
        functools.partial(down_kernel, wx, wy, wz),
        in_specs=[vmem] * 3,
        out_specs=[vmem] * 2,
        out_shape=[wide, core],
        scratch_shapes=[wide_buf] * 2,
    )(rhs, inverse, shift_diag)
    coarse = padded_2(
        jnp.stack([0.5 * pool(remain), 1.0 / (6.0 + coarse_shift)]), coarse_sides, False
    )
    fix_buf = pltpu.VMEM(coarse.shape[1:], jnp.float32)
    pressure = pl.pallas_call(
        functools.partial(up_kernel, wx, wy, wz, cx),
        in_specs=[vmem] * 4,
        out_specs=vmem,
        out_shape=core,
        scratch_shapes=[fix_buf] * 3 + [wide_buf] * 3,
    )(coarse, rhs, inverse, smooth)
    return (pressure, surface_force)


def solution(mesh):
    return jax.shard_map(
        body,
        mesh=mesh,
        in_specs=(
            P("gx", "gy", "gz"),
            P("gx", "gy", "gz"),
            P(None, ("gx", "gy", "gz")),
            P(None, ("gx", "gy", "gz")),
            P(("gx", "gy", "gz")),
            P(None, ("gx", "gy", "gz")),
            P(("gx", "gy", "gz"), None),
            P(("gx", "gy", "gz")),
            P(None, ("gx", "gy", "gz")),
        ),
        out_specs=(P("gx", "gy", "gz"), P(None, ("gx", "gy", "gz"))),
        check_vma=False,
    )
```

profile of v0, /device:TPU:0, one launch (start us, length us, event | category | flops | bytes accessed | tf_op | source)
XLA Modules:
  0.0 220.2 jit_solution(13432621911680485201)
XLA Ops:
  0.6 0.8 fusion.28
  1.4 6.4 %collective-permute-start.1 = (f32[3,64]{1,0:T(4,128)S(1)}, f32[3,64]{1,0:T(4,128)S(1)}, u32[]{:S(2)}, u32[]{:S(2)}) collective-permute-start(f32[3,64]{1,0:T(4,128)S(1)} %get-tuple-element.30), channel_id=1, source_target_pairs={{1,0},{2,1},{3,2},{4,3},{5,4},{6,5},{7,6},{8,7},{9,8},{10,9},{11,1... | collective-permute-start | bytes 2312 | tf_op jit(solution)/shard_map/ppermute | solution.py:29
  7.8 1.8 add_select_fusion.con_ref
  9.6 4.8 %collective-permute-done = f32[3,64]{1,0:T(4,128)S(1)} collective-permute-done((f32[3,64]{1,0:T(4,128)S(1)}, f32[3,64]{1,0:T(4,128)S(1)}, u32[]{:S(2)}, u32[]{:S(2)}) %collective-permute-start) | collective-permute-done | bytes 800 | tf_op jit(solution)/shard_map/ppermute | solution.py:27
  14.4 1.1 concatenate.33
  15.5 0.7 concatenate.34.pos_ref
  16.2 15.1 %shard_map.104 = (f32[3,8192]{1,0:T(4,128)}, f32[32,2048]{1,0:T(8,128)}) custom-call(f32[8,8320]{1,0:T(8,128)} %concatenate.34.pos_ref, f32[3,8192]{1,0:T(4,128)} %nrm_ref.1, f32[1,8192]{1,0:T(1,128)} %bitcast.43, f32[6,8192]{1,0:T(8,128)} %wgt_ref.1, s32[6,8192]{1,0:T(8,128)} %add_select_fusion.con_ref, s32[1,8192]{1,0:T(1,128)} %bitcast.44, s32[1,8192]{1,0:T(1,128)} %bitcast.45), custom_call_target="tpu_custom_call" | custom-call | flops 3221225472 | bytes 40000000 | tf_op jit(solution)/shard_map/pallas_call | solution.py:262
  31.3 1.9 copy.13
  33.3 2.6 %all-to-all-start = ((f32[32,1,2048]{2,1,0:T(1,128)}), f32[32,1,2048]{2,1,0:T(1,128)S(1)}, u32[]{:S(2)}, u32[]{:S(2)}) async-start(f32[32,1,2048]{2,1,0:T(1,128)} %copy.13), calls=%async_computation | async-start | bytes 524288 | tf_op jit(solution)/shard_map/all_to_all | solution.py:351
  36.1 3.6 %collective-permute-start.8 = (f32[16,32,128]{2,1,0:T(8,128)S(1)}, f32[16,32,128]{2,1,0:T(8,128)S(1)}, u32[]{:S(2)}, u32[]{:S(2)}) collective-permute-start(f32[16,32,128]{2,1,0:T(8,128)S(1)} %get-tuple-element.20), channel_id=1, source_target_pairs={{0,1},{1,2},{2,3},{4,5},{5,6},{6,7},{8,9},{9,10},{10,11},{12,13},{... | collective-permute-start | bytes 786440 | tf_op jit(solution)/shard_map/ppermute | solution.py:27
  39.7 1.3 collective-permute-start.9
  41.0 5.8 %all-to-all-done = f32[32,1,2048]{2,1,0:T(1,128)S(1)} async-done(((f32[32,1,2048]{2,1,0:T(1,128)}), f32[32,1,2048]{2,1,0:T(1,128)S(1)}, u32[]{:S(2)}, u32[]{:S(2)}) %all-to-all-start) | async-done | bytes 262176 | tf_op jit(solution)/shard_map/all_to_all | solution.py:351
  47.0 0.8 copy.14.val_ref
  47.8 0.7 broadcast_in_dim.20.col_ref
  48.5 0.8 copy.15.row_ref
  49.3 46.5 %shard_map.105 = f32[512,512]{1,0:T(8,128)} custom-call(f32[512,512]{1,0:T(8,128)} %bitcast.42, f32[32,1,1024]{2,1,0:T(1,128)} %copy.14.val_ref, s32[32,1,1024]{2,1,0:T(1,128)} %copy.15.row_ref, s32[32,1,1024]{2,1,0:T(1,128)} %broadcast_in_dim.20.col_ref), custom_call_target="tpu_custom_call" | custom-call | flops 34359738368 | bytes 4000000 | tf_op jit(solution)/shard_map/pallas_call | solution.py:316
  95.7 1.2 fusion.26
  96.9 1.9 collective-permute-start.2
  98.8 1.3 collective-permute-start.3
  100.3 3.0 %collective-permute-start.10 = (f32[16,8,768]{2,1,0:T(8,128)S(1)}, f32[16,8,768]{2,1,0:T(8,128)S(1)}, u32[]{:S(2)}, u32[]{:S(2)}) collective-permute-start(f32[16,8,768]{2,1,0:T(8,128)S(1)} %get-tuple-element.14), channel_id=1, source_target_pairs={{0,4},{4,8},{8,12},{1,5},{5,9},{9,13},{2,6},{6,10},{10,14},{3,7},{... | collective-permute-start | bytes 1179656 | tf_op jit(solution)/shard_map/ppermute | solution.py:27
  103.3 1.3 collective-permute-start.11
  104.6 0.8 collective-permute-done.2
  105.4 4.1 %collective-permute-done.3 = f32[16,32,128]{2,1,0:T(8,128)S(1)} collective-permute-done((f32[16,32,128]{2,1,0:T(8,128)S(1)}, f32[16,32,128]{2,1,0:T(8,128)S(1)}, u32[]{:S(2)}, u32[]{:S(2)}) %collective-permute-start.3) | collective-permute-done | bytes 262176 | tf_op jit(solution)/shard_map/ppermute | solution.py:29
  109.6 1.3 collective-permute-start.4
  110.9 1.3 collective-permute-start.5
  112.2 11.4 %collective-permute-done.11 = f32[16,8,768]{2,1,0:T(8,128)S(1)} collective-permute-done((f32[16,8,768]{2,1,0:T(8,128)S(1)}, f32[16,8,768]{2,1,0:T(8,128)S(1)}, u32[]{:S(2)}, u32[]{:S(2)}) %collective-permute-start.11) | collective-permute-done | bytes 393248 | tf_op jit(solution)/shard_map/ppermute | solution.py:29
  123.7 1.3 collective-permute-start.12
  125.1 1.3 collective-permute-start.13
  126.4 11.6 %collective-permute-done.5 = f32[16,8,768]{2,1,0:T(8,128)S(1)} collective-permute-done((f32[16,8,768]{2,1,0:T(8,128)S(1)}, f32[16,8,768]{2,1,0:T(8,128)S(1)}, u32[]{:S(2)}, u32[]{:S(2)}) %collective-permute-start.5) | collective-permute-done | bytes 393248 | tf_op jit(solution)/shard_map/ppermute | solution.py:29
  138.1 1.3 collective-permute-start.6
  139.5 1.3 collective-permute-start.7
  141.5 2.1 pad_maximum_fusion.1.inverse
  143.7 2.2 pad_maximum_fusion.rhs
  145.8 15.4 %shard_map.106 = (f32[26,48,768]{2,1,0:T(8,128)}, f32[16,32,512]{2,1,0:T(8,128)}) custom-call(f32[26,48,768]{2,1,0:T(8,128)} %pad_maximum_fusion.rhs, f32[26,48,768]{2,1,0:T(8,128)} %pad_maximum_fusion.1.inverse, f32[16,32,512]{2,1,0:T(8,128)} %shift.1), custom_call_target="tpu_custom_call" | custom-call | tf_op jit(solution)/shard_map/pallas_call | solution.py:366
  161.2 1.4 bitcast_reduce_fusion.1
  163.3 4.3 %collective-permute-start.14 = (f32[2,8,16,128]{3,2,1,0:T(8,128)S(1)}, f32[2,8,16,128]{3,2,1,0:T(8,128)S(1)}, u32[]{:S(2)}, u32[]{:S(2)}) collective-permute-start(f32[2,8,16,128]{3,2,1,0:T(8,128)S(1)} %get-tuple-element.26), channel_id=1, source_target_pairs={{0,1},{1,2},{2,3},{4,5},{5,6},{6,7},{8,9},{9,10},{10,11},{12,13},{... | collective-permute-start | bytes 393224 | tf_op jit(solution)/shard_map/ppermute | solution.py:27
  167.6 1.3 collective-permute-start.15
  168.9 2.4 %collective-permute-done.14 = f32[2,8,16,128]{3,2,1,0:T(8,128)S(1)} collective-permute-done((f32[2,8,16,128]{3,2,1,0:T(8,128)S(1)}, f32[2,8,16,128]{3,2,1,0:T(8,128)S(1)}, u32[]{:S(2)}, u32[]{:S(2)}) %collective-permute-start.14) | collective-permute-done | bytes 131104 | tf_op jit(solution)/shard_map/ppermute | solution.py:27
  171.2 4.5 %collective-permute-done.15 = f32[2,8,16,128]{3,2,1,0:T(8,128)S(1)} collective-permute-done((f32[2,8,16,128]{3,2,1,0:T(8,128)S(1)}, f32[2,8,16,128]{3,2,1,0:T(8,128)S(1)}, u32[]{:S(2)}, u32[]{:S(2)}) %collective-permute-start.15) | collective-permute-done | bytes 131104 | tf_op jit(solution)/shard_map/ppermute | solution.py:29
  175.8 3.0 %collective-permute-start.16 = (f32[2,8,8,512]{3,2,1,0:T(8,128)S(1)}, f32[2,8,8,512]{3,2,1,0:T(8,128)S(1)}, u32[]{:S(2)}, u32[]{:S(2)}) collective-permute-start(f32[2,8,8,512]{3,2,1,0:T(8,128)S(1)} %get-tuple-element.24), channel_id=1, source_target_pairs={{0,4},{4,8},{8,12},{1,5},{5,9},{9,13},{2,6},{6,10},{10,14},{3,7},{... | collective-permute-start | bytes 786440 | tf_op jit(solution)/shard_map/ppermute | solution.py:27
  178.8 1.3 collective-permute-start.17
  180.1 4.4 %collective-permute-done.16 = f32[2,8,8,512]{3,2,1,0:T(8,128)S(1)} collective-permute-done((f32[2,8,8,512]{3,2,1,0:T(8,128)S(1)}, f32[2,8,8,512]{3,2,1,0:T(8,128)S(1)}, u32[]{:S(2)}, u32[]{:S(2)}) %collective-permute-start.16) | collective-permute-done | bytes 262176 | tf_op jit(solution)/shard_map/ppermute | solution.py:27
  184.5 6.4 %collective-permute-done.17 = f32[2,8,8,512]{3,2,1,0:T(8,128)S(1)} collective-permute-done((f32[2,8,8,512]{3,2,1,0:T(8,128)S(1)}, f32[2,8,8,512]{3,2,1,0:T(8,128)S(1)}, u32[]{:S(2)}, u32[]{:S(2)}) %collective-permute-start.17) | collective-permute-done | bytes 262176 | tf_op jit(solution)/shard_map/ppermute | solution.py:29
  191.2 1.4 collective-permute-start.18
  192.6 1.5 collective-permute-start.19
  194.2 2.3 %collective-permute-done.19 = f32[2,5,32,512]{3,2,1,0:T(8,128)S(1)} collective-permute-done((f32[2,5,32,512]{3,2,1,0:T(8,128)S(1)}, f32[2,5,32,512]{3,2,1,0:T(8,128)S(1)}, u32[]{:S(2)}, u32[]{:S(2)}) %collective-permute-start.19) | collective-permute-done | bytes 655392 | tf_op jit(solution)/shard_map/ppermute | solution.py:29
  196.6 1.7 pad_maximum_fusion.2.coarse
  198.3 21.9 %shard_map.107 = f32[16,32,512]{2,1,0:T(8,128)} custom-call(f32[2,18,32,512]{3,2,1,0:T(8,128)} %pad_maximum_fusion.2.coarse, f32[26,48,768]{2,1,0:T(8,128)} %pad_maximum_fusion.rhs, f32[26,48,768]{2,1,0:T(8,128)} %pad_maximum_fusion.1.inverse, f32[26,48,768]{2,1,0:T(8,128)} %get-tuple-element.8.smooth), custom_call_target="tpu_custom_call" | custom-call | tf_op jit(solution)/shard_map/pallas_call | solution.py:377
  (38 shorter events, 2.8 us)
Async XLA Ops:
  1.4 8.2 %collective-permute-start.1 = (f32[3,64]{1,0:T(4,128)S(1)}, f32[3,64]{1,0:T(4,128)S(1)}, u32[]{:S(2)}, u32[]{:S(2)}) collective-permute-start(f32[3,64]{1,0:T(4,128)S(1)} %get-tuple-element.30), channel_id=1, source_target_pairs={{1,0},{2,1},{3,2},{4,3},{5,4},{6,5},{7,6},{8,7},{9,8},{10,9},{11,1... | collective-permute-start | bytes 2312 | tf_op jit(solution)/shard_map/ppermute | solution.py:29
  7.8 6.6 %collective-permute-start = (f32[3,64]{1,0:T(4,128)S(1)}, f32[3,64]{1,0:T(4,128)S(1)}, u32[]{:S(2)}, u32[]{:S(2)}) collective-permute-start(f32[3,64]{1,0:T(4,128)S(1)} %get-tuple-element.31), channel_id=1, source_target_pairs={{0,1},{1,2},{2,3},{3,4},{4,5},{5,6},{6,7},{7,8},{8,9},{9,10},{10,1... | collective-permute-start | bytes 2312 | tf_op jit(solution)/shard_map/ppermute | solution.py:27
  16.2 19.6 %copy-start.1 = (f32[16,32,512]{2,1,0:T(8,128)S(1)}, f32[16,32,512]{2,1,0:T(8,128)}, u32[]{:S(2)}) copy-start(f32[16,32,512]{2,1,0:T(8,128)} %shift.1) | copy-start | bytes 3145732
  33.3 13.5 %all-to-all-start = ((f32[32,1,2048]{2,1,0:T(1,128)}), f32[32,1,2048]{2,1,0:T(1,128)S(1)}, u32[]{:S(2)}, u32[]{:S(2)}) async-start(f32[32,1,2048]{2,1,0:T(1,128)} %copy.13), calls=%async_computation | async-start | bytes 524288 | tf_op jit(solution)/shard_map/all_to_all | solution.py:351
  36.1 64.1 %collective-permute-start.8 = (f32[16,32,128]{2,1,0:T(8,128)S(1)}, f32[16,32,128]{2,1,0:T(8,128)S(1)}, u32[]{:S(2)}, u32[]{:S(2)}) collective-permute-start(f32[16,32,128]{2,1,0:T(8,128)S(1)} %get-tuple-element.20), channel_id=1, source_target_pairs={{0,1},{1,2},{2,3},{4,5},{5,6},{6,7},{8,9},{9,10},{10,11},{12,13},{... | collective-permute-start | bytes 786440 | tf_op jit(solution)/shard_map/ppermute | solution.py:27
  39.7 60.5 %collective-permute-start.9 = (f32[16,32,128]{2,1,0:T(8,128)S(1)}, f32[16,32,128]{2,1,0:T(8,128)S(1)}, u32[]{:S(2)}, u32[]{:S(2)}) collective-permute-start(f32[16,32,128]{2,1,0:T(8,128)S(1)} %get-tuple-element.21), channel_id=1, source_target_pairs={{1,0},{2,1},{3,2},{5,4},{6,5},{7,6},{9,8},{10,9},{11,10},{13,12},{... | collective-permute-start | bytes 786440 | tf_op jit(solution)/shard_map/ppermute | solution.py:29
  95.7 13.8 %copy-start = (f32[512,512]{1,0:T(8,128)S(1)}, f32[512,512]{1,0:T(8,128)}, u32[]{:S(2)}) copy-start(f32[512,512]{1,0:T(8,128)} %shard_map.105) | copy-start | bytes 3145732
  96.9 8.5 %collective-permute-start.2 = (f32[16,32,128]{2,1,0:T(8,128)S(1)}, f32[16,32,128]{2,1,0:T(8,128)S(1)}, u32[]{:S(2)}, u32[]{:S(2)}) collective-permute-start(f32[16,32,128]{2,1,0:T(8,128)S(1)} %get-tuple-element.22), channel_id=1, source_target_pairs={{0,1},{1,2},{2,3},{4,5},{5,6},{6,7},{8,9},{9,10},{10,11},{12,13},{... | collective-permute-start | bytes 786440 | tf_op jit(solution)/shard_map/ppermute | solution.py:27
  98.8 10.7 %collective-permute-start.3 = (f32[16,32,128]{2,1,0:T(8,128)S(1)}, f32[16,32,128]{2,1,0:T(8,128)S(1)}, u32[]{:S(2)}, u32[]{:S(2)}) collective-permute-start(f32[16,32,128]{2,1,0:T(8,128)S(1)} %get-tuple-element.23), channel_id=1, source_target_pairs={{1,0},{2,1},{3,2},{5,4},{6,5},{7,6},{9,8},{10,9},{11,10},{13,12},{... | collective-permute-start | bytes 786440 | tf_op jit(solution)/shard_map/ppermute | solution.py:29
  100.3 11.9 %collective-permute-start.10 = (f32[16,8,768]{2,1,0:T(8,128)S(1)}, f32[16,8,768]{2,1,0:T(8,128)S(1)}, u32[]{:S(2)}, u32[]{:S(2)}) collective-permute-start(f32[16,8,768]{2,1,0:T(8,128)S(1)} %get-tuple-element.14), channel_id=1, source_target_pairs={{0,4},{4,8},{8,12},{1,5},{5,9},{9,13},{2,6},{6,10},{10,14},{3,7},{... | collective-permute-start | bytes 1179656 | tf_op jit(solution)/shard_map/ppermute | solution.py:27
  103.3 20.3 %collective-permute-start.11 = (f32[16,8,768]{2,1,0:T(8,128)S(1)}, f32[16,8,768]{2,1,0:T(8,128)S(1)}, u32[]{:S(2)}, u32[]{:S(2)}) collective-permute-start(f32[16,8,768]{2,1,0:T(8,128)S(1)} %get-tuple-element.15), channel_id=1, source_target_pairs={{4,0},{8,4},{12,8},{5,1},{9,5},{13,9},{6,2},{10,6},{14,10},{7,3},{... | collective-permute-start | bytes 1179656 | tf_op jit(solution)/shard_map/ppermute | solution.py:29
  109.6 16.8 %collective-permute-start.4 = (f32[16,8,768]{2,1,0:T(8,128)S(1)}, f32[16,8,768]{2,1,0:T(8,128)S(1)}, u32[]{:S(2)}, u32[]{:S(2)}) collective-permute-start(f32[16,8,768]{2,1,0:T(8,128)S(1)} %get-tuple-element.16), channel_id=1, source_target_pairs={{0,4},{4,8},{8,12},{1,5},{5,9},{9,13},{2,6},{6,10},{10,14},{3,7},{... | collective-permute-start | bytes 1179656 | tf_op jit(solution)/shard_map/ppermute | solution.py:27
  110.9 27.1 %collective-permute-start.5 = (f32[16,8,768]{2,1,0:T(8,128)S(1)}, f32[16,8,768]{2,1,0:T(8,128)S(1)}, u32[]{:S(2)}, u32[]{:S(2)}) collective-permute-start(f32[16,8,768]{2,1,0:T(8,128)S(1)} %get-tuple-element.17), channel_id=1, source_target_pairs={{4,0},{8,4},{12,8},{5,1},{9,5},{13,9},{6,2},{10,6},{14,10},{7,3},{... | collective-permute-start | bytes 1179656 | tf_op jit(solution)/shard_map/ppermute | solution.py:29
  123.7 17.7 %collective-permute-start.12 = (f32[5,48,768]{2,1,0:T(8,128)S(1)}, f32[5,48,768]{2,1,0:T(8,128)S(1)}, u32[]{:S(2)}, u32[]{:S(2)}) collective-permute-start(f32[5,48,768]{2,1,0:T(8,128)S(1)} %get-tuple-element.10), channel_id=1, source_target_pairs={{0,16},{1,17},{2,18},{3,19},{4,20},{5,21},{6,22},{7,23},{8,24},{9,... | collective-permute-start | bytes 2211848 | tf_op jit(solution)/shard_map/ppermute | solution.py:27
  125.1 16.4 %collective-permute-start.13 = (f32[5,48,768]{2,1,0:T(8,128)S(1)}, f32[5,48,768]{2,1,0:T(8,128)S(1)}, u32[]{:S(2)}, u32[]{:S(2)}) collective-permute-start(f32[5,48,768]{2,1,0:T(8,128)S(1)} %get-tuple-element.11), channel_id=1, source_target_pairs={{16,0},{17,1},{18,2},{19,3},{20,4},{21,5},{22,6},{23,7},{24,8},{25... | collective-permute-start | bytes 2211848 | tf_op jit(solution)/shard_map/ppermute | solution.py:29
  138.1 5.5 %collective-permute-start.6 = (f32[5,48,768]{2,1,0:T(8,128)S(1)}, f32[5,48,768]{2,1,0:T(8,128)S(1)}, u32[]{:S(2)}, u32[]{:S(2)}) collective-permute-start(f32[5,48,768]{2,1,0:T(8,128)S(1)} %get-tuple-element.12), channel_id=1, source_target_pairs={{0,16},{1,17},{2,18},{3,19},{4,20},{5,21},{6,22},{7,23},{8,24},{9,... | collective-permute-start | bytes 2211848 | tf_op jit(solution)/shard_map/ppermute | solution.py:27
  139.5 4.2 %collective-permute-start.7 = (f32[5,48,768]{2,1,0:T(8,128)S(1)}, f32[5,48,768]{2,1,0:T(8,128)S(1)}, u32[]{:S(2)}, u32[]{:S(2)}) collective-permute-start(f32[5,48,768]{2,1,0:T(8,128)S(1)} %get-tuple-element.13), channel_id=1, source_target_pairs={{16,0},{17,1},{18,2},{19,3},{20,4},{21,5},{22,6},{23,7},{24,8},{25... | collective-permute-start | bytes 2211848 | tf_op jit(solution)/shard_map/ppermute | solution.py:29
  163.3 7.9 %collective-permute-start.14 = (f32[2,8,16,128]{3,2,1,0:T(8,128)S(1)}, f32[2,8,16,128]{3,2,1,0:T(8,128)S(1)}, u32[]{:S(2)}, u32[]{:S(2)}) collective-permute-start(f32[2,8,16,128]{3,2,1,0:T(8,128)S(1)} %get-tuple-element.26), channel_id=1, source_target_pairs={{0,1},{1,2},{2,3},{4,5},{5,6},{6,7},{8,9},{9,10},{10,11},{12,13},{... | collective-permute-start | bytes 393224 | tf_op jit(solution)/shard_map/ppermute | solution.py:27
  167.6 8.2 %collective-permute-start.15 = (f32[2,8,16,128]{3,2,1,0:T(8,128)S(1)}, f32[2,8,16,128]{3,2,1,0:T(8,128)S(1)}, u32[]{:S(2)}, u32[]{:S(2)}) collective-permute-start(f32[2,8,16,128]{3,2,1,0:T(8,128)S(1)} %get-tuple-element.27), channel_id=1, source_target_pairs={{1,0},{2,1},{3,2},{5,4},{6,5},{7,6},{9,8},{10,9},{11,10},{13,12},{... | collective-permute-start | bytes 393224 | tf_op jit(solution)/shard_map/ppermute | solution.py:29
  175.8 8.7 %collective-permute-start.16 = (f32[2,8,8,512]{3,2,1,0:T(8,128)S(1)}, f32[2,8,8,512]{3,2,1,0:T(8,128)S(1)}, u32[]{:S(2)}, u32[]{:S(2)}) collective-permute-start(f32[2,8,8,512]{3,2,1,0:T(8,128)S(1)} %get-tuple-element.24), channel_id=1, source_target_pairs={{0,4},{4,8},{8,12},{1,5},{5,9},{9,13},{2,6},{6,10},{10,14},{3,7},{... | collective-permute-start | bytes 786440 | tf_op jit(solution)/shard_map/ppermute | solution.py:27
  178.8 12.1 %collective-permute-start.17 = (f32[2,8,8,512]{3,2,1,0:T(8,128)S(1)}, f32[2,8,8,512]{3,2,1,0:T(8,128)S(1)}, u32[]{:S(2)}, u32[]{:S(2)}) collective-permute-start(f32[2,8,8,512]{3,2,1,0:T(8,128)S(1)} %get-tuple-element.25), channel_id=1, source_target_pairs={{4,0},{8,4},{12,8},{5,1},{9,5},{13,9},{6,2},{10,6},{14,10},{7,3},{... | collective-permute-start | bytes 786440 | tf_op jit(solution)/shard_map/ppermute | solution.py:29
  191.2 3.1 %collective-permute-start.18 = (f32[2,5,32,512]{3,2,1,0:T(8,128)S(1)}, f32[2,5,32,512]{3,2,1,0:T(8,128)S(1)}, u32[]{:S(2)}, u32[]{:S(2)}) collective-permute-start(f32[2,5,32,512]{3,2,1,0:T(8,128)S(1)} %get-tuple-element.18), channel_id=1, source_target_pairs={{0,16},{1,17},{2,18},{3,19},{4,20},{5,21},{6,22},{7,23},{8,24},{9,... | collective-permute-start | bytes 1966088 | tf_op jit(solution)/shard_map/ppermute | solution.py:27
  192.6 4.0 %collective-permute-start.19 = (f32[2,5,32,512]{3,2,1,0:T(8,128)S(1)}, f32[2,5,32,512]{3,2,1,0:T(8,128)S(1)}, u32[]{:S(2)}, u32[]{:S(2)}) collective-permute-start(f32[2,5,32,512]{3,2,1,0:T(8,128)S(1)} %get-tuple-element.19), channel_id=1, source_target_pairs={{16,0},{17,1},{18,2},{19,3},{20,4},{21,5},{22,6},{23,7},{24,8},{25... | collective-permute-start | bytes 1966088 | tf_op jit(solution)/shard_map/ppermute | solution.py:29
where the time goes:
time: 221 us; the launch traced here: 220 us
  Pallas kernels  98.8 us (45%)
  waiting for transfers between devices  58.7 us (27%)
  starting transfers between devices  41.9 us (19%)
  other arithmetic  9.97 us (5%)
  local copies, waits for them, and re-layouts  8.32 us (4%)
    pallas_call x1, Pallas kernels, scatter(): pl.pallas_call(scatter_kernel, grid=(sources,), in_specs=[whole, one, one...  46.5 us
    ppermute x10, waiting for transfers between devices, padded_2(): lax.ppermute(head, axis, [((i + 1) % count, i) for i in range(ends)])  40.4 us
    pallas_call x1, Pallas kernels, body(): pl.pallas_call(functools.partial(up_kernel, wx, wy, wz, cx), in_specs=[vm...  21.9 us
    ppermute x10, starting transfers between devices, padded_2(): lax.ppermute(tail, axis, [(i, (i + 1) % count) for i in range(ends)])  21.1 us
    ppermute x10, starting transfers between devices, padded_2(): lax.ppermute(head, axis, [((i + 1) % count, i) for i in range(ends)])  18.2 us
    pallas_call x1, Pallas kernels, body(): pl.pallas_call(functools.partial(down_kernel, wx, wy, wz), in_specs=[vmem...  15.4 us
    pallas_call x1, Pallas kernels, points(): pl.pallas_call(functools.partial(points_kernel, ndevice, capacity), grid=...  15.1 us
    ppermute x10, waiting for transfers between devices, padded_2(): lax.ppermute(tail, axis, [(i, (i + 1) % count) for i in range(ends)])  12.6 us
  transfers between devices with their start and end apart: 21, of which 12 were waited for; matrix products, arithmetic and copies ran while one was open for 4% of the time, Pallas kernels for 21%

commit v1 on v0

--- a/solution.py
+++ b/solution.py
@@ -51,6 +51,22 @@
     return total + pltpu.roll(cells, 1, 1) + pltpu.roll(cells, nz - 1, 1)
 
 
+LANES = 2 * HALO
+
+
+def split3(x):
+    a = x.astype(jnp.bfloat16)
+    rest = x - a.astype(jnp.float32)
+    b = rest.astype(jnp.bfloat16)
+    c = (rest - b.astype(jnp.float32)).astype(jnp.bfloat16)
+    return a, b, c
+
+
+MESH = pl.DeviceIdType.MESH
+FINE = SMOOTH
+COARSE = COARSE_SMOOTH - 1 + (SMOOTH + 1) // 2
+
+
 def sweep(rhs, inverse, src, dst, update, first, last, pair, keep=None):
     old, new = pair
 
@@ -79,114 +95,355 @@
     lax.fori_loop(0, slabs, slab, 0)
 
 
-def down_kernel(wx, wy, wz, rhs, inverse, shift, smooth, remain, one, update):
-    slabs = rhs.shape[0]
-    ny, nz = remain.shape[1:]
-    pairs = factors(SMOOTH)
-    bufs = (one, smooth) if SMOOTH % 2 == 0 else (smooth, one)
-    begin(rhs, inverse, bufs[0], update, slabs)
+def near(axes):
+    ok = None
+    where = {}
+    for axis, step in axes:
+        place = lax.axis_index(axis) + step
+        fits = (place >= 0) & (place < lax.axis_size(axis))
+        ok = fits if ok is None else ok & fits
+        where[axis] = place
+    return ok, where
+
+
+SIDES = (-1, 1)
+LINKS = (
+    [(("gy", a),) for a in SIDES]
+    + [(("gz", b),) for b in SIDES]
+    + [(("gy", a), ("gz", b)) for b in SIDES for a in SIDES]
+    + [(("gx", a),) for a in SIDES]
+)
+MIRROR = [1, 0, 3, 2, 7, 6, 5, 4, 9, 8]
+
+
+def greet(links):
+    barrier = pltpu.get_barrier_semaphore()
+    peers = 0
+    for link in links:
+        ok, where = near(link)
+        peers = peers + ok.astype(jnp.int32)
+
+        @pl.when(ok)
+        def _():
+            pl.semaphore_signal(barrier, inc=1, device_id=where, device_id_type=MESH)
+
+    pl.semaphore_wait(barrier, peers)
+
+
+class Field:
+    def __init__(self, ext, depth, wide, send, recv, send_sem, recv_sem, land=None):
+        self.ext, self.depth, self.wide = ext, depth, wide
+        self.send, self.recv = send, recv
+        self.send_sem, self.recv_sem = send_sem, recv_sem
+        self.land = land
+        self.nx = ext.shape[0] - 2 * depth
+        self.ny = ext.shape[1] - 2 * wide
+        self.nz = ext.shape[2] - 128
+
+    def message(self, m):
+        d, nx, ny, nz, h = self.depth, self.nx, self.ny, self.nz, self.wide
+        ext = self.ext
+        if m < 2:
+            if h == 8:
+                rows = (0, ny - h)[m]
+                src = ext.at[pl.ds(d, nx), pl.ds(rows, h), pl.ds(0, nz)]
+                place = (ny + h, ny)[m]
+                got = ext.at[pl.ds(d, nx), pl.ds(place, h), pl.ds(0, nz)]
+                other = ext.at[pl.ds(d, nx), pl.ds((ny, ny + h)[m], h), pl.ds(0, nz)]
+            else:
+                src = self.send[0].at[m]
+                got = self.recv[0].at[m]
+                other = self.recv[0].at[1 - m]
+        elif m < 4:
+            src = self.send[1].at[m - 2]
+            got = self.recv[1].at[m - 2]
+            other = self.recv[1].at[3 - m]
+        elif m < 8:
+            b, a = divmod(m - 4, 2)
+            src = self.send[1].at[b, pl.ds((0, ny - 8)[a], 8)]
+            got = self.recv[2].at[b, a]
+            other = self.recv[2].at[1 - b, 1 - a]
+        else:
+            a = m - 8
+            src = ext.at[pl.ds((d, nx)[a], d)]
+            if self.land is None:
+                got = ext.at[pl.ds((0, d + nx)[a], d)]
+                other = ext.at[pl.ds((d + nx, 0)[a], d)]
+            else:
+                got = self.land.at[a]
+                other = self.land.at[1 - a]
+        return src, other, got
+
+    def copy(self, m, incoming):
+        src, other, got = self.message(m)
+        k = m if incoming else MIRROR[m]
+        return pltpu.make_async_remote_copy(
+            src_ref=got if incoming else src,
+            dst_ref=got if incoming else other,
+            send_sem=self.send_sem.at[m],
+            recv_sem=self.recv_sem.at[k],
+            device_id=near(LINKS[m])[1],
+            device_id_type=MESH,
+        )
+
+    def start(self, which):
+        for m in which:
+            @pl.when(near(LINKS[m])[0])
+            def _():
+                self.copy(m, False).start()
+
+    def finish(self, which):
+        for m in which:
+            ok = near(LINKS[m])[0]
+
+            @pl.when(ok)
+            def _():
+                self.copy(m, False).wait_send()
+                self.copy(m, True).wait_recv()
+
+            @pl.when(jnp.logical_not(ok))
+            def _():
+                got = self.message(m)[2]
+                got[...] = jnp.zeros(got.shape, jnp.float32)
+
+    def pack(self):
+        d, nx, ny, nz, h = self.depth, self.nx, self.ny, self.nz, self.wide
+        ext = self.ext
+        if h != 8:
+            sub = lax.broadcasted_iota(jnp.int32, (8, nz), 0)
+
+            def pair(t, carry):
+                one, two = d + 2 * t, d + 2 * t + 1
+                low = jnp.where(sub < h, ext[one, :8, :nz], pltpu.roll(ext[two, :8, :nz], h, 0))
+                high = jnp.where(
+                    sub < h, pltpu.roll(ext[one, ny - 8 : ny, :nz], h, 0), ext[two, ny - 8 : ny, :nz]
+                )
+                self.send[0][0, t] = low
+                self.send[0][1, t] = high
+                return carry
+
+            lax.fori_loop(0, nx // 2, pair, 0)
+        group = lax.broadcasted_iota(jnp.int32, (ny, 128), 1) // (2 * h)
+
+        def slab(x, carry):
+            low, high = carry
+            mine = group == x
+            shift = 2 * h * x + h
+            low = jnp.where(mine, pltpu.roll(ext[d + x, :ny, :128], shift, 1), low)
+            high = jnp.where(mine, pltpu.roll(ext[d + x, :ny, nz - 128 : nz], shift, 1), high)
+            return low, high
+
+        zero = jnp.zeros((ny, 128), jnp.float32)
+        low, high = lax.fori_loop(0, nx, slab, (zero, zero))
+        self.send[1][0] = low
+        self.send[1][1] = high
+
+    def unpack(self):
+        d, nx, ny, nz, h = self.depth, self.nx, self.ny, self.nz, self.wide
+        ext = self.ext
+        if h != 8:
+            sub = lax.broadcasted_iota(jnp.int32, (8, nz), 0)
+
+            def pair(t, carry):
+                minus, plus = self.recv[0][0, t], self.recv[0][1, t]
+                ext[d + 2 * t, ny : ny + 8, :nz] = jnp.where(sub < h, plus, pltpu.roll(minus, h, 0))
+                ext[d + 2 * t + 1, ny : ny + 8, :nz] = jnp.where(
+                    sub < h, pltpu.roll(plus, h, 0), minus
+                )
+                return carry
+
+            lax.fori_loop(0, nx // 2, pair, 0)
+        ends = []
+        for b in range(2):
+            corner = (self.recv[2][b, 1], self.recv[2][b, 0])
+            if h == 8:
+                ends.append(jnp.concatenate([self.recv[1][b], *corner], axis=0))
+            else:
+                sub = lax.broadcasted_iota(jnp.int32, (8, 128), 0)
+                ends.append(
+                    jnp.concatenate([self.recv[1][b], jnp.where(sub < h, *corner)], axis=0)
+                )
+        lane = lax.broadcasted_iota(jnp.int32, ends[0].shape, 1)
+        both = jnp.where(lane % (2 * h) < h, ends[0], ends[1])
+        edge = (lane < h) | (lane >= 128 - h)
+
+        def slab(x, carry):
+            moved = pltpu.roll(both, 128 - h - 2 * h * x, 1)
+            ext[d + x, :, nz : nz + 128] = jnp.where(edge, moved, 0.0)
+            return carry
+
+        lax.fori_loop(0, nx, slab, 0)
+
+
+def exchange(fields, between=None):
+    for field in fields:
+        field.pack()
+        field.start(range(8))
+    if between is not None:
+        between()
+    for field in fields:
+        field.finish(range(8))
+        field.unpack()
+        field.start((8, 9))
+    for field in fields:
+        field.finish((8, 9))
+
+
+def pooled(src, pairs, into, after):
+    nx, ny, nz = src.shape
+    depth = COARSE
+
+    def add(j, carry):
+        pairs[j] = src[2 * j] + src[2 * j + 1]
+        return carry
+
+    lax.fori_loop(0, nx // 2, add, 0)
+    flat = pairs[...].reshape(nx // 2 * ny, nz)
+
+    def halves(rows, cols, dim):
+        r = lax.broadcasted_iota(jnp.int32, (rows, cols), dim)
+        c = lax.broadcasted_iota(jnp.int32, (rows, cols), 1 - dim)
+        return (r == jnp.right_shift(c, 1)).astype(jnp.float32).astype(jnp.bfloat16)
+
+    along_z = halves(nz, nz // 2, 1)
+    along_y = halves(nx // 2 * ny // 2, nx // 2 * ny, 0)
+    flat = sum(jnp.dot(p, along_z, preferred_element_type=jnp.float32) for p in split3(flat))
+    flat = sum(jnp.dot(along_y, p, preferred_element_type=jnp.float32) for p in split3(flat))
+    out = after(0.5 * flat).reshape(nx // 2, ny // 2, nz // 2)
+    into[depth : depth + nx // 2, : ny // 2, : nz // 2] = out
+
+
+def cycle_kernel(
+    forcing, shift, pressure,
+    rhs, inverse, one, two, update, land, crhs, cinverse, cone, ctwo, cupdate, remain, pairs,
+    ysend, yrecv, zsend, zrecv, yzrecv, czsend, czrecv, cyzrecv, send_sem, recv_sem,
+):
+    greet(LINKS)
+    nx, ny, nz = forcing.shape
+
+    def fine(k, ext, landing=None):
+        return Field(
+            ext, FINE, 4, (ysend.at[k], zsend.at[k]), (yrecv.at[k], zrecv.at[k], yzrecv.at[k]),
+            send_sem.at[k], recv_sem.at[k], landing,
+        )
+
+    def coarse(k, ext):
+        return Field(
+            ext, COARSE, 8, (None, czsend.at[k]), (None, czrecv.at[k], cyzrecv.at[k]),
+            send_sem.at[3 + k], recv_sem.at[3 + k],
+        )
+
+    def load(x, carry):
+        rhs[FINE + x, :ny, :nz] = forcing[x]
+        inverse[FINE + x, :ny, :nz] = 1.0 / (6.0 + shift[x])
+        return carry
+
+    lax.fori_loop(0, nx, load, 0)
+    pooled(shift, pairs, cinverse, lambda total: 1.0 / (6.0 + total))
+    exchange([fine(0, rhs), fine(1, inverse), coarse(0, cinverse)])
+
+    slabs = nx + 2 * FINE
+    pairs_of = factors(SMOOTH)
+    bufs = (one, two)
+    begin(rhs, inverse, one, update, slabs)
     for k in range(1, SMOOTH):
-        sweep(
-            rhs, inverse, bufs[(k - 1) % 2], bufs[k % 2], update, k, slabs - k, pairs[k]
-        )
-
-    def slab(x, carry):
+        sweep(rhs, inverse, bufs[(k - 1) % 2], bufs[k % 2], update, k, slabs - k, pairs_of[k])
+    smooth = bufs[(SMOOTH - 1) % 2]
+    other = bufs[SMOOTH % 2]
+
+    def residual(x, carry):
         cells = smooth[x]
-        near = rhs[x] + beside(smooth, x, cells)
-        core = (slice(wy, wy + ny), slice(wz, wz + nz))
-        remain[x - wx] = near[core] - (6.0 + shift[x - wx]) * cells[core]
+        total = rhs[x] + beside(smooth, x, cells)
+        remain[x - FINE] = total[:ny, :nz] - (6.0 + shift[x - FINE]) * cells[:ny, :nz]
         return carry
 
-    lax.fori_loop(wx, slabs - wx, slab, 0)
-
-
-def up_kernel(
-    wx, wy, wz, cx, coarse, rhs, inverse, smooth, pressure,
-    fix_a, fix_b, fix_update, one, two, update,
-):
-    crhs, cinverse = coarse.at[0], coarse.at[1]
-    cslabs, cny, cnz = fix_a.shape
-    slabs, fny, fnz = one.shape
-    ny, nz = pressure.shape[1:]
-    pairs = factors(COARSE_SMOOTH)
-    bufs = (fix_a, fix_b)
-    begin(crhs, cinverse, fix_a, fix_update, cslabs)
+    lax.fori_loop(FINE, FINE + nx, residual, 0)
+    pooled(remain, pairs, crhs, lambda total: total)
+    exchange([fine(2, smooth, land), coarse(1, crhs)])
+
+    cslabs = crhs.shape[0]
+    pairs_of = factors(COARSE_SMOOTH)
+    cbufs = (cone, ctwo)
+    begin(crhs, cinverse, cone, cupdate, cslabs)
     for k in range(1, COARSE_SMOOTH):
         sweep(
-            crhs, cinverse, bufs[(k - 1) % 2], bufs[k % 2], fix_update, k, cslabs - k, pairs[k]
+            crhs, cinverse, cbufs[(k - 1) % 2], cbufs[k % 2], cupdate, k, cslabs - k, pairs_of[k]
         )
-    fix = bufs[(COARSE_SMOOTH - 1) % 2]
-
-    low = cx - (SMOOTH + 1) // 2
+    fix = cbufs[(COARSE_SMOOTH - 1) % 2]
+
+    low = COARSE - (FINE + 1) // 2
     count = cslabs - 2 * low
+    cny, cnz = fix.shape[1:]
+    fny, fnz = smooth.shape[1:]
     flat = fix[low : low + count].reshape(count * cny, cnz)
 
-    def onehot(shape, offset_f, offset_c, fine_dim, fine_per, coarse_per):
+    def fan(shape, fine_dim, per_f, per_c, core, jump):
         f = lax.broadcasted_iota(jnp.int32, shape, fine_dim)
         c = lax.broadcasted_iota(jnp.int32, shape, 1 - fine_dim)
-        block, inner = 0, f
-        for g in range(1, shape[fine_dim] // fine_per):
-            block = block + (f >= g * fine_per).astype(jnp.int32)
-        inner = f - block * fine_per
-        half = jnp.right_shift(inner - offset_f + 2 * offset_c, 1)
-        return (c == half + block * coarse_per).astype(jnp.float32).astype(jnp.bfloat16)
-
-    fan_y = onehot((count * fny, count * cny), wy, wy, 0, fny, cny)
-    fan_z = onehot((cnz, fnz), wz, wz, 1, fnz, cnz)
-    tall = sum(
-        jnp.dot(fan_y, piece, preferred_element_type=jnp.float32) for piece in split3(flat)
-    )
-    full = sum(
-        jnp.dot(piece, fan_z, preferred_element_type=jnp.float32) for piece in split3(tall)
-    )
+        block = 0
+        for g in range(1, shape[fine_dim] // per_f):
+            block = block + (f >= g * per_f).astype(jnp.int32)
+        inner = f - block * per_f
+        target = jnp.right_shift(inner, 1) + jnp.where(inner >= core, jump, 0) + block * per_c
+        return (c == target).astype(jnp.float32).astype(jnp.bfloat16)
+
+    fan_y = fan((count * fny, count * cny), 0, fny, cny, ny + 4, cny - fny // 2)
+    fan_z = fan((cnz, fnz), 1, fnz, cnz, nz + 64, cnz - fnz // 2)
+    tall = sum(jnp.dot(fan_y, p, preferred_element_type=jnp.float32) for p in split3(flat))
+    full = sum(jnp.dot(p, fan_z, preferred_element_type=jnp.float32) for p in split3(tall))
     for j in range(count):
         part = full[j * fny : (j + 1) * fny]
         for half in range(2):
-            x = wx + 2 * (low + j - cx) + half
-            if wx - SMOOTH <= x < slabs - wx + SMOOTH:
-                one[x] = smooth[x] + part
-
-    pairs = factors(SMOOTH)
-    bufs = (one, two)
+            x = FINE + 2 * (low + j - COARSE) + half
+            if 0 <= x < FINE:
+                smooth[x] = land[0, x] + part
+            elif FINE <= x < FINE + nx:
+                smooth[x] = smooth[x] + part
+            elif FINE + nx <= x < slabs:
+                smooth[x] = land[1, x - FINE - nx] + part
+
+    pairs_of = factors(SMOOTH)
+    bufs = (smooth, other)
 
     def keep(x, cells):
-        pressure[x - wx] = cells[wy : wy + ny, wz : wz + nz]
-
-    edge = wx - SMOOTH
+        pressure[x - FINE] = cells[:ny, :nz]
+
     for k in range(SMOOTH):
         sweep(
             rhs, inverse, bufs[k % 2], bufs[(k + 1) % 2], update,
-            edge + k + 1, slabs - edge - k - 1, pairs[k], keep if k == SMOOTH - 1 else None,
+            k + 1, slabs - k - 1, pairs_of[k], keep if k == SMOOTH - 1 else None,
         )
 
 
-LANES = 2 * HALO
-HIGH = lax.Precision.HIGHEST
-
-
-def pair_matrix(rows, cols, offset=0):
-    r = lax.broadcasted_iota(jnp.int32, (rows, cols), 0)
-    c = lax.broadcasted_iota(jnp.int32, (rows, cols), 1)
-    return (r == (c + offset) // 2).astype(jnp.float32)
-
-
-def pool(field):
-    nx, ny, nz = field.shape
-    halves = jnp.sum(field.reshape(nx // 2, 2, ny, nz), axis=1)
-    flat = halves.reshape(nx // 2 * ny, nz)
-    along_z = jnp.dot(flat, pair_matrix(nz // 2, nz).T, precision=HIGH)
-    along_y = jnp.dot(
-        pair_matrix(nx // 2 * ny // 2, nx // 2 * ny), along_z, precision=HIGH
-    )
-    return along_y.reshape(nx // 2, ny // 2, nz // 2)
-
-
-def split3(x):
-    a = x.astype(jnp.bfloat16)
-    rest = x - a.astype(jnp.float32)
-    b = rest.astype(jnp.bfloat16)
-    c = (rest - b.astype(jnp.float32)).astype(jnp.bfloat16)
-    return a, b, c
+def cycle(forcing, shift):
+    nx, ny, nz = forcing.shape
+    cx, cy, cz = nx // 2, ny // 2, nz // 2
+
+    def buf(*shape):
+        return pltpu.VMEM(shape, jnp.float32)
+
+    wide = buf(nx + 2 * FINE, ny + 8, nz + 128)
+    cwide = buf(cx + 2 * COARSE, cy + 16, cz + 128)
+    vmem = pl.BlockSpec(memory_space=pltpu.VMEM)
+    return pl.pallas_call(
+        cycle_kernel,
+        in_specs=[vmem] * 2,
+        out_specs=vmem,
+        out_shape=jax.ShapeDtypeStruct(forcing.shape, jnp.float32),
+        scratch_shapes=[wide] * 5
+        + [buf(2, FINE, ny + 8, nz + 128)]
+        + [cwide] * 5
+        + [buf(nx, ny, nz), buf(cx, ny, nz)]
+        + [buf(3, 2, nx // 2, 8, nz)] * 2
+        + [buf(3, 2, ny, 128)] * 2
+        + [buf(3, 2, 2, 8, 128)]
+        + [buf(2, 2, cy, 128)] * 2
+        + [buf(2, 2, 2, 8, 128)]
+        + [pltpu.SemaphoreType.DMA((5, 10))] * 2,
+        compiler_params=pltpu.CompilerParams(
+            collective_id=1, has_side_effects=True, vmem_limit_bytes=60 * 2**20
+        ),
+    )(forcing, shift)
 
 
 def points_kernel(
@@ -351,36 +608,7 @@
     got = lax.all_to_all(packed, ("gx", "gy", "gz"), split_axis=0, concat_axis=0, tiled=True)
     forcing = scatter(pressure_rhs, got[:, :capacity], got[:, capacity:].astype(jnp.int32))
 
-    nx, ny, nz = pressure_rhs.shape
-    wx, wy, wz = 2 * SMOOTH - 1, 8, 128
-    cx = COARSE_SMOOTH - 1 + (SMOOTH + 1) // 2
-    sides = (("gz", 2, wz), ("gy", 1, wy), ("gx", 0, wx))
-    coarse_sides = (("gz", 3, wz), ("gy", 2, wy), ("gx", 1, cx))
-    coarse_shift = 0.5 * pool(shift_diag)
-    inverse = padded_2(1.0 / (6.0 + shift_diag), sides, False)
-    rhs = padded_2(forcing, sides, False)
-    wide = jax.ShapeDtypeStruct(rhs.shape, jnp.float32)
-    core = jax.ShapeDtypeStruct(pressure_rhs.shape, jnp.float32)
-    vmem = pl.BlockSpec(memory_space=pltpu.VMEM)
-    wide_buf = pltpu.VMEM(rhs.shape, jnp.float32)
-    smooth, remain = pl.pallas_call(
-        functools.partial(down_kernel, wx, wy, wz),
-        in_specs=[vmem] * 3,
-        out_specs=[vmem] * 2,
-        out_shape=[wide, core],
-        scratch_shapes=[wide_buf] * 2,
-    )(rhs, inverse, shift_diag)
-    coarse = padded_2(
-        jnp.stack([0.5 * pool(remain), 1.0 / (6.0 + coarse_shift)]), coarse_sides, False
-    )
-    fix_buf = pltpu.VMEM(coarse.shape[1:], jnp.float32)
-    pressure = pl.pallas_call(
-        functools.partial(up_kernel, wx, wy, wz, cx),
-        in_specs=[vmem] * 4,
-        out_specs=vmem,
-        out_shape=core,
-        scratch_shapes=[fix_buf] * 3 + [wide_buf] * 3,
-    )(coarse, rhs, inverse, smooth)
+    pressure = cycle(forcing, shift_diag)
     return (pressure, surface_force)
 
 

time: 221 us -> 157 us (0.71)
  the two profiles are of different devices: /device:TPU:0 before, /device:TPU:15 now
where the time goes in v1:
time: 157 us; the launch traced here: 156 us
  Pallas kernels  127 us (81%)
  blocking collectives  16.8 us (11%)
  local copies, waits for them, and re-layouts  7.61 us (5%)
  other arithmetic  1.89 us (1%)
    pallas_call x1, Pallas kernels, cycle(): pl.pallas_call(cycle_kernel, in_specs=[vmem] * 2, out_specs=vmem, out_sha...  65.1 us
    pallas_call x1, Pallas kernels, scatter(): pl.pallas_call(scatter_kernel, grid=(sources,), in_specs=[whole, one, one...  46.5 us
    all_to_all x1, blocking collectives, body(): lax.all_to_all(packed, ('gx', 'gy', 'gz'), split_axis=0, concat_axis=0, t...  16.8 us
    pallas_call x1, Pallas kernels, points(): pl.pallas_call(functools.partial(points_kernel, ndevice, capacity), grid=...  15 us
  transfers between devices with their start and end apart: 2, of which 1 were waited for; matrix products, arithmetic and copies ran while one was open for 1% of the time, Pallas kernels for 0%

profile of v1, /device:TPU:15, one launch (start us, length us, event | category | flops | bytes accessed | tf_op | source)
XLA Modules:
  0.0 156.2 jit_solution(17389833138227433108)
XLA Ops:
  0.6 0.8 fusion.4
  1.4 0.2 collective-permute-start.1
  1.6 1.3 collective-permute-start
  2.9 0.0 copy-start
  2.9 1.8 %add_select_fusion.con_ref = s32[6,8192]{1,0:T(8,128)} fusion(s32[6,8192]{1,0:T(8,128)} %param.17, s32[]{:T(128)S(6)} %mul.15), kind=kLoop, calls=%fused_computation | loop fusion | flops 638976 | bytes 393220 | tf_op jit(solution)/shard_map/jit(remainder)/select_n | solution.py:602
  4.7 0.0 collective-permute-done.1
  4.7 1.2 collective-permute-done
  5.9 0.0 copy-done
  5.9 0.2 concatenate.6
  6.1 0.7 concatenate.7.pos_ref
  6.8 15.0 %shard_map.104 = (f32[3,8192]{1,0:T(4,128)}, f32[32,2048]{1,0:T(8,128)}) custom-call(f32[8,8320]{1,0:T(8,128)} %concatenate.7.pos_ref, f32[3,8192]{1,0:T(4,128)} %nrm_ref.1, f32[1,8192]{1,0:T(1,128)} %bitcast.18, f32[6,8192]{1,0:T(8,128)} %wgt_ref.1, s32[6,8192]{1,0:T(8,128)} %add_select_fusion.con_ref, s32[1,8192]{1,0:T(1,128)} %bitcast.19, s32[1,8192]{1,0:T(1,128)} %bitcast.20), custom_call_target="tpu_custom_call" | custom-call | flops 3221225472 | bytes 40000000 | tf_op jit(solution)/shard_map/pallas_call | solution.py:519
  21.8 1.2 copy.13
  23.1 16.8 %all_to_all.12 = f32[32,1,2048]{2,1,0:T(1,128)S(1)} all-to-all(f32[32,1,2048]{2,1,0:T(1,128)S(1)} %copy.13), channel_id=1, replica_groups=mesh['gx'=2,'gy'=4,'gz'=4] {'gx','gy','gz'}, dimensions={0} | all-to-all | bytes 524288 | tf_op jit(solution)/shard_map/all_to_all | solution.py:608
  39.8 0.1 copy.18
  39.9 0.1 multiply_subtract_fusion
  40.0 0.8 copy.14.val_ref
  40.8 0.7 broadcast_in_dim.20.col_ref
  41.6 0.8 copy.15.row_ref
  42.3 46.5 %shard_map.105 = f32[512,512]{1,0:T(8,128)} custom-call(f32[512,512]{1,0:T(8,128)} %bitcast.17, f32[32,1,1024]{2,1,0:T(1,128)} %copy.14.val_ref, s32[32,1,1024]{2,1,0:T(1,128)} %copy.15.row_ref, s32[32,1,1024]{2,1,0:T(1,128)} %broadcast_in_dim.20.col_ref), custom_call_target="tpu_custom_call" | custom-call | flops 34359738368 | bytes 4000000 | tf_op jit(solution)/shard_map/pallas_call | solution.py:573
  88.8 65.1 %shard_map.106 = f32[16,32,512]{2,1,0:T(8,128)} custom-call(f32[16,32,512]{2,1,0:T(8,128)} %bitcast.13, f32[16,32,512]{2,1,0:T(8,128)} %shift.1), custom_call_target="tpu_custom_call" | custom-call | tf_op jit(solution)/shard_map/pallas_call | solution.py:428
  153.9 2.3 %copy.20 = f32[16,32,512]{2,1,0:T(8,128)} copy(f32[16,32,512]{2,1,0:T(8,128)} %shard_map.106) | data formatting | bytes 2097152
  (1 shorter events, 0.0 us)
Async XLA Ops:
  1.4 3.3 %collective-permute-start.1 = (f32[3,64]{1,0:T(4,128)S(1)}, f32[3,64]{1,0:T(4,128)S(1)}, u32[]{:S(2)}, u32[]{:S(2)}) collective-permute-start(f32[3,64]{1,0:T(4,128)S(1)} %get-tuple-element.8), channel_id=1, source_target_pairs={{1,0},{2,1},{3,2},{4,3},{5,4},{6,5},{7,6},{8,7},{9,8},{10,9},{11,1... | collective-permute-start | bytes 2312 | tf_op jit(solution)/shard_map/ppermute | solution.py:29
  1.6 4.3 %collective-permute-start = (f32[3,64]{1,0:T(4,128)S(1)}, f32[3,64]{1,0:T(4,128)S(1)}, u32[]{:S(2)}, u32[]{:S(2)}) collective-permute-start(f32[3,64]{1,0:T(4,128)S(1)} %get-tuple-element.9), channel_id=1, source_target_pairs={{0,1},{1,2},{2,3},{3,4},{4,5},{5,6},{6,7},{7,8},{8,9},{9,10},{10,1... | collective-permute-start | bytes 2312 | tf_op jit(solution)/shard_map/ppermute | solution.py:27
  2.9 3.0 %copy-start = (f32[3,8192]{1,0:T(4,128)S(1)}, f32[3,8192]{1,0:T(4,128)}, u32[]{:S(2)}) copy-start(f32[3,8192]{1,0:T(4,128)} %param.11) | copy-start | bytes 294916

commit v2 on v1

--- a/solution.py
+++ b/solution.py
@@ -446,89 +446,114 @@
     )(forcing, shift)
 
 
+BIN = 256
+
+
+def hot_rows(index, rows, dtype=jnp.bfloat16):
+    r = lax.broadcasted_iota(jnp.int32, (rows, index.shape[1]), 0)
+    if rows > BIN:
+        return r == index
+    return r.astype(jnp.float32).astype(dtype) == index.astype(jnp.float32).astype(dtype)
+
+
 def points_kernel(
-    ndevice, capacity, pos_ref, nrm_ref, ten_ref, wgt_ref, con_ref, own_ref, cel_ref,
+    ndevice, capacity, nbin, pos_ref, nrm_ref, ten_ref, wgt_ref, con_ref, own_ref, cel_ref,
     force_ref, packed_ref, carry_ref,
 ):
-    step = pl.program_id(0)
-    chunk = ten_ref.shape[1]
-
-    @pl.when(step == 0)
-    def _():
-        packed_ref[...] = jnp.zeros_like(packed_ref)
-        carry_ref[...] = jnp.zeros_like(carry_ref)
-
-    jumps = []
-    for sub in range(chunk // LANES):
-        here = pl.ds(sub * LANES, LANES)
-        base = pl.multiple_of(step * chunk + sub * LANES, LANES)
-        lower = pos_ref[:, pl.ds(base, LANES)]
-        upper = pos_ref[:, pl.ds(base + LANES, LANES)]
-        centre_pos = jnp.concatenate([lower[:, HALO:], upper[:, :HALO]], axis=1)
-        total = jnp.zeros_like(lower)
-        for which in range(con_ref.shape[0]):
-            index = con_ref[which : which + 1, here] - base
-            wide = jnp.broadcast_to(index, lower.shape)
-            low = jnp.bitwise_and(wide, LANES - 1)
-            near = jnp.take_along_axis(lower, low, axis=1, mode="promise_in_bounds")
-            far = jnp.take_along_axis(upper, low, axis=1, mode="promise_in_bounds")
-            picked = jnp.where(wide < LANES, near, far)
-            total = total + wgt_ref[which : which + 1, here] * (picked - centre_pos)
-        force = ten_ref[:, here] * total[:3]
-        force_ref[:, here] = force
-        jumps.append(jnp.sum(force * nrm_ref[:, here], axis=0, keepdims=True))
-    jump = jnp.concatenate(jumps, axis=1)
-
-    hot = (lax.broadcasted_iota(jnp.int32, (ndevice, chunk), 0) == own_ref[...]).astype(jnp.float32)
-    hot_half = hot.astype(jnp.bfloat16)
+    chunk = 4 * LANES
+    nhi = capacity // BIN
+    per = packed_ref.shape[0] // ndevice
+    cells_per_bin = BIN * BIN
+    npoint = ten_ref.shape[1]
+    zero = jnp.zeros((), jnp.bfloat16)
+
+    def classes(here):
+        return own_ref[:, here] + ndevice * jnp.right_shift(cel_ref[:, here], 16)
+
+    def count(i, total):
+        here = pl.ds(pl.multiple_of(i * chunk, chunk), chunk)
+        hot = hot_rows(classes(here), nbin * ndevice)
+        return total + jnp.sum(jnp.where(hot, 1.0, 0.0).astype(jnp.float32), axis=1, keepdims=True)
+
+    counts = lax.fori_loop(
+        0, npoint // chunk, count, jnp.zeros((nbin * ndevice, 1), jnp.float32)
+    )
+    base = jnp.zeros((ndevice, 1), jnp.float32)
+    for b in range(nbin):
+        carry_ref[b * ndevice : (b + 1) * ndevice] = base
+        base = base + counts[b * ndevice : (b + 1) * ndevice]
+    packed_ref[...] = jnp.zeros_like(packed_ref)
     before = (
         lax.broadcasted_iota(jnp.int32, (chunk, chunk), 0)
         < lax.broadcasted_iota(jnp.int32, (chunk, chunk), 1)
-    ).astype(jnp.bfloat16)
-    earlier = jnp.dot(hot_half, before, preferred_element_type=jnp.float32) + carry_ref[...]
-    rank = jnp.sum(hot * earlier, axis=0, keepdims=True).astype(jnp.int32)
-    carry_ref[...] = carry_ref[...] + jnp.sum(hot, axis=1, keepdims=True)
-    slots = (
-        lax.broadcasted_iota(jnp.int32, (capacity, chunk), 0) == rank
     ).astype(jnp.float32).astype(jnp.bfloat16)
-    cell = cel_ref[...]
-    parts = [piece.astype(jnp.float32) for piece in split3(jump)]
-    for bits in (0, 8, 16):
-        piece = jnp.bitwise_and(jnp.right_shift(cell, bits), 255).astype(jnp.float32)
-        parts.append(piece)
-    left = jnp.concatenate([(hot * part).astype(jnp.bfloat16) for part in parts], axis=0)
-    packed = lax.dot_general(
-        left, slots, (((1,), (1,)), ((), ())), preferred_element_type=jnp.float32
-    )
-    n = ndevice
-    values = packed[0:n] + packed[n : 2 * n] + packed[2 * n : 3 * n]
-    cells = packed[3 * n : 4 * n] + 256.0 * packed[4 * n : 5 * n] + 65536.0 * packed[5 * n :]
-    packed_ref[:, :capacity] += values
-    packed_ref[:, capacity:] += cells
-
-
-def points(padded, normals, tension, edge_weight, relative, owner_ids, cell_map, ndevice, capacity):
+
+    def step(i, carry):
+        start = pl.multiple_of(i * chunk, chunk)
+        jumps = []
+        for sub in range(chunk // LANES):
+            base = pl.multiple_of(start + sub * LANES, LANES)
+            here = pl.ds(base, LANES)
+            lower = pos_ref[:, here]
+            upper = pos_ref[:, pl.ds(base + LANES, LANES)]
+            centre_pos = jnp.concatenate([lower[:, HALO:], upper[:, :HALO]], axis=1)
+            total = jnp.zeros_like(lower)
+            for which in range(con_ref.shape[0]):
+                index = con_ref[which : which + 1, here] - base
+                wide = jnp.broadcast_to(index, lower.shape)
+                low = jnp.bitwise_and(wide, LANES - 1)
+                near_by = jnp.take_along_axis(lower, low, axis=1, mode="promise_in_bounds")
+                far = jnp.take_along_axis(upper, low, axis=1, mode="promise_in_bounds")
+                picked = jnp.where(wide < LANES, near_by, far)
+                total = total + wgt_ref[which : which + 1, here] * (picked - centre_pos)
+            force = ten_ref[:, here] * total[:3]
+            force_ref[:, here] = force
+            jumps.append(jnp.sum(force * nrm_ref[:, here], axis=0, keepdims=True))
+        jump = jnp.concatenate(jumps, axis=1)
+
+        here = pl.ds(start, chunk)
+        hot = hot_rows(classes(here), nbin * ndevice)
+        ones = jnp.where(hot, jnp.ones((), jnp.bfloat16), zero)
+        earlier = jnp.dot(ones, before, preferred_element_type=jnp.float32) + carry_ref[...]
+        wide_ones = ones.astype(jnp.float32)
+        rank = jnp.sum(wide_ones * earlier, axis=0, keepdims=True).astype(jnp.int32)
+        carry_ref[...] = carry_ref[...] + jnp.sum(wide_ones, axis=1, keepdims=True)
+        slot = hot_rows(jnp.bitwise_and(rank, BIN - 1), BIN)
+        slots = jnp.where(slot, jnp.ones((), jnp.bfloat16), zero)
+        row = own_ref[:, here] * per + jnp.right_shift(rank, 8)
+        here_value = hot_rows(row, packed_ref.shape[0])
+        here_cell = hot_rows(row + per // 2, packed_ref.shape[0])
+        cell = cel_ref[:, here] + 1
+        total = packed_ref[...]
+        for piece, bits in zip(split3(jump), (0, 8, 16)):
+            digit = jnp.left_shift(jnp.bitwise_and(jnp.right_shift(cell, bits), 255), bits)
+            digit = digit.astype(jnp.float32).astype(jnp.bfloat16)
+            left = jnp.where(here_value, piece, jnp.where(here_cell, digit, zero))
+            total = total + lax.dot_general(
+                left, slots, (((1,), (1,)), ((), ())), preferred_element_type=jnp.float32
+            )
+        packed_ref[...] = total
+        return carry
+
+    lax.fori_loop(0, npoint // chunk, step, 0)
+
+
+def points(
+    padded, normals, tension, edge_weight, relative, owner_ids, cell_map, ndevice, capacity, nbin
+):
     npoint = tension.shape[0]
-    chunk = 4 * LANES if npoint % (4 * LANES) == 0 else LANES
     padded = jnp.concatenate([padded, jnp.zeros((5, padded.shape[1]), jnp.float32)], axis=0)
-    neigh = relative.shape[0]
-
-    def rows(count):
-        return pl.BlockSpec((count, chunk), lambda i: (0, i))
-
+    per = max(8, 2 * (capacity // BIN))
+    vmem = pl.BlockSpec(memory_space=pltpu.VMEM)
     return pl.pallas_call(
-        functools.partial(points_kernel, ndevice, capacity),
-        grid=(npoint // chunk,),
-        in_specs=[
-            pl.BlockSpec(padded.shape, lambda i: (0, 0)),
-            rows(3), rows(1), rows(neigh), rows(neigh), rows(1), rows(1),
-        ],
-        out_specs=[rows(3), pl.BlockSpec((ndevice, 2 * capacity), lambda i: (0, 0))],
+        functools.partial(points_kernel, ndevice, capacity, nbin),
+        in_specs=[vmem] * 7,
+        out_specs=[vmem] * 2,
         out_shape=[
             jax.ShapeDtypeStruct((3, npoint), jnp.float32),
-            jax.ShapeDtypeStruct((ndevice, 2 * capacity), jnp.float32),
+            jax.ShapeDtypeStruct((ndevice * per, BIN), jnp.float32),
         ],
-        scratch_shapes=[pltpu.VMEM((ndevice, 1), jnp.float32)],
+        scratch_shapes=[pltpu.VMEM((nbin * ndevice, 1), jnp.float32)],
         cost_estimate=pl.CostEstimate(
             flops=2 * npoint * capacity * 6 * ndevice, bytes_accessed=40000000, transcendentals=0
         ),
@@ -537,49 +562,107 @@
     )
 
 
-def scatter_kernel(rhs_ref, val_ref, row_ref, col_ref, out_ref):
-    @pl.when(pl.program_id(0) == 0)
-    def _():
-        out_ref[...] = rhs_ref[...]
-
-    nrow, ncol = out_ref.shape
-    count = val_ref.shape[2]
-    value = val_ref[0]
-    first = value.astype(jnp.bfloat16)
-    second = (value - first.astype(jnp.float32)).astype(jnp.bfloat16)
-    by_row = (
-        (lax.broadcasted_iota(jnp.int32, (nrow, count), 0) == row_ref[0])
-        .astype(jnp.float32)
-        .astype(jnp.bfloat16)
-    )
-    same = lax.broadcasted_iota(jnp.int32, (ncol, count), 0) == col_ref[0]
-    total = out_ref[...]
-    for piece in (first, second):
-        by_col = jnp.where(same, piece.astype(jnp.float32), 0.0).astype(jnp.bfloat16)
-        total = total + lax.dot_general(
-            by_row, by_col, (((1,), (1,)), ((), ())), preferred_element_type=jnp.float32
-        )
-    out_ref[...] = total
-
-
-def scatter(rhs, values, cells):
+GROUP = 8
+
+
+def scatter_kernel(nbin, rhs_ref, got_ref, out_ref, acc_ref, flat_ref, ends_ref, bound_ref, sem):
+    nrow, nz = rhs_ref.shape
+    nsource = bound_ref.shape[0]
+    per = got_ref.shape[0] // nsource
+    chunks = per // 2 * (BIN // LANES)
+    rows = nrow // nbin
+    nflat = got_ref.shape[0]
+    for half in range(BIN // LANES):
+        flat_ref[half * nflat : (half + 1) * nflat] = got_ref[:, half * LANES : (half + 1) * LANES]
+    got = got_ref[...].reshape(nsource, per, BIN)
+    cell_row = lax.broadcasted_iota(jnp.int32, got.shape, 1) >= per // 2
+    used = cell_row & (got > 0.0)
+    lane = lax.broadcasted_iota(jnp.int32, (nsource, LANES), 1)
+    ends = jnp.zeros((nsource, LANES), jnp.float32)
+    for b in range(nbin):
+        inside = jnp.where(used & (got <= float((b + 1) * BIN * BIN)), 1.0, 0.0)
+        total = jnp.sum(jnp.sum(inside, axis=1), axis=1, keepdims=True)
+        ends = jnp.where(lane == b + 1, total, ends)
+    ends_ref[...] = ends.astype(jnp.int32)
+    copy = pltpu.make_async_copy(ends_ref, bound_ref, sem)
+    copy.start()
+    copy.wait()
+    level = lax.broadcasted_iota(jnp.int32, (BIN, LANES), 0).astype(jnp.float32)
+    level = level.astype(jnp.bfloat16)
+    zero, unit = jnp.zeros((), jnp.bfloat16), jnp.ones((), jnp.bfloat16)
+
+    def quarter(b, carry):
+        def span(source):
+            at = jnp.minimum(source, nsource - 1)
+            first = jnp.minimum(jnp.right_shift(bound_ref[at, b], 7), chunks - 1)
+            last = jnp.right_shift(bound_ref[at, b + 1] + LANES - 1, 7)
+            return first, jnp.maximum(last, first + 1)
+
+        acc_ref[...] = jnp.zeros_like(acc_ref)
+
+        def work(state):
+            source, chunk, last = state
+            highs, lows, cols = [], [], []
+            for _ in range(GROUP):
+                at = jnp.minimum(source, nsource - 1)
+                row = jnp.bitwise_and(chunk, 1) * nflat + at * per + jnp.right_shift(chunk, 1)
+                value = flat_ref[pl.ds(row, 1)]
+                cell = flat_ref[pl.ds(row + per // 2, 1)].astype(jnp.int32) - 1
+                fits = (jnp.right_shift(cell, 16) == b) & (source < nsource)
+                half = jnp.bitwise_and(jnp.right_shift(cell, 8), 1)
+                place = half * rows + jnp.bitwise_and(jnp.right_shift(cell, 9), rows - 1)
+                place = jnp.where(fits, place, BIN).astype(jnp.float32).astype(jnp.bfloat16)
+                col = jnp.bitwise_and(cell, BIN - 1).astype(jnp.float32).astype(jnp.bfloat16)
+                first = value.astype(jnp.bfloat16)
+                second = (value - first.astype(jnp.float32)).astype(jnp.bfloat16)
+                same = level == place
+                highs.append(jnp.where(same, first, zero))
+                lows.append(jnp.where(same, second, zero))
+                cols.append(jnp.where(level == col, unit, zero))
+                over = chunk + 1 >= last
+                source = jnp.where(over, source + 1, source)
+                following = span(source)
+                chunk = jnp.where(over, following[0], chunk + 1)
+                last = jnp.where(over, following[1], last)
+            high = jnp.concatenate(highs, axis=1)
+            low = jnp.concatenate(lows, axis=1)
+            right = jnp.concatenate(cols, axis=1)
+            dims = (((1,), (1,)), ((), ()))
+            acc_ref[...] += lax.dot_general(
+                high, right, dims, preferred_element_type=jnp.float32
+            ) + lax.dot_general(low, right, dims, preferred_element_type=jnp.float32)
+            return source, chunk, last
+
+        lax.while_loop(lambda state: state[0] < nsource, work, (jnp.int32(0), *span(0)))
+        here = pl.ds(pl.multiple_of(b * rows, rows), rows)
+        for half in range(2):
+            cols = slice(half * BIN, (half + 1) * BIN)
+            out_ref[here, cols] = rhs_ref[here, cols] + acc_ref[half * rows : (half + 1) * rows]
+        return carry
+
+    lax.fori_loop(0, nbin, quarter, 0)
+
+
+def scatter(rhs, got, nsource, nbin):
     nx, ny, nz = rhs.shape
     nrow = nx * ny
-    sources, count = values.shape
-    rows = cells // nz
-    cols = cells - rows * nz
-    one = pl.BlockSpec((1, 1, count), lambda i: (i, 0, 0))
-    whole = pl.BlockSpec((nrow, nz), lambda i: (0, 0))
+    vmem = pl.BlockSpec(memory_space=pltpu.VMEM)
     out = pl.pallas_call(
-        scatter_kernel,
-        grid=(sources,),
-        in_specs=[whole, one, one, one],
-        out_specs=whole,
+        functools.partial(scatter_kernel, nbin),
+        in_specs=[vmem] * 2,
+        out_specs=vmem,
         out_shape=jax.ShapeDtypeStruct((nrow, nz), jnp.float32),
+        scratch_shapes=[
+            pltpu.VMEM((BIN, BIN), jnp.float32),
+            pltpu.VMEM((got.size // LANES, LANES), jnp.float32),
+            pltpu.VMEM((nsource, LANES), jnp.int32),
+            pltpu.SMEM((nsource, LANES), jnp.int32),
+            pltpu.SemaphoreType.DMA,
+        ],
         cost_estimate=pl.CostEstimate(
-            flops=4 * nrow * nz * sources * count, bytes_accessed=4000000, transcendentals=0
+            flops=4 * nrow * nz * got.size // 4, bytes_accessed=4000000, transcendentals=0
         ),
-    )(rhs.reshape(nrow, nz), values[:, None], rows[:, None], cols[:, None])
+    )(rhs.reshape(nrow, nz), got)
     return out.reshape(nx, ny, nz)
 
 
@@ -601,13 +684,13 @@
     padded = padded_2(positions, ((("gx", "gy", "gz"), 1, HALO),), True)
     relative = (connectivity - begin + HALO + total) % total
     capacity = 4 * npoint // ndevice
+    nbin = pressure_rhs.size // (BIN * BIN)
     surface_force, packed = points(
         padded, normals, tension, edge_weight, relative, owner_map[:, 0], cell_map,
-        ndevice, capacity,
+        ndevice, capacity, nbin,
     )
     got = lax.all_to_all(packed, ("gx", "gy", "gz"), split_axis=0, concat_axis=0, tiled=True)
-    forcing = scatter(pressure_rhs, got[:, :capacity], got[:, capacity:].astype(jnp.int32))
-
+    forcing = scatter(pressure_rhs, got, ndevice, nbin)
     pressure = cycle(forcing, shift_diag)
     return (pressure, surface_force)
 

time: 157 us -> 130 us (0.83); the launches traced: 156 us -> 132 us
  Pallas kernels: 127 us -> 105 us
  local copies, waits for them, and re-layouts: 7.61 us -> 3.99 us
    pallas_call x2, Pallas kernels: 61.5 us -> 28.9 us  [the longest x1 15.4 us: points(): pl.pallas_call(functools.partial(points_kernel, ndevice, capacity, nbin),...]
    pallas_call x1, Pallas kernels: 65.1 us -> 75.9 us  [cycle(): pl.pallas_call(cycle_kernel, in_specs=[vmem] * 2, out_specs=vmem, out_sha...]
    broadcast_in_dim x4 -> x0, local copies, waits for them, and re-layouts: 2.31 us -> none  [the longest x2 0.79 us: scatter(): values[:, None]]
where the time goes in v2:
time: 130 us; the launch traced here: 132 us
  Pallas kernels  105 us (81%)
  blocking collectives  18.3 us (14%)
  local copies, waits for them, and re-layouts  3.99 us (3%)
  other arithmetic  1.8 us (1%)
  starting transfers between devices  1.47 us (1%)
    pallas_call x1, Pallas kernels, cycle(): pl.pallas_call(cycle_kernel, in_specs=[vmem] * 2, out_specs=vmem, out_sha...  75.9 us
    all_to_all x1, blocking collectives, body(): lax.all_to_all(packed, ('gx', 'gy', 'gz'), split_axis=0, concat_axis=0, t...  18.3 us
    pallas_call x1, Pallas kernels, points(): pl.pallas_call(functools.partial(points_kernel, ndevice, capacity, nbin),...  15.4 us
    pallas_call x1, Pallas kernels, scatter(): pl.pallas_call(functools.partial(scatter_kernel, nbin), in_specs=[vmem] *...  13.5 us
  transfers between devices with their start and end apart: 2, of which 1 were waited for; matrix products, arithmetic and copies ran while one was open for 1% of the time, Pallas kernels for 0%

profile of v2, /device:TPU:15, one launch (start us, length us, event | category | flops | bytes accessed | tf_op | source)
XLA Modules:
  0.0 132.1 jit_solution(14914917042715009723)
XLA Ops:
  0.6 0.8 fusion.1
  1.4 0.2 collective-permute-start.1
  1.6 1.3 collective-permute-start
  2.9 0.0 copy-start
  2.9 1.8 %add_select_fusion.con_ref = s32[6,8192]{1,0:T(8,128)} fusion(s32[6,8192]{1,0:T(8,128)} %param.17, s32[]{:T(128)S(6)} %mul.11), kind=kLoop, calls=%fused_computation | loop fusion | flops 638976 | bytes 393220 | tf_op jit(solution)/shard_map/jit(remainder)/select_n | solution.py:685
  4.7 0.0 collective-permute-done.1
  4.7 1.2 collective-permute-done
  5.9 0.0 copy-done
  5.9 0.2 concatenate.6
  6.1 0.7 concatenate.7.pos_ref
  6.8 15.4 %shard_map.104 = (f32[3,8192]{1,0:T(4,128)}, f32[256,256]{1,0:T(8,128)}) custom-call(f32[8,8320]{1,0:T(8,128)} %concatenate.7.pos_ref, f32[3,8192]{1,0:T(4,128)} %nrm_ref.1, f32[1,8192]{1,0:T(1,128)} %bitcast.11, f32[6,8192]{1,0:T(8,128)} %wgt_ref.1, s32[6,8192]{1,0:T(8,128)} %add_select_fusion.con_ref, s32[1,8192]{1,0:T(1,128)} %bitcast.12, s32[1,8192]{1,0:T(1,128)} %bitcast.13), custom_call_target="tpu_custom_call" | custom-call | flops 3221225472 | bytes 40000000 | tf_op jit(solution)/shard_map/pallas_call | solution.py:548
  22.2 18.3 %all_to_all.11 = f32[32,8,256]{2,1,0:T(8,128)} all-to-all(f32[32,8,256]{2,1,0:T(8,128)} %bitcast.8), channel_id=1, replica_groups=mesh['gx'=2,'gy'=4,'gz'=4] {'gx','gy','gz'}, dimensions={0} | all-to-all | bytes 524288 | tf_op jit(solution)/shard_map/all_to_all | solution.py:692
  40.4 13.5 %shard_map.105 = f32[512,512]{1,0:T(8,128)} custom-call(f32[512,512]{1,0:T(8,128)} %bitcast.10, f32[256,256]{1,0:T(8,128)} %bitcast.9), custom_call_target="tpu_custom_call" | custom-call | flops 17179869184 | bytes 4000000 | tf_op jit(solution)/shard_map/pallas_call | solution.py:650
  53.9 75.9 %shard_map.106 = f32[16,32,512]{2,1,0:T(8,128)} custom-call(f32[16,32,512]{2,1,0:T(8,128)} %bitcast.7, f32[16,32,512]{2,1,0:T(8,128)} %shift.1), custom_call_target="tpu_custom_call" | custom-call | tf_op jit(solution)/shard_map/pallas_call | solution.py:428
  129.9 2.3 %copy.12 = f32[16,32,512]{2,1,0:T(8,128)} copy(f32[16,32,512]{2,1,0:T(8,128)} %shard_map.106) | data formatting | bytes 2097152
Async XLA Ops:
  1.4 3.3 %collective-permute-start.1 = (f32[3,64]{1,0:T(4,128)S(1)}, f32[3,64]{1,0:T(4,128)S(1)}, u32[]{:S(2)}, u32[]{:S(2)}) collective-permute-start(f32[3,64]{1,0:T(4,128)S(1)} %get-tuple-element.6), channel_id=1, source_target_pairs={{1,0},{2,1},{3,2},{4,3},{5,4},{6,5},{7,6},{8,7},{9,8},{10,9},{11,1... | collective-permute-start | bytes 2312 | tf_op jit(solution)/shard_map/ppermute | solution.py:29
  1.6 4.3 %collective-permute-start = (f32[3,64]{1,0:T(4,128)S(1)}, f32[3,64]{1,0:T(4,128)S(1)}, u32[]{:S(2)}, u32[]{:S(2)}) collective-permute-start(f32[3,64]{1,0:T(4,128)S(1)} %get-tuple-element.7), channel_id=1, source_target_pairs={{0,1},{1,2},{2,3},{3,4},{4,5},{5,6},{6,7},{7,8},{8,9},{9,10},{10,1... | collective-permute-start | bytes 2312 | tf_op jit(solution)/shard_map/ppermute | solution.py:27
  2.9 3.0 %copy-start = (f32[3,8192]{1,0:T(4,128)S(1)}, f32[3,8192]{1,0:T(4,128)}, u32[]{:S(2)}) copy-start(f32[3,8192]{1,0:T(4,128)} %param.11) | copy-start | bytes 294916

commit v3 on v2

--- a/solution.py
+++ b/solution.py
@@ -10,27 +10,11 @@
 HALO = 64
 SMOOTH = 3
 COARSE_SMOOTH = 4
+LANES = 2 * HALO
 
 
 centre = 1.125
 spread = 0.875
-
-
-def padded_2(cells, sides, closed):
-    for axis, dim, width in sides:
-        count = lax.axis_size(axis)
-        ends = count if closed else count - 1
-        head = lax.slice_in_dim(cells, 0, width, axis=dim)
-        tail = lax.slice_in_dim(cells, cells.shape[dim] - width, cells.shape[dim], axis=dim)
-        cells = jnp.concatenate(
-            [
-                lax.ppermute(tail, axis, [(i, (i + 1) % count) for i in range(ends)]),
-                cells,
-                lax.ppermute(head, axis, [((i + 1) % count, i) for i in range(ends)]),
-            ],
-            axis=dim,
-        )
-    return cells
 
 
 def factors(sweeps):
@@ -44,16 +28,6 @@
     return pairs
 
 
-def beside(ref, x, cells):
-    ny, nz = cells.shape
-    total = ref[x - 1] + ref[x + 1]
-    total = total + pltpu.roll(cells, 1, 0) + pltpu.roll(cells, ny - 1, 0)
-    return total + pltpu.roll(cells, 1, 1) + pltpu.roll(cells, nz - 1, 1)
-
-
-LANES = 2 * HALO
-
-
 def split3(x):
     a = x.astype(jnp.bfloat16)
     rest = x - a.astype(jnp.float32)
@@ -67,22 +41,43 @@
 COARSE = COARSE_SMOOTH - 1 + (SMOOTH + 1) // 2
 
 
+UNROLL = 4
+VMEM_LIMIT = 36 * 2**20
+
+
+def around(src, x, r):
+    ny, nz = src.shape[1:]
+    sub = lax.broadcasted_iota(jnp.int32, (8, nz), 0)
+    here = slice(r, r + 8)
+    below, above = (r - 8) % ny, (r + 8) % ny
+    cells = src[x, here]
+    total = src[x - 1, here] + src[x + 1, here]
+    total = total + (
+        pltpu.roll(jnp.where(sub == 7, src[x, below : below + 8], cells), 1, 0)
+        + pltpu.roll(jnp.where(sub == 0, src[x, above : above + 8], cells), 7, 0)
+    )
+    return cells, total + (pltpu.roll(cells, 1, 1) + pltpu.roll(cells, nz - 1, 1))
+
+
 def sweep(rhs, inverse, src, dst, update, first, last, pair, keep=None):
     old, new = pair
+    rows = src.shape[1] if keep is None else keep.shape[1]
 
     def slab(x, carry):
-        cells = src[x]
-        change = new * (inverse[x] * (rhs[x] + beside(src, x, cells)) - cells)
-        if old:
-            change = change + old * update[x]
-        if keep is None:
-            update[x] = change
-            dst[x] = cells + change
-        else:
-            keep(x, cells + change)
-        return carry
-
-    lax.fori_loop(first, last, slab, 0)
+        for r in range(0, rows, 8):
+            here = slice(r, r + 8)
+            cells, total = around(src, x, r)
+            change = new * (inverse[x, here] * (rhs[x, here] + total) - cells)
+            if old:
+                change = change + old * update[x, here]
+            if keep is None:
+                update[x, here] = change
+                dst[x, here] = cells + change
+            else:
+                keep[x - first, here] = (cells + change)[:, : keep.shape[2]]
+        return carry
+
+    lax.fori_loop(first, last, slab, 0, unroll=UNROLL)
 
 
 def begin(rhs, inverse, dst, update, slabs):
@@ -92,7 +87,7 @@
         dst[x] = change
         return carry
 
-    lax.fori_loop(0, slabs, slab, 0)
+    lax.fori_loop(0, slabs, slab, 0, unroll=2)
 
 
 def near(axes):
@@ -210,19 +205,10 @@
         d, nx, ny, nz, h = self.depth, self.nx, self.ny, self.nz, self.wide
         ext = self.ext
         if h != 8:
-            sub = lax.broadcasted_iota(jnp.int32, (8, nz), 0)
-
-            def pair(t, carry):
-                one, two = d + 2 * t, d + 2 * t + 1
-                low = jnp.where(sub < h, ext[one, :8, :nz], pltpu.roll(ext[two, :8, :nz], h, 0))
-                high = jnp.where(
-                    sub < h, pltpu.roll(ext[one, ny - 8 : ny, :nz], h, 0), ext[two, ny - 8 : ny, :nz]
-                )
-                self.send[0][0, t] = low
-                self.send[0][1, t] = high
-                return carry
-
-            lax.fori_loop(0, nx // 2, pair, 0)
+            for x in range(nx):
+                at = slice(d * (x % 8), d * (x % 8) + d)
+                self.send[0][0, x // 8, at] = ext[d + x, :d, :nz]
+                self.send[0][1, x // 8, at] = ext[d + x, ny - d : ny, :nz]
         group = lax.broadcasted_iota(jnp.int32, (ny, 128), 1) // (2 * h)
 
         def slab(x, carry):
@@ -234,7 +220,7 @@
             return low, high
 
         zero = jnp.zeros((ny, 128), jnp.float32)
-        low, high = lax.fori_loop(0, nx, slab, (zero, zero))
+        low, high = lax.fori_loop(0, nx, slab, (zero, zero), unroll=8)
         self.send[1][0] = low
         self.send[1][1] = high
 
@@ -242,17 +228,10 @@
         d, nx, ny, nz, h = self.depth, self.nx, self.ny, self.nz, self.wide
         ext = self.ext
         if h != 8:
-            sub = lax.broadcasted_iota(jnp.int32, (8, nz), 0)
-
-            def pair(t, carry):
-                minus, plus = self.recv[0][0, t], self.recv[0][1, t]
-                ext[d + 2 * t, ny : ny + 8, :nz] = jnp.where(sub < h, plus, pltpu.roll(minus, h, 0))
-                ext[d + 2 * t + 1, ny : ny + 8, :nz] = jnp.where(
-                    sub < h, pltpu.roll(plus, h, 0), minus
-                )
-                return carry
-
-            lax.fori_loop(0, nx // 2, pair, 0)
+            for x in range(nx):
+                at = slice(d * (x % 8), d * (x % 8) + d)
+                ext[d + x, ny : ny + d, :nz] = self.recv[0][1, x // 8, at]
+                ext[d + x, ny + 8 - d : ny + 8, :nz] = self.recv[0][0, x // 8, at]
         ends = []
         for b in range(2):
             corner = (self.recv[2][b, 1], self.recv[2][b, 0])
@@ -272,33 +251,21 @@
             ext[d + x, :, nz : nz + 128] = jnp.where(edge, moved, 0.0)
             return carry
 
-        lax.fori_loop(0, nx, slab, 0)
-
-
-def exchange(fields, between=None):
-    for field in fields:
-        field.pack()
-        field.start(range(8))
-    if between is not None:
-        between()
-    for field in fields:
-        field.finish(range(8))
-        field.unpack()
-        field.start((8, 9))
-    for field in fields:
-        field.finish((8, 9))
-
-
-def pooled(src, pairs, into, after):
-    nx, ny, nz = src.shape
-    depth = COARSE
-
+        lax.fori_loop(0, nx, slab, 0, unroll=8)
+
+
+def pair_up(src, pairs):
     def add(j, carry):
         pairs[j] = src[2 * j] + src[2 * j + 1]
         return carry
 
-    lax.fori_loop(0, nx // 2, add, 0)
-    flat = pairs[...].reshape(nx // 2 * ny, nz)
+    lax.fori_loop(0, pairs.shape[0], add, 0)
+
+
+def pooled(pairs, into, after):
+    cx, ny, nz = pairs.shape
+    depth = COARSE
+    flat = pairs[...].reshape(cx * ny, nz)
 
     def halves(rows, cols, dim):
         r = lax.broadcasted_iota(jnp.int32, (rows, cols), dim)
@@ -306,41 +273,69 @@
         return (r == jnp.right_shift(c, 1)).astype(jnp.float32).astype(jnp.bfloat16)
 
     along_z = halves(nz, nz // 2, 1)
-    along_y = halves(nx // 2 * ny // 2, nx // 2 * ny, 0)
+    along_y = halves(cx * ny // 2, cx * ny, 0)
     flat = sum(jnp.dot(p, along_z, preferred_element_type=jnp.float32) for p in split3(flat))
     flat = sum(jnp.dot(along_y, p, preferred_element_type=jnp.float32) for p in split3(flat))
-    out = after(0.5 * flat).reshape(nx // 2, ny // 2, nz // 2)
-    into[depth : depth + nx // 2, : ny // 2, : nz // 2] = out
-
-
-def cycle_kernel(
-    forcing, shift, pressure,
-    rhs, inverse, one, two, update, land, crhs, cinverse, cone, ctwo, cupdate, remain, pairs,
-    ysend, yrecv, zsend, zrecv, yzrecv, czsend, czrecv, cyzrecv, send_sem, recv_sem,
-):
-    greet(LINKS)
+    out = after(0.5 * flat).reshape(cx, ny // 2, nz // 2)
+    into[depth : depth + cx, : ny // 2, : nz // 2] = out
+
+
+def fine_field(ext, bufs, sems, landing=None):
+    ysend, yrecv, zsend, zrecv, yzrecv = bufs
+    return Field(ext, FINE, 4, (ysend, zsend), (yrecv, zrecv, yzrecv), *sems, landing)
+
+
+def coarse_field(ext, bufs, sems):
+    zsend, zrecv, yzrecv = bufs
+    return Field(ext, COARSE, 8, (None, zsend), (None, zrecv, yzrecv), *sems)
+
+
+def buf(*shape):
+    return pltpu.VMEM(shape, jnp.float32)
+
+
+def wide_shapes(nx, ny, nz):
+    cx, cy, cz = nx // 2, ny // 2, nz // 2
+    return (
+        (nx + 2 * FINE, ny + 8, nz + 128),
+        (cx + 2 * COARSE, cy + 16, cz + 128),
+    )
+
+
+def fine_scratch(nx, ny, nz):
+    rows = (2, nx // 8, 8 * FINE, nz)
+    return [buf(*rows)] * 2 + [buf(2, ny, 128)] * 2 + [buf(2, 2, 8, 128)]
+
+
+def coarse_scratch(nx, ny, nz):
+    return [buf(2, ny // 2, 128)] * 2 + [buf(2, 2, 8, 128)]
+
+
+FIRST, LAST = range(8), (8, 9)
+
+
+def cycle_kernel(forcing, shift, inverse, cinverse, pressure, *scratch):
+    (rhs, one, two, update, land, crhs, cone, ctwo, cupdate, pairs), scratch = (
+        scratch[:10], scratch[10:],
+    )
+    bufs_a, bufs_b, bufs_c = scratch[:5], scratch[5:10], scratch[10:13]
+    send_sem, recv_sem = scratch[13:]
     nx, ny, nz = forcing.shape
-
-    def fine(k, ext, landing=None):
-        return Field(
-            ext, FINE, 4, (ysend.at[k], zsend.at[k]), (yrecv.at[k], zrecv.at[k], yzrecv.at[k]),
-            send_sem.at[k], recv_sem.at[k], landing,
-        )
-
-    def coarse(k, ext):
-        return Field(
-            ext, COARSE, 8, (None, czsend.at[k]), (None, czrecv.at[k], cyzrecv.at[k]),
-            send_sem.at[3 + k], recv_sem.at[3 + k],
-        )
+    sems = [(send_sem.at[k], recv_sem.at[k]) for k in range(3)]
 
     def load(x, carry):
         rhs[FINE + x, :ny, :nz] = forcing[x]
-        inverse[FINE + x, :ny, :nz] = 1.0 / (6.0 + shift[x])
-        return carry
-
-    lax.fori_loop(0, nx, load, 0)
-    pooled(shift, pairs, cinverse, lambda total: 1.0 / (6.0 + total))
-    exchange([fine(0, rhs), fine(1, inverse), coarse(0, cinverse)])
+        return carry
+
+    lax.fori_loop(0, nx, load, 0, unroll=2)
+    field = fine_field(rhs, bufs_a, sems[0])
+    field.pack()
+    greet(LINKS)
+    field.start(FIRST)
+    field.finish(FIRST)
+    field.unpack()
+    field.start(LAST)
+    field.finish(LAST)
 
     slabs = nx + 2 * FINE
     pairs_of = factors(SMOOTH)
@@ -351,31 +346,31 @@
     smooth = bufs[(SMOOTH - 1) % 2]
     other = bufs[SMOOTH % 2]
 
-    def residual(x, carry):
-        cells = smooth[x]
-        total = rhs[x] + beside(smooth, x, cells)
-        remain[x - FINE] = total[:ny, :nz] - (6.0 + shift[x - FINE]) * cells[:ny, :nz]
-        return carry
-
-    lax.fori_loop(FINE, FINE + nx, residual, 0)
-    pooled(remain, pairs, crhs, lambda total: total)
-    exchange([fine(2, smooth, land), coarse(1, crhs)])
-
+    def residual(j, carry):
+        for r in range(0, ny, 8):
+            here = slice(r, r + 8)
+            both = 0.0
+            for half in range(2):
+                x = 2 * j + half
+                cells, total = around(smooth, FINE + x, r)
+                total = total[:, :nz] + rhs[FINE + x, here, :nz]
+                both = both + (total - (6.0 + shift[x, here]) * cells[:, :nz])
+            pairs[j, here] = both
+        return carry
+
+    lax.fori_loop(0, nx // 2, residual, 0, unroll=2)
+    pooled(pairs, crhs, lambda total: total)
+    coarse = coarse_field(crhs, bufs_c, sems[2])
+    coarse.pack()
+    coarse.start(FIRST)
+    field = fine_field(smooth, bufs_b, sems[1], land)
+    field.pack()
+    field.start(FIRST)
     cslabs = crhs.shape[0]
-    pairs_of = factors(COARSE_SMOOTH)
-    cbufs = (cone, ctwo)
-    begin(crhs, cinverse, cone, cupdate, cslabs)
-    for k in range(1, COARSE_SMOOTH):
-        sweep(
-            crhs, cinverse, cbufs[(k - 1) % 2], cbufs[k % 2], cupdate, k, cslabs - k, pairs_of[k]
-        )
-    fix = cbufs[(COARSE_SMOOTH - 1) % 2]
-
     low = COARSE - (FINE + 1) // 2
     count = cslabs - 2 * low
-    cny, cnz = fix.shape[1:]
+    cny, cnz = crhs.shape[1:]
     fny, fnz = smooth.shape[1:]
-    flat = fix[low : low + count].reshape(count * cny, cnz)
 
     def fan(shape, fine_dim, per_f, per_c, core, jump):
         f = lax.broadcasted_iota(jnp.int32, shape, fine_dim)
@@ -389,6 +384,26 @@
 
     fan_y = fan((count * fny, count * cny), 0, fny, cny, ny + 4, cny - fny // 2)
     fan_z = fan((cnz, fnz), 1, fnz, cnz, nz + 64, cnz - fnz // 2)
+    coarse.finish(FIRST)
+    coarse.unpack()
+    coarse.start(LAST)
+    field.finish(FIRST)
+    field.unpack()
+    field.start(LAST)
+    coarse.finish(LAST)
+
+    pairs_of = factors(COARSE_SMOOTH)
+    cbufs = (cone, ctwo)
+    begin(crhs, cinverse, cone, cupdate, cslabs)
+    for k in range(1, COARSE_SMOOTH):
+        sweep(
+            crhs, cinverse, cbufs[(k - 1) % 2], cbufs[k % 2], cupdate, k, cslabs - k, pairs_of[k]
+        )
+    fix = cbufs[(COARSE_SMOOTH - 1) % 2]
+
+    field.finish(LAST)
+    flat = fix[low : low + count].reshape(count * cny, cnz)
+
     tall = sum(jnp.dot(fan_y, p, preferred_element_type=jnp.float32) for p in split3(flat))
     full = sum(jnp.dot(p, fan_z, preferred_element_type=jnp.float32) for p in split3(tall))
     for j in range(count):
@@ -405,48 +420,37 @@
     pairs_of = factors(SMOOTH)
     bufs = (smooth, other)
 
-    def keep(x, cells):
-        pressure[x - FINE] = cells[:ny, :nz]
-
     for k in range(SMOOTH):
         sweep(
             rhs, inverse, bufs[k % 2], bufs[(k + 1) % 2], update,
-            k + 1, slabs - k - 1, pairs_of[k], keep if k == SMOOTH - 1 else None,
+            k + 1, slabs - k - 1, pairs_of[k], pressure if k == SMOOTH - 1 else None,
         )
 
 
-def cycle(forcing, shift):
+def cycle(forcing, shift, inverse, cinverse):
     nx, ny, nz = forcing.shape
-    cx, cy, cz = nx // 2, ny // 2, nz // 2
-
-    def buf(*shape):
-        return pltpu.VMEM(shape, jnp.float32)
-
-    wide = buf(nx + 2 * FINE, ny + 8, nz + 128)
-    cwide = buf(cx + 2 * COARSE, cy + 16, cz + 128)
+    wide, cwide = (buf(*shape) for shape in wide_shapes(nx, ny, nz))
     vmem = pl.BlockSpec(memory_space=pltpu.VMEM)
     return pl.pallas_call(
         cycle_kernel,
-        in_specs=[vmem] * 2,
+        in_specs=[vmem] * 4,
         out_specs=vmem,
         out_shape=jax.ShapeDtypeStruct(forcing.shape, jnp.float32),
-        scratch_shapes=[wide] * 5
+        scratch_shapes=[wide] * 4
         + [buf(2, FINE, ny + 8, nz + 128)]
-        + [cwide] * 5
-        + [buf(nx, ny, nz), buf(cx, ny, nz)]
-        + [buf(3, 2, nx // 2, 8, nz)] * 2
-        + [buf(3, 2, ny, 128)] * 2
-        + [buf(3, 2, 2, 8, 128)]
-        + [buf(2, 2, cy, 128)] * 2
-        + [buf(2, 2, 2, 8, 128)]
-        + [pltpu.SemaphoreType.DMA((5, 10))] * 2,
+        + [cwide] * 4
+        + [buf(nx // 2, ny, nz)]
+        + fine_scratch(nx, ny, nz) * 2
+        + coarse_scratch(nx, ny, nz)
+        + [pltpu.SemaphoreType.DMA((3, 10))] * 2,
         compiler_params=pltpu.CompilerParams(
-            collective_id=1, has_side_effects=True, vmem_limit_bytes=60 * 2**20
+            collective_id=1, has_side_effects=True, vmem_limit_bytes=VMEM_LIMIT
         ),
-    )(forcing, shift)
+    )(forcing, shift, inverse, cinverse)
 
 
 BIN = 256
+AXES = ("gx", "gy", "gz")
 
 
 def hot_rows(index, rows, dtype=jnp.bfloat16):
@@ -456,51 +460,140 @@
     return r.astype(jnp.float32).astype(dtype) == index.astype(jnp.float32).astype(dtype)
 
 
-def points_kernel(
-    ndevice, capacity, nbin, pos_ref, nrm_ref, ten_ref, wgt_ref, con_ref, own_ref, cel_ref,
-    force_ref, packed_ref, carry_ref,
+def place_of(index):
+    where = {}
+    for axis in reversed(AXES):
+        count = lax.axis_size(axis)
+        where[axis] = lax.rem(index, count)
+        index = lax.div(index, count)
+    return where
+
+
+def front_kernel(
+    ndevice, capacity, nbin, pos_ref, nrm_ref, ten_ref, wgt_ref, con_ref, own_ref, cel_ref, shift,
+    force_ref, got_ref, inverse, cinverse, *scratch,
 ):
+    (packed_ref, carry_ref, rank_ref, jump_ref, pad_ref, psend, precv, pairs), scratch = (
+        scratch[:8], scratch[8:],
+    )
+    fine_bufs, coarse_bufs = scratch[:5], scratch[5:8]
+    send_sem, recv_sem, all_send, all_recv, pos_send, pos_recv = scratch[8:]
     chunk = 4 * LANES
-    nhi = capacity // BIN
     per = packed_ref.shape[0] // ndevice
-    cells_per_bin = BIN * BIN
     npoint = ten_ref.shape[1]
-    zero = jnp.zeros((), jnp.bfloat16)
+    nx, ny, nz = shift.shape
+    zero, unit = jnp.zeros((), jnp.bfloat16), jnp.ones((), jnp.bfloat16)
+    me = lax.axis_index(AXES)
+    barrier = pltpu.get_barrier_semaphore()
+
+    def other(p):
+        return lax.rem(me + p, ndevice)
+
+    def hello(p, carry):
+        pl.semaphore_signal(barrier, inc=1, device_id=place_of(other(p)), device_id_type=MESH)
+        return carry
+
+    lax.fori_loop(1, ndevice, hello, 0)
+
+    def load(x, carry):
+        inverse[FINE + x, :ny, :nz] = 1.0 / (6.0 + shift[x])
+        return carry
+
+    lax.fori_loop(0, nx, load, 0, unroll=2)
+    pair_up(shift, pairs)
+    pooled(pairs, cinverse, lambda total: 1.0 / (6.0 + total))
+    fine = fine_field(inverse, fine_bufs, (send_sem.at[0], recv_sem.at[0]))
+    coarse = coarse_field(cinverse, coarse_bufs, (send_sem.at[1], recv_sem.at[1]))
+    fine.pack()
+    coarse.pack()
+    psend[0, :3] = pos_ref[:, npoint - LANES :]
+    psend[1, :3] = pos_ref[:, :LANES]
+
+    def spread_out(j, carry):
+        lower = pos_ref[:, pl.ds(pl.multiple_of(j * LANES - LANES, LANES), LANES)]
+        upper = pos_ref[:, pl.ds(pl.multiple_of(j * LANES, LANES), LANES)]
+        both = jnp.concatenate([lower[:, HALO:], upper[:, :HALO]], axis=1)
+        pad_ref[:3, pl.ds(pl.multiple_of(j * LANES, LANES), LANES)] = both
+        return carry
+
+    lax.fori_loop(1, npoint // LANES, spread_out, 0, unroll=7)
+
+    pl.semaphore_wait(barrier, ndevice - 1)
+
+    def edge(side, incoming):
+        return pltpu.make_async_remote_copy(
+            src_ref=psend.at[side],
+            dst_ref=precv.at[side],
+            send_sem=pos_send.at[side],
+            recv_sem=pos_recv.at[side],
+            device_id=place_of(other((1, ndevice - 1)[side])),
+            device_id_type=MESH,
+        )
+
+    for side in range(2):
+        edge(side, False).start()
+    fine.start(FIRST)
+    coarse.start(FIRST)
 
     def classes(here):
         return own_ref[:, here] + ndevice * jnp.right_shift(cel_ref[:, here], 16)
 
     def count(i, total):
         here = pl.ds(pl.multiple_of(i * chunk, chunk), chunk)
-        hot = hot_rows(classes(here), nbin * ndevice)
-        return total + jnp.sum(jnp.where(hot, 1.0, 0.0).astype(jnp.float32), axis=1, keepdims=True)
+        hot = jnp.where(hot_rows(classes(here), nbin * ndevice), 1.0, 0.0).astype(jnp.float32)
+        return total + (
+            hot[:, :LANES] + hot[:, LANES : 2 * LANES]
+            + (hot[:, 2 * LANES : 3 * LANES] + hot[:, 3 * LANES :])
+        )
 
     counts = lax.fori_loop(
-        0, npoint // chunk, count, jnp.zeros((nbin * ndevice, 1), jnp.float32)
-    )
+        0, npoint // chunk, count, jnp.zeros((nbin * ndevice, LANES), jnp.float32), unroll=2
+    )
+    counts = jnp.sum(counts, axis=1, keepdims=True)
     base = jnp.zeros((ndevice, 1), jnp.float32)
     for b in range(nbin):
         carry_ref[b * ndevice : (b + 1) * ndevice] = base
         base = base + counts[b * ndevice : (b + 1) * ndevice]
-    packed_ref[...] = jnp.zeros_like(packed_ref)
     before = (
         lax.broadcasted_iota(jnp.int32, (chunk, chunk), 0)
         < lax.broadcasted_iota(jnp.int32, (chunk, chunk), 1)
     ).astype(jnp.float32).astype(jnp.bfloat16)
 
-    def step(i, carry):
-        start = pl.multiple_of(i * chunk, chunk)
-        jumps = []
-        for sub in range(chunk // LANES):
-            base = pl.multiple_of(start + sub * LANES, LANES)
+    def order(i, carry):
+        here = pl.ds(pl.multiple_of(i * chunk, chunk), chunk)
+        ones = jnp.where(hot_rows(classes(here), nbin * ndevice), unit, zero)
+        earlier = jnp.dot(ones, before, preferred_element_type=jnp.float32) + carry
+        wide = ones.astype(jnp.float32)
+        rank_ref[:, here] = jnp.sum(wide * earlier, axis=0, keepdims=True).astype(jnp.int32)
+        return carry + jnp.sum(wide, axis=1, keepdims=True)
+
+    lax.fori_loop(0, npoint // chunk, order, carry_ref[...], unroll=2)
+
+    for side in range(2):
+        edge(side, True).wait_send()
+        edge(side, True).wait_recv()
+    pad_ref[:3, :LANES] = jnp.concatenate(
+        [precv[0, :3, HALO:], pos_ref[:, :HALO]], axis=1
+    )
+    pad_ref[:3, npoint:] = jnp.concatenate(
+        [pos_ref[:, npoint - HALO :], precv[1, :3, :HALO]], axis=1
+    )
+    begin_at = me * npoint
+    everything = npoint * ndevice
+
+    def pull(i, carry):
+        for sub in range(2):
+            base = pl.multiple_of(i * 2 * LANES + sub * LANES, LANES)
             here = pl.ds(base, LANES)
-            lower = pos_ref[:, here]
-            upper = pos_ref[:, pl.ds(base + LANES, LANES)]
+            lower = pad_ref[:, here]
+            upper = pad_ref[:, pl.ds(base + LANES, LANES)]
             centre_pos = jnp.concatenate([lower[:, HALO:], upper[:, :HALO]], axis=1)
+            index = con_ref[:, here] - begin_at + HALO
+            index = jnp.where(index < 0, index + everything, index)
+            index = jnp.where(index >= everything, index - everything, index) - base
             total = jnp.zeros_like(lower)
             for which in range(con_ref.shape[0]):
-                index = con_ref[which : which + 1, here] - base
-                wide = jnp.broadcast_to(index, lower.shape)
+                wide = jnp.broadcast_to(index[which : which + 1], lower.shape)
                 low = jnp.bitwise_and(wide, LANES - 1)
                 near_by = jnp.take_along_axis(lower, low, axis=1, mode="promise_in_bounds")
                 far = jnp.take_along_axis(upper, low, axis=1, mode="promise_in_bounds")
@@ -508,24 +601,30 @@
                 total = total + wgt_ref[which : which + 1, here] * (picked - centre_pos)
             force = ten_ref[:, here] * total[:3]
             force_ref[:, here] = force
-            jumps.append(jnp.sum(force * nrm_ref[:, here], axis=0, keepdims=True))
-        jump = jnp.concatenate(jumps, axis=1)
-
-        here = pl.ds(start, chunk)
-        hot = hot_rows(classes(here), nbin * ndevice)
-        ones = jnp.where(hot, jnp.ones((), jnp.bfloat16), zero)
-        earlier = jnp.dot(ones, before, preferred_element_type=jnp.float32) + carry_ref[...]
-        wide_ones = ones.astype(jnp.float32)
-        rank = jnp.sum(wide_ones * earlier, axis=0, keepdims=True).astype(jnp.int32)
-        carry_ref[...] = carry_ref[...] + jnp.sum(wide_ones, axis=1, keepdims=True)
-        slot = hot_rows(jnp.bitwise_and(rank, BIN - 1), BIN)
-        slots = jnp.where(slot, jnp.ones((), jnp.bfloat16), zero)
+            jump_ref[:, here] = jnp.sum(force * nrm_ref[:, here], axis=0, keepdims=True)
+        return carry
+
+    lax.fori_loop(0, npoint // (2 * LANES), pull, 0, unroll=2)
+
+    fine.finish(FIRST)
+    fine.unpack()
+    fine.start(LAST)
+    coarse.finish(FIRST)
+    coarse.unpack()
+    coarse.start(LAST)
+
+    packed_ref[...] = jnp.zeros_like(packed_ref)
+
+    def pack(i, carry):
+        here = pl.ds(pl.multiple_of(i * chunk, chunk), chunk)
+        rank = rank_ref[:, here]
+        slots = jnp.where(hot_rows(jnp.bitwise_and(rank, BIN - 1), BIN), unit, zero)
         row = own_ref[:, here] * per + jnp.right_shift(rank, 8)
         here_value = hot_rows(row, packed_ref.shape[0])
         here_cell = hot_rows(row + per // 2, packed_ref.shape[0])
         cell = cel_ref[:, here] + 1
         total = packed_ref[...]
-        for piece, bits in zip(split3(jump), (0, 8, 16)):
+        for piece, bits in zip(split3(jump_ref[:, here]), (0, 8, 16)):
             digit = jnp.left_shift(jnp.bitwise_and(jnp.right_shift(cell, bits), 255), bits)
             digit = digit.astype(jnp.float32).astype(jnp.bfloat16)
             left = jnp.where(here_value, piece, jnp.where(here_cell, digit, zero))
@@ -535,30 +634,76 @@
         packed_ref[...] = total
         return carry
 
-    lax.fori_loop(0, npoint // chunk, step, 0)
-
-
-def points(
-    padded, normals, tension, edge_weight, relative, owner_ids, cell_map, ndevice, capacity, nbin
+    lax.fori_loop(0, npoint // chunk, pack, 0, unroll=2)
+
+    def rows_of(device):
+        return pl.ds(pl.multiple_of(device * per, per), per)
+
+    def deal(p, incoming):
+        return pltpu.make_async_remote_copy(
+            src_ref=packed_ref.at[rows_of(other(p))],
+            dst_ref=got_ref.at[rows_of(other(ndevice - p) if incoming else me)],
+            send_sem=all_send.at[p],
+            recv_sem=all_recv.at[p],
+            device_id=place_of(other(p)),
+            device_id_type=MESH,
+        )
+
+    def send(p, carry):
+        deal(p, False).start()
+        return carry
+
+    lax.fori_loop(1, ndevice, send, 0)
+    got_ref[rows_of(me)] = packed_ref[rows_of(me)]
+    fine.finish(LAST)
+    coarse.finish(LAST)
+
+    def receive(p, carry):
+        deal(p, False).wait_send()
+        deal(p, True).wait_recv()
+        return carry
+
+    lax.fori_loop(1, ndevice, receive, 0)
+
+
+def front(
+    positions, normals, tension, edge_weight, connectivity, owner_ids, cell_map, shift,
+    ndevice, capacity, nbin,
 ):
     npoint = tension.shape[0]
-    padded = jnp.concatenate([padded, jnp.zeros((5, padded.shape[1]), jnp.float32)], axis=0)
+    nx, ny, nz = shift.shape
     per = max(8, 2 * (capacity // BIN))
     vmem = pl.BlockSpec(memory_space=pltpu.VMEM)
+    wide, cwide = wide_shapes(nx, ny, nz)
     return pl.pallas_call(
-        functools.partial(points_kernel, ndevice, capacity, nbin),
-        in_specs=[vmem] * 7,
-        out_specs=[vmem] * 2,
+        functools.partial(front_kernel, ndevice, capacity, nbin),
+        in_specs=[vmem] * 8,
+        out_specs=[vmem] * 4,
         out_shape=[
-            jax.ShapeDtypeStruct((3, npoint), jnp.float32),
-            jax.ShapeDtypeStruct((ndevice * per, BIN), jnp.float32),
+            jax.ShapeDtypeStruct(shape, jnp.float32)
+            for shape in ((3, npoint), (ndevice * per, BIN), wide, cwide)
         ],
-        scratch_shapes=[pltpu.VMEM((nbin * ndevice, 1), jnp.float32)],
-        cost_estimate=pl.CostEstimate(
-            flops=2 * npoint * capacity * 6 * ndevice, bytes_accessed=40000000, transcendentals=0
+        scratch_shapes=[
+            buf(ndevice * per, BIN),
+            buf(nbin * ndevice, 1),
+            pltpu.VMEM((1, npoint), jnp.int32),
+            buf(1, npoint),
+            buf(8, npoint + LANES),
+            buf(2, 8, LANES),
+            buf(2, 8, LANES),
+            buf(nx // 2, ny, nz),
+        ]
+        + fine_scratch(nx, ny, nz)
+        + coarse_scratch(nx, ny, nz)
+        + [pltpu.SemaphoreType.DMA((2, 10))] * 2
+        + [pltpu.SemaphoreType.DMA((ndevice,))] * 2
+        + [pltpu.SemaphoreType.DMA((2,))] * 2,
+        compiler_params=pltpu.CompilerParams(
+            collective_id=0, has_side_effects=True, vmem_limit_bytes=VMEM_LIMIT
         ),
     )(
-        padded, normals, tension[None], edge_weight, relative, owner_ids[None], cell_map[None]
+        positions, normals, tension[None], edge_weight, connectivity, owner_ids[None],
+        cell_map[None], shift,
     )
 
 
@@ -678,20 +823,15 @@
     connectivity,
 ):
     npoint = positions.shape[1]
-    ndevice = lax.axis_size(("gx", "gy", "gz"))
-    total = npoint * ndevice
-    begin = lax.axis_index(("gx", "gy", "gz")) * npoint
-    padded = padded_2(positions, ((("gx", "gy", "gz"), 1, HALO),), True)
-    relative = (connectivity - begin + HALO + total) % total
+    ndevice = lax.axis_size(AXES)
     capacity = 4 * npoint // ndevice
     nbin = pressure_rhs.size // (BIN * BIN)
-    surface_force, packed = points(
-        padded, normals, tension, edge_weight, relative, owner_map[:, 0], cell_map,
-        ndevice, capacity, nbin,
-    )
-    got = lax.all_to_all(packed, ("gx", "gy", "gz"), split_axis=0, concat_axis=0, tiled=True)
+    surface_force, got, inverse, cinverse = front(
+        positions, normals, tension, edge_weight, connectivity, owner_map[:, 0], cell_map,
+        shift_diag, ndevice, capacity, nbin,
+    )
     forcing = scatter(pressure_rhs, got, ndevice, nbin)
-    pressure = cycle(forcing, shift_diag)
+    pressure = cycle(forcing, shift_diag, inverse, cinverse)
     return (pressure, surface_force)
 
 

time: 130 us -> 100 us (0.77); the launches traced: 132 us -> 98.9 us
  Pallas kernels: 105 us -> 85.4 us
  blocking collectives: 18.3 us -> 0 us
  local copies, waits for them, and re-layouts: 3.99 us -> 12.8 us
  other arithmetic: 1.8 us -> 0 us
  starting transfers between devices: 1.47 us -> 0 us
    pallas_call x2, Pallas kernels: 91.3 us -> 72.8 us  [the longest x1 47.5 us: cycle(): pl.pallas_call(cycle_kernel, in_specs=[vmem] * 4, out_specs=vmem, out_sha...]
    all_to_all x1 -> x0, blocking collectives: 18.3 us -> none  [body(): lax.all_to_all(packed, ('gx', 'gy', 'gz'), split_axis=0, concat_axis=0, t...]
    unnamed x3 -> x28, local copies, waits for them, and re-layouts: 2.29 us -> 12.8 us
    select_n x1 -> x0, other arithmetic: 1.8 us -> none  [body(): relative = (connectivity - begin + HALO + total) % total]
    ppermute x2 -> x0, starting transfers between devices: 1.47 us -> none  [the longest x1 1.3 us: padded_2(): lax.ppermute(tail, axis, [(i, (i + 1) % count) for i in range(ends)])]
  transfers between devices with their start and end apart: 2 -> 0, of which waited for: 1 -> 0; matrix products, arithmetic and copies ran while one was open for 1% -> 0% of each run, Pallas kernels for 0% -> 0%
where the time goes in v3:
time: 100 us; the launch traced here: 98.9 us
  Pallas kernels  85.4 us (85%)
  local copies, waits for them, and re-layouts  12.8 us (13%)
    pallas_call x1, Pallas kernels, cycle(): pl.pallas_call(cycle_kernel, in_specs=[vmem] * 4, out_specs=vmem, out_sha...  47.5 us
    pallas_call x1, Pallas kernels, front(): pl.pallas_call(functools.partial(front_kernel, ndevice, capacity, nbin),...  25.3 us
    unnamed x28, local copies, waits for them, and re-layouts  12.8 us
    pallas_call x1, Pallas kernels, scatter(): pl.pallas_call(functools.partial(scatter_kernel, nbin), in_specs=[vmem] *...  12.6 us

profile of v3, /device:TPU:15, one launch (start us, length us, event | category | flops | bytes accessed | tf_op | source)
XLA Modules:
  0.0 98.9 jit_solution(15931050385316448642)
XLA Ops:
  0.6 0.0 copy-start
  0.6 1.2 %copy-done = f32[16,32,512]{2,1,0:T(8,128)S(1)} copy-done((f32[16,32,512]{2,1,0:T(8,128)S(1)}, f32[16,32,512]{2,1,0:T(8,128)}, u32[]{:S(2)}) %copy-start) | copy-done | bytes 1048600
  1.9 0.0 copy-start.5
  1.9 0.9 copy-done.5
  2.8 0.0 copy-start.6
  2.8 0.9 copy-done.6
  3.8 0.0 copy-start.7
  3.8 0.9 copy-done.7
  4.7 0.0 copy-start.8
  4.7 0.9 copy-done.8
  5.6 0.0 copy-start.9
  5.6 0.8 copy-done.9
  6.3 0.0 copy-start.10
  6.3 0.8 copy-done.10
  7.1 0.0 copy-start.11
  7.1 0.8 copy-done.11
  7.8 25.3 %shard_map.104 = (f32[3,8192]{1,0:T(4,128)S(1)}, f32[256,256]{1,0:T(8,128)S(1)}, f32[22,40,640]{2,1,0:T(8,128)S(1)}, f32[18,32,384]{2,1,0:T(8,128)S(1)}) custom-call(f32[3,8192]{1,0:T(4,128)S(1)} %copy-done.7, f32[3,8192]{1,0:T(4,128)S(1)} %copy-done.8, f32[1,8192]{1,0:T(1,128)S(1)} %bitcast.6, f32[6,8192]{1,0:T(8,128)S(1)} %copy-done.5, ...), custom_call_target="tpu_custom_call" | custom-call | tf_op jit(solution)/shard_map/pallas_call | solution.py:678
  33.1 0.0 copy-start.3
  33.1 0.9 copy-done.3
  34.0 0.0 copy-start.12
  34.1 0.7 copy-done.12
  34.7 0.0 copy-start.1
  34.7 12.6 %shard_map.105 = f32[512,512]{1,0:T(8,128)} custom-call(f32[512,512]{1,0:T(8,128)} %bitcast.9, f32[256,256]{1,0:T(8,128)} %copy-done.12), custom_call_target="tpu_custom_call" | custom-call | flops 17179869184 | bytes 4000000 | tf_op jit(solution)/shard_map/pallas_call | solution.py:795
  47.4 0.0 copy-done.1
  47.4 0.0 copy-start.2
  47.4 1.2 %copy-done.2 = f32[512,512]{1,0:T(8,128)S(1)} copy-done((f32[512,512]{1,0:T(8,128)S(1)}, f32[512,512]{1,0:T(8,128)}, u32[]{:S(2)}) %copy-start.2) | copy-done | bytes 1048600
  48.6 0.0 copy-start.4
  48.6 1.2 %copy-done.4 = f32[18,32,384]{2,1,0:T(8,128)S(1)} copy-done((f32[18,32,384]{2,1,0:T(8,128)S(1)}, f32[18,32,384]{2,1,0:T(8,128)}, u32[]{:S(2)}) %copy-start.4) | copy-done | bytes 884760
  49.8 47.5 %shard_map.106 = f32[16,32,512]{2,1,0:T(8,128)S(1)} custom-call(f32[16,32,512]{2,1,0:T(8,128)S(1)} %bitcast.5, f32[16,32,512]{2,1,0:T(8,128)S(1)} %copy-done.1, f32[22,40,640]{2,1,0:T(8,128)S(1)} %get-tuple-element.7.inverse, f32[18,32,384]{2,1,0:T(8,128)S(1)} %copy-done.4), custom_call_target="tpu_custom_call" | custom-call | tf_op jit(solution)/shard_map/pallas_call | solution.py:434
  97.3 1.0 copy.13
  98.2 0.7 copy.14
Async XLA Ops:
  0.6 1.2 %copy-start = (f32[16,32,512]{2,1,0:T(8,128)S(1)}, f32[16,32,512]{2,1,0:T(8,128)}, u32[]{:S(2)}) copy-start(f32[16,32,512]{2,1,0:T(8,128)} %shift.3) | copy-start | bytes 3145732
  1.9 0.9 copy-start.5
  2.8 0.9 copy-start.6
  3.8 0.9 copy-start.7
  4.7 0.9 copy-start.8
  5.6 0.8 copy-start.9
  6.3 0.8 copy-start.10
  7.1 0.8 copy-start.11
  33.1 0.9 copy-start.3
  34.0 0.7 copy-start.12
  34.7 12.6 %copy-start.1 = (f32[16,32,512]{2,1,0:T(8,128)S(1)}, f32[16,32,512]{2,1,0:T(8,128)}, u32[]{:S(2)}) copy-start(f32[16,32,512]{2,1,0:T(8,128)} %shift.3) | copy-start | bytes 3145732
  47.4 1.2 %copy-start.2 = (f32[512,512]{1,0:T(8,128)S(1)}, f32[512,512]{1,0:T(8,128)}, u32[]{:S(2)}) copy-start(f32[512,512]{1,0:T(8,128)} %shard_map.105) | copy-start | bytes 3145732
  48.6 1.2 %copy-start.4 = (f32[18,32,384]{2,1,0:T(8,128)S(1)}, f32[18,32,384]{2,1,0:T(8,128)}, u32[]{:S(2)}) copy-start(f32[18,32,384]{2,1,0:T(8,128)} %copy-done.3) | copy-start | bytes 2654212

commit v4 on v3

--- a/solution.py
+++ b/solution.py
@@ -314,7 +314,10 @@
 FIRST, LAST = range(8), (8, 9)
 
 
-def cycle_kernel(forcing, shift, inverse, cinverse, pressure, *scratch):
+def cycle_kernel(forcing, shift_hbm, inverse, cinverse, pressure, *scratch):
+    shift, load_sem, scratch = scratch[0], scratch[-1], scratch[1:-1]
+    fetch = pltpu.make_async_copy(shift_hbm, shift, load_sem)
+    fetch.start()
     (rhs, one, two, update, land, crhs, cone, ctwo, cupdate, pairs), scratch = (
         scratch[:10], scratch[10:],
     )
@@ -345,6 +348,8 @@
         sweep(rhs, inverse, bufs[(k - 1) % 2], bufs[k % 2], update, k, slabs - k, pairs_of[k])
     smooth = bufs[(SMOOTH - 1) % 2]
     other = bufs[SMOOTH % 2]
+
+    fetch.wait()
 
     def residual(j, carry):
         for r in range(0, ny, 8):
@@ -433,24 +438,30 @@
     vmem = pl.BlockSpec(memory_space=pltpu.VMEM)
     return pl.pallas_call(
         cycle_kernel,
-        in_specs=[vmem] * 4,
+        in_specs=[vmem, pl.BlockSpec(memory_space=pltpu.HBM), vmem, vmem],
         out_specs=vmem,
         out_shape=jax.ShapeDtypeStruct(forcing.shape, jnp.float32),
-        scratch_shapes=[wide] * 4
+        scratch_shapes=[buf(nx, ny, nz)]
+        + [wide] * 4
         + [buf(2, FINE, ny + 8, nz + 128)]
         + [cwide] * 4
         + [buf(nx // 2, ny, nz)]
         + fine_scratch(nx, ny, nz) * 2
         + coarse_scratch(nx, ny, nz)
-        + [pltpu.SemaphoreType.DMA((3, 10))] * 2,
+        + [pltpu.SemaphoreType.DMA((3, 10))] * 2
+        + [pltpu.SemaphoreType.DMA],
         compiler_params=pltpu.CompilerParams(
             collective_id=1, has_side_effects=True, vmem_limit_bytes=VMEM_LIMIT
         ),
-    )(forcing, shift, inverse, cinverse)
+    )(forcing, in_hbm(shift), inverse, cinverse)
 
 
 BIN = 256
 AXES = ("gx", "gy", "gz")
+
+
+def in_hbm(x):
+    return pltpu.with_memory_space_constraint(x, pltpu.HBM)
 
 
 def hot_rows(index, rows, dtype=jnp.bfloat16):
@@ -470,9 +481,20 @@
 
 
 def front_kernel(
-    ndevice, capacity, nbin, pos_ref, nrm_ref, ten_ref, wgt_ref, con_ref, own_ref, cel_ref, shift,
-    force_ref, got_ref, inverse, cinverse, *scratch,
+    ndevice, capacity, nbin, *refs
 ):
+    sources, refs = refs[:8], refs[8:]
+    (force_ref, got_ref, inverse, cinverse), refs = refs[:4], refs[4:]
+    (pos_ref, nrm_ref, ten_ref, wgt_ref, con_ref, own_ref, cel_ref, shift), scratch = (
+        refs[:8], refs[8:],
+    )
+    load_sem, scratch = scratch[-1], scratch[:-1]
+
+    def fetch(k):
+        return pltpu.make_async_copy(sources[k], refs[k], load_sem.at[k])
+
+    for k in (7, 0, 5, 6, 4, 3, 2, 1):
+        fetch(k).start()
     (packed_ref, carry_ref, rank_ref, jump_ref, pad_ref, psend, precv, pairs), scratch = (
         scratch[:8], scratch[8:],
     )
@@ -495,6 +517,8 @@
 
     lax.fori_loop(1, ndevice, hello, 0)
 
+    fetch(7).wait()
+
     def load(x, carry):
         inverse[FINE + x, :ny, :nz] = 1.0 / (6.0 + shift[x])
         return carry
@@ -506,6 +530,7 @@
     coarse = coarse_field(cinverse, coarse_bufs, (send_sem.at[1], recv_sem.at[1]))
     fine.pack()
     coarse.pack()
+    fetch(0).wait()
     psend[0, :3] = pos_ref[:, npoint - LANES :]
     psend[1, :3] = pos_ref[:, :LANES]
 
@@ -546,6 +571,8 @@
             + (hot[:, 2 * LANES : 3 * LANES] + hot[:, 3 * LANES :])
         )
 
+    for k in (5, 6):
+        fetch(k).wait()
     counts = lax.fori_loop(
         0, npoint // chunk, count, jnp.zeros((nbin * ndevice, LANES), jnp.float32), unroll=2
     )
@@ -569,6 +596,8 @@
 
     lax.fori_loop(0, npoint // chunk, order, carry_ref[...], unroll=2)
 
+    for k in (4, 3, 2, 1):
+        fetch(k).wait()
     for side in range(2):
         edge(side, True).wait_send()
         edge(side, True).wait_recv()
@@ -677,13 +706,21 @@
     wide, cwide = wide_shapes(nx, ny, nz)
     return pl.pallas_call(
         functools.partial(front_kernel, ndevice, capacity, nbin),
-        in_specs=[vmem] * 8,
+        in_specs=[pl.BlockSpec(memory_space=pltpu.HBM)] * 8,
         out_specs=[vmem] * 4,
         out_shape=[
             jax.ShapeDtypeStruct(shape, jnp.float32)
             for shape in ((3, npoint), (ndevice * per, BIN), wide, cwide)
         ],
         scratch_shapes=[
+            buf(3, npoint),
+            buf(3, npoint),
+            buf(1, npoint),
+            buf(*edge_weight.shape),
+            pltpu.VMEM(connectivity.shape, jnp.int32),
+            pltpu.VMEM((1, npoint), jnp.int32),
+            pltpu.VMEM((1, npoint), jnp.int32),
+            buf(nx, ny, nz),
             buf(ndevice * per, BIN),
             buf(nbin * ndevice, 1),
             pltpu.VMEM((1, npoint), jnp.int32),
@@ -697,21 +734,34 @@
         + coarse_scratch(nx, ny, nz)
         + [pltpu.SemaphoreType.DMA((2, 10))] * 2
         + [pltpu.SemaphoreType.DMA((ndevice,))] * 2
-        + [pltpu.SemaphoreType.DMA((2,))] * 2,
+        + [pltpu.SemaphoreType.DMA((2,))] * 2
+        + [pltpu.SemaphoreType.DMA((8,))],
         compiler_params=pltpu.CompilerParams(
-            collective_id=0, has_side_effects=True, vmem_limit_bytes=VMEM_LIMIT
+            collective_id=0, has_side_effects=True, vmem_limit_bytes=20 * 2**20
         ),
     )(
-        positions, normals, tension[None], edge_weight, connectivity, owner_ids[None],
-        cell_map[None], shift,
-    )
-
-
-GROUP = 8
-
-
-def scatter_kernel(nbin, rhs_ref, got_ref, out_ref, acc_ref, flat_ref, ends_ref, bound_ref, sem):
+        *map(
+            in_hbm,
+            (
+                positions, normals, tension[None], edge_weight, connectivity, owner_ids[None],
+                cell_map[None], shift,
+            ),
+        )
+    )
+
+
+GROUP = 24
+
+
+def scatter_kernel(
+    nbin, rhs_hbm, got_ref, force_ref, out_ref, force_hbm,
+    rhs_ref, acc_ref, flat_ref, ends_ref, bound_ref, sems,
+):
     nrow, nz = rhs_ref.shape
+    fetch = pltpu.make_async_copy(rhs_hbm, rhs_ref, sems.at[1])
+    fetch.start()
+    put = pltpu.make_async_copy(force_ref, force_hbm, sems.at[2])
+    put.start()
     nsource = bound_ref.shape[0]
     per = got_ref.shape[0] // nsource
     chunks = per // 2 * (BIN // LANES)
@@ -729,9 +779,10 @@
         total = jnp.sum(jnp.sum(inside, axis=1), axis=1, keepdims=True)
         ends = jnp.where(lane == b + 1, total, ends)
     ends_ref[...] = ends.astype(jnp.int32)
-    copy = pltpu.make_async_copy(ends_ref, bound_ref, sem)
+    copy = pltpu.make_async_copy(ends_ref, bound_ref, sems.at[0])
     copy.start()
     copy.wait()
+    fetch.wait()
     level = lax.broadcasted_iota(jnp.int32, (BIN, LANES), 0).astype(jnp.float32)
     level = level.astype(jnp.bfloat16)
     zero, unit = jnp.zeros((), jnp.bfloat16), jnp.ones((), jnp.bfloat16)
@@ -786,29 +837,36 @@
         return carry
 
     lax.fori_loop(0, nbin, quarter, 0)
-
-
-def scatter(rhs, got, nsource, nbin):
+    put.wait()
+
+
+def scatter(rhs, got, force, nsource, nbin):
     nx, ny, nz = rhs.shape
     nrow = nx * ny
     vmem = pl.BlockSpec(memory_space=pltpu.VMEM)
-    out = pl.pallas_call(
+    hbm = pl.BlockSpec(memory_space=pltpu.HBM)
+    out, force = pl.pallas_call(
         functools.partial(scatter_kernel, nbin),
-        in_specs=[vmem] * 2,
-        out_specs=vmem,
-        out_shape=jax.ShapeDtypeStruct((nrow, nz), jnp.float32),
+        in_specs=[hbm, vmem, vmem],
+        out_specs=[vmem, hbm],
+        out_shape=[
+            jax.ShapeDtypeStruct((nrow, nz), jnp.float32),
+            jax.ShapeDtypeStruct(force.shape, jnp.float32),
+        ],
         scratch_shapes=[
+            pltpu.VMEM((nrow, nz), jnp.float32),
             pltpu.VMEM((BIN, BIN), jnp.float32),
             pltpu.VMEM((got.size // LANES, LANES), jnp.float32),
             pltpu.VMEM((nsource, LANES), jnp.int32),
             pltpu.SMEM((nsource, LANES), jnp.int32),
-            pltpu.SemaphoreType.DMA,
+            pltpu.SemaphoreType.DMA((3,)),
         ],
+        compiler_params=pltpu.CompilerParams(vmem_limit_bytes=24 * 2**20),
         cost_estimate=pl.CostEstimate(
             flops=4 * nrow * nz * got.size // 4, bytes_accessed=4000000, transcendentals=0
         ),
-    )(rhs.reshape(nrow, nz), got)
-    return out.reshape(nx, ny, nz)
+    )(in_hbm(rhs.reshape(nrow, nz)), got, force)
+    return out.reshape(nx, ny, nz), force
 
 
 def body(
@@ -830,7 +888,7 @@
         positions, normals, tension, edge_weight, connectivity, owner_map[:, 0], cell_map,
         shift_diag, ndevice, capacity, nbin,
     )
-    forcing = scatter(pressure_rhs, got, ndevice, nbin)
+    forcing, surface_force = scatter(pressure_rhs, got, surface_force, ndevice, nbin)
     pressure = cycle(forcing, shift_diag, inverse, cinverse)
     return (pressure, surface_force)
 

time: 100 us -> 80 us (0.80)
  local copies, waits for them, and re-layouts: 12.8 us -> 0.97 us
  Pallas kernels: 85.4 us -> 78.1 us
    unnamed x28 -> x1, local copies, waits for them, and re-layouts: 12.8 us -> 0.97 us
    pallas_call x2, Pallas kernels: 60.1 us -> 52.5 us  [the longest x1 42.8 us: cycle(): pl.pallas_call(cycle_kernel, in_specs=[vmem, pl.BlockSpec(memory_space=pl...]
where the time goes in v4:
time: 80 us; the launch traced here: 79.7 us
  Pallas kernels  78.1 us (98%)
  local copies, waits for them, and re-layouts  0.97 us (1%)
    pallas_call x1, Pallas kernels, cycle(): pl.pallas_call(cycle_kernel, in_specs=[vmem, pl.BlockSpec(memory_space=pl...  42.8 us
    pallas_call x1, Pallas kernels, front(): pl.pallas_call(functools.partial(front_kernel, ndevice, capacity, nbin),...  25.6 us
    pallas_call x1, Pallas kernels, scatter(): pl.pallas_call(functools.partial(scatter_kernel, nbin), in_specs=[hbm, vm...  9.73 us

profile of v4, /device:TPU:15, one launch (start us, length us, event | category | flops | bytes accessed | tf_op | source)
XLA Modules:
  0.0 79.7 jit_solution(5747853007552685794)
XLA Ops:
  0.6 25.6 %shard_map.104 = (f32[3,8192]{1,0:T(4,128)S(1)}, f32[256,256]{1,0:T(8,128)S(1)}, f32[22,40,640]{2,1,0:T(8,128)S(1)}, f32[18,32,384]{2,1,0:T(8,128)S(1)}) custom-call(f32[3,8192]{1,0:T(4,128)} %refs_0_.1, f32[3,8192]{1,0:T(4,128)} %refs_1_.1, f32[1,8192]{1,0:T(1,128)} %bitcast.6, f32[6,8192]{1,0:T(8,128)} %refs_3_.1, s32[6,8192]{1,0:T(8,128)} %refs_4_.1, ...), custom_call_target="tpu_custom_call" | custom-call | tf_op jit(solution)/shard_map/pallas_call | solution.py:707
  26.3 9.7 %shard_map.105 = (f32[512,512]{1,0:T(8,128)S(1)}, f32[3,8192]{1,0:T(4,128)}) custom-call(f32[512,512]{1,0:T(8,128)} %bitcast.9, f32[256,256]{1,0:T(8,128)S(1)} %get-tuple-element.8.got_ref, f32[3,8192]{1,0:T(4,128)S(1)} %get-tuple-element.9.force_ref), custom_call_target="tpu_custom_call" | custom-call | flops 17179869184 | bytes 4000000 | tf_op jit(solution)/shard_map/pallas_call | solution.py:848
  36.0 42.8 %shard_map.106 = f32[16,32,512]{2,1,0:T(8,128)S(1)} custom-call(f32[16,32,512]{2,1,0:T(8,128)S(1)} %bitcast.5, f32[16,32,512]{2,1,0:T(8,128)} %shift_hbm.1, f32[22,40,640]{2,1,0:T(8,128)S(1)} %get-tuple-element.11.inverse, f32[18,32,384]{2,1,0:T(8,128)S(1)} %get-tuple-element.12.cinverse), custom_call_target="tpu_custom_call" | custom-call | tf_op jit(solution)/shard_map/pallas_call | solution.py:439
  78.8 1.0 %copy.12 = f32[16,32,512]{2,1,0:T(8,128)} copy(f32[16,32,512]{2,1,0:T(8,128)S(1)} %shard_map.106) | data formatting | bytes 2097152

commit v5 on v4

--- a/solution.py
+++ b/solution.py
@@ -481,7 +481,7 @@
 
 
 def front_kernel(
-    ndevice, capacity, nbin, *refs
+    ndevice, nbin, *refs
 ):
     sources, refs = refs[:8], refs[8:]
     (force_ref, got_ref, inverse, cinverse), refs = refs[:4], refs[4:]
@@ -495,13 +495,14 @@
 
     for k in (7, 0, 5, 6, 4, 3, 2, 1):
         fetch(k).start()
-    (packed_ref, carry_ref, rank_ref, jump_ref, pad_ref, psend, precv, pairs), scratch = (
-        scratch[:8], scratch[8:],
+    (packed_ref, total_ref, carry_ref, rank_ref, jump_ref, pad_ref, psend, precv, pairs), scratch = (
+        scratch[:9], scratch[9:],
     )
     fine_bufs, coarse_bufs = scratch[:5], scratch[5:8]
     send_sem, recv_sem, all_send, all_recv, pos_send, pos_recv = scratch[8:]
     chunk = 4 * LANES
-    per = packed_ref.shape[0] // ndevice
+    split = 4
+    per = 2 * split
     npoint = ten_ref.shape[1]
     nx, ny, nz = shift.shape
     zero, unit = jnp.zeros((), jnp.bfloat16), jnp.ones((), jnp.bfloat16)
@@ -517,19 +518,6 @@
 
     lax.fori_loop(1, ndevice, hello, 0)
 
-    fetch(7).wait()
-
-    def load(x, carry):
-        inverse[FINE + x, :ny, :nz] = 1.0 / (6.0 + shift[x])
-        return carry
-
-    lax.fori_loop(0, nx, load, 0, unroll=2)
-    pair_up(shift, pairs)
-    pooled(pairs, cinverse, lambda total: 1.0 / (6.0 + total))
-    fine = fine_field(inverse, fine_bufs, (send_sem.at[0], recv_sem.at[0]))
-    coarse = coarse_field(cinverse, coarse_bufs, (send_sem.at[1], recv_sem.at[1]))
-    fine.pack()
-    coarse.pack()
     fetch(0).wait()
     psend[0, :3] = pos_ref[:, npoint - LANES :]
     psend[1, :3] = pos_ref[:, :LANES]
@@ -542,8 +530,6 @@
         return carry
 
     lax.fori_loop(1, npoint // LANES, spread_out, 0, unroll=7)
-
-    pl.semaphore_wait(barrier, ndevice - 1)
 
     def edge(side, incoming):
         return pltpu.make_async_remote_copy(
@@ -555,11 +541,6 @@
             device_id_type=MESH,
         )
 
-    for side in range(2):
-        edge(side, False).start()
-    fine.start(FIRST)
-    coarse.start(FIRST)
-
     def classes(here):
         return own_ref[:, here] + ndevice * jnp.right_shift(cel_ref[:, here], 16)
 
@@ -596,6 +577,82 @@
 
     lax.fori_loop(0, npoint // chunk, order, carry_ref[...], unroll=2)
 
+    pl.semaphore_wait(barrier, ndevice - 1)
+
+    for side in range(2):
+        edge(side, False).start()
+    def rows_of(device):
+        return pl.ds(pl.multiple_of(device * per, per), per)
+
+    def deal(part, p, incoming):
+        return pltpu.make_async_remote_copy(
+            src_ref=packed_ref.at[part, rows_of(other(p))],
+            dst_ref=got_ref.at[part, rows_of(other(ndevice - p) if incoming else me)],
+            send_sem=all_send.at[part, p],
+            recv_sem=all_recv.at[part, p],
+            device_id=place_of(other(p)),
+            device_id_type=MESH,
+        )
+
+    def send(part):
+        def one(p, carry):
+            deal(part, p, False).start()
+            return carry
+
+        lax.fori_loop(1, ndevice, one, 0)
+
+    def pack(part, pieces):
+        total_ref[...] = jnp.zeros_like(total_ref)
+
+        def some(i, carry):
+            here = pl.ds(pl.multiple_of(i * chunk, chunk), chunk)
+            rank = rank_ref[:, here]
+            slots = jnp.where(hot_rows(jnp.bitwise_and(rank, BIN - 1), BIN), unit, zero)
+            row = own_ref[:, here] * split + jnp.right_shift(rank, 8)
+            hot = hot_rows(row, total_ref.shape[0])
+            total = total_ref[...]
+            for piece in pieces(here):
+                left = jnp.where(hot, piece, zero)
+                total = total + lax.dot_general(
+                    left, slots, (((1,), (1,)), ((), ())), preferred_element_type=jnp.float32
+                )
+            total_ref[...] = total
+            return carry
+
+        lax.fori_loop(0, npoint // chunk, some, 0, unroll=2)
+        sub = lax.broadcasted_iota(jnp.int32, (per, LANES), 0)
+        for t in range(ndevice // 2):
+            one = total_ref[t * per : t * per + per, :LANES]
+            two = total_ref[t * per : t * per + per, LANES:]
+            at = 2 * t * per
+            packed_ref[part, at : at + per] = jnp.where(sub < split, one, pltpu.roll(two, split, 0))
+            packed_ref[part, at + per : at + 2 * per] = jnp.where(
+                sub < split, pltpu.roll(one, split, 0), two
+            )
+
+    def digits(here):
+        cell = cel_ref[:, here] + 1
+        for bits in (0, 8, 16):
+            digit = jnp.left_shift(jnp.bitwise_and(jnp.right_shift(cell, bits), 255), bits)
+            yield digit.astype(jnp.float32).astype(jnp.bfloat16)
+
+    pack(1, digits)
+    send(1)
+    fetch(7).wait()
+
+    def load(x, carry):
+        inverse[FINE + x, :ny, :nz] = 1.0 / (6.0 + shift[x])
+        return carry
+
+    lax.fori_loop(0, nx, load, 0, unroll=2)
+    pair_up(shift, pairs)
+    pooled(pairs, cinverse, lambda total: 1.0 / (6.0 + total))
+    fine = fine_field(inverse, fine_bufs, (send_sem.at[0], recv_sem.at[0]))
+    coarse = coarse_field(cinverse, coarse_bufs, (send_sem.at[1], recv_sem.at[1]))
+    fine.pack()
+    coarse.pack()
+    fine.start(FIRST)
+    coarse.start(FIRST)
     for k in (4, 3, 2, 1):
         fetch(k).wait()
     for side in range(2):
@@ -635,61 +692,23 @@
 
     lax.fori_loop(0, npoint // (2 * LANES), pull, 0, unroll=2)
 
+    pack(0, lambda here: split3(jump_ref[:, here])[:2])
+    send(0)
+    for part in range(2):
+        got_ref[part, rows_of(me)] = packed_ref[part, rows_of(me)]
     fine.finish(FIRST)
     fine.unpack()
     fine.start(LAST)
     coarse.finish(FIRST)
     coarse.unpack()
     coarse.start(LAST)
-
-    packed_ref[...] = jnp.zeros_like(packed_ref)
-
-    def pack(i, carry):
-        here = pl.ds(pl.multiple_of(i * chunk, chunk), chunk)
-        rank = rank_ref[:, here]
-        slots = jnp.where(hot_rows(jnp.bitwise_and(rank, BIN - 1), BIN), unit, zero)
-        row = own_ref[:, here] * per + jnp.right_shift(rank, 8)
-        here_value = hot_rows(row, packed_ref.shape[0])
-        here_cell = hot_rows(row + per // 2, packed_ref.shape[0])
-        cell = cel_ref[:, here] + 1
-        total = packed_ref[...]
-        for piece, bits in zip(split3(jump_ref[:, here]), (0, 8, 16)):
-            digit = jnp.left_shift(jnp.bitwise_and(jnp.right_shift(cell, bits), 255), bits)
-            digit = digit.astype(jnp.float32).astype(jnp.bfloat16)
-            left = jnp.where(here_value, piece, jnp.where(here_cell, digit, zero))
-            total = total + lax.dot_general(
-                left, slots, (((1,), (1,)), ((), ())), preferred_element_type=jnp.float32
-            )
-        packed_ref[...] = total
-        return carry
-
-    lax.fori_loop(0, npoint // chunk, pack, 0, unroll=2)
-
-    def rows_of(device):
-        return pl.ds(pl.multiple_of(device * per, per), per)
-
-    def deal(p, incoming):
-        return pltpu.make_async_remote_copy(
-            src_ref=packed_ref.at[rows_of(other(p))],
-            dst_ref=got_ref.at[rows_of(other(ndevice - p) if incoming else me)],
-            send_sem=all_send.at[p],
-            recv_sem=all_recv.at[p],
-            device_id=place_of(other(p)),
-            device_id_type=MESH,
-        )
-
-    def send(p, carry):
-        deal(p, False).start()
-        return carry
-
-    lax.fori_loop(1, ndevice, send, 0)
-    got_ref[rows_of(me)] = packed_ref[rows_of(me)]
     fine.finish(LAST)
     coarse.finish(LAST)
 
     def receive(p, carry):
-        deal(p, False).wait_send()
-        deal(p, True).wait_recv()
+        for part in range(2):
+            deal(part, p, False).wait_send()
+            deal(part, p, True).wait_recv()
         return carry
 
     lax.fori_loop(1, ndevice, receive, 0)
@@ -697,20 +716,19 @@
 
 def front(
     positions, normals, tension, edge_weight, connectivity, owner_ids, cell_map, shift,
-    ndevice, capacity, nbin,
+    ndevice, nbin,
 ):
     npoint = tension.shape[0]
     nx, ny, nz = shift.shape
-    per = max(8, 2 * (capacity // BIN))
     vmem = pl.BlockSpec(memory_space=pltpu.VMEM)
     wide, cwide = wide_shapes(nx, ny, nz)
     return pl.pallas_call(
-        functools.partial(front_kernel, ndevice, capacity, nbin),
+        functools.partial(front_kernel, ndevice, nbin),
         in_specs=[pl.BlockSpec(memory_space=pltpu.HBM)] * 8,
         out_specs=[vmem] * 4,
         out_shape=[
             jax.ShapeDtypeStruct(shape, jnp.float32)
-            for shape in ((3, npoint), (ndevice * per, BIN), wide, cwide)
+            for shape in ((3, npoint), (2, 8 * ndevice, LANES), wide, cwide)
         ],
         scratch_shapes=[
             buf(3, npoint),
@@ -721,7 +739,8 @@
             pltpu.VMEM((1, npoint), jnp.int32),
             pltpu.VMEM((1, npoint), jnp.int32),
             buf(nx, ny, nz),
-            buf(ndevice * per, BIN),
+            buf(2, 8 * ndevice, LANES),
+            buf(4 * ndevice, BIN),
             buf(nbin * ndevice, 1),
             pltpu.VMEM((1, npoint), jnp.int32),
             buf(1, npoint),
@@ -733,7 +752,7 @@
         + fine_scratch(nx, ny, nz)
         + coarse_scratch(nx, ny, nz)
         + [pltpu.SemaphoreType.DMA((2, 10))] * 2
-        + [pltpu.SemaphoreType.DMA((ndevice,))] * 2
+        + [pltpu.SemaphoreType.DMA((2, ndevice))] * 2
         + [pltpu.SemaphoreType.DMA((2,))] * 2
         + [pltpu.SemaphoreType.DMA((8,))],
         compiler_params=pltpu.CompilerParams(
@@ -755,7 +774,7 @@
 
 def scatter_kernel(
     nbin, rhs_hbm, got_ref, force_ref, out_ref, force_hbm,
-    rhs_ref, acc_ref, flat_ref, ends_ref, bound_ref, sems,
+    rhs_ref, acc_ref, ends_ref, bound_ref, sems,
 ):
     nrow, nz = rhs_ref.shape
     fetch = pltpu.make_async_copy(rhs_hbm, rhs_ref, sems.at[1])
@@ -763,15 +782,11 @@
     put = pltpu.make_async_copy(force_ref, force_hbm, sems.at[2])
     put.start()
     nsource = bound_ref.shape[0]
-    per = got_ref.shape[0] // nsource
-    chunks = per // 2 * (BIN // LANES)
+    per = got_ref.shape[1] // nsource
+    chunks = per
     rows = nrow // nbin
-    nflat = got_ref.shape[0]
-    for half in range(BIN // LANES):
-        flat_ref[half * nflat : (half + 1) * nflat] = got_ref[:, half * LANES : (half + 1) * LANES]
-    got = got_ref[...].reshape(nsource, per, BIN)
-    cell_row = lax.broadcasted_iota(jnp.int32, got.shape, 1) >= per // 2
-    used = cell_row & (got > 0.0)
+    got = got_ref[1].reshape(nsource, per, LANES)
+    used = got > 0.0
     lane = lax.broadcasted_iota(jnp.int32, (nsource, LANES), 1)
     ends = jnp.zeros((nsource, LANES), jnp.float32)
     for b in range(nbin):
@@ -801,9 +816,10 @@
             highs, lows, cols = [], [], []
             for _ in range(GROUP):
                 at = jnp.minimum(source, nsource - 1)
-                row = jnp.bitwise_and(chunk, 1) * nflat + at * per + jnp.right_shift(chunk, 1)
-                value = flat_ref[pl.ds(row, 1)]
-                cell = flat_ref[pl.ds(row + per // 2, 1)].astype(jnp.int32) - 1
+                half = jnp.bitwise_and(chunk, 1)
+                row = at * per + half * (per // 2) + jnp.right_shift(chunk, 1)
+                value = got_ref[0, pl.ds(row, 1)]
+                cell = got_ref[1, pl.ds(row, 1)].astype(jnp.int32) - 1
                 fits = (jnp.right_shift(cell, 16) == b) & (source < nsource)
                 half = jnp.bitwise_and(jnp.right_shift(cell, 8), 1)
                 place = half * rows + jnp.bitwise_and(jnp.right_shift(cell, 9), rows - 1)
@@ -856,14 +872,13 @@
         scratch_shapes=[
             pltpu.VMEM((nrow, nz), jnp.float32),
             pltpu.VMEM((BIN, BIN), jnp.float32),
-            pltpu.VMEM((got.size // LANES, LANES), jnp.float32),
             pltpu.VMEM((nsource, LANES), jnp.int32),
             pltpu.SMEM((nsource, LANES), jnp.int32),
             pltpu.SemaphoreType.DMA((3,)),
         ],
         compiler_params=pltpu.CompilerParams(vmem_limit_bytes=24 * 2**20),
         cost_estimate=pl.CostEstimate(
-            flops=4 * nrow * nz * got.size // 4, bytes_accessed=4000000, transcendentals=0
+            flops=4 * nrow * nz * got.size // 2, bytes_accessed=4000000, transcendentals=0
         ),
     )(in_hbm(rhs.reshape(nrow, nz)), got, force)
     return out.reshape(nx, ny, nz), force
@@ -880,13 +895,11 @@
     cell_map,
     connectivity,
 ):
-    npoint = positions.shape[1]
     ndevice = lax.axis_size(AXES)
-    capacity = 4 * npoint // ndevice
     nbin = pressure_rhs.size // (BIN * BIN)
     surface_force, got, inverse, cinverse = front(
         positions, normals, tension, edge_weight, connectivity, owner_map[:, 0], cell_map,
-        shift_diag, ndevice, capacity, nbin,
+        shift_diag, ndevice, nbin,
     )
     forcing, surface_force = scatter(pressure_rhs, got, surface_force, ndevice, nbin)
     pressure = cycle(forcing, shift_diag, inverse, cinverse)

time: 80 us -> 82.1 us (1.026)
  Pallas kernels: 78.1 us -> 80.6 us
    pallas_call x1, Pallas kernels: 25.6 us -> 27.4 us  [front(): pl.pallas_call(functools.partial(front_kernel, ndevice, nbin), in_specs=[...]
where the time goes in v5:
time: 82.1 us; the launch traced here: 82.2 us
  Pallas kernels  80.6 us (98%)
  local copies, waits for them, and re-layouts  0.97 us (1%)
    pallas_call x1, Pallas kernels, cycle(): pl.pallas_call(cycle_kernel, in_specs=[vmem, pl.BlockSpec(memory_space=pl...  43.4 us
    pallas_call x1, Pallas kernels, front(): pl.pallas_call(functools.partial(front_kernel, ndevice, nbin), in_specs=[...  27.4 us
    pallas_call x1, Pallas kernels, scatter(): pl.pallas_call(functools.partial(scatter_kernel, nbin), in_specs=[hbm, vm...  9.72 us

profile of v5, /device:TPU:15, one launch (start us, length us, event | category | flops | bytes accessed | tf_op | source)
XLA Modules:
  0.0 82.2 jit_solution(10632816975811565480)
XLA Ops:
  0.6 27.4 %shard_map.104 = (f32[3,8192]{1,0:T(4,128)S(1)}, f32[2,256,128]{2,1,0:T(8,128)S(1)}, f32[22,40,640]{2,1,0:T(8,128)S(1)}, f32[18,32,384]{2,1,0:T(8,128)S(1)}) custom-call(f32[3,8192]{1,0:T(4,128)} %refs_0_.1, f32[3,8192]{1,0:T(4,128)} %refs_1_.1, f32[1,8192]{1,0:T(1,128)} %bitcast.6, f32[6,8192]{1,0:T(8,128)} %refs_3_.1, s32[6,8192]{1,0:T(8,128)} %refs_4_.1, ...), custom_call_target="tpu_custom_call" | custom-call | tf_op jit(solution)/shard_map/pallas_call | solution.py:725
  28.1 9.7 %shard_map.105 = (f32[512,512]{1,0:T(8,128)S(1)}, f32[3,8192]{1,0:T(4,128)}) custom-call(f32[512,512]{1,0:T(8,128)} %bitcast.9, f32[2,256,128]{2,1,0:T(8,128)S(1)} %get-tuple-element.8.got_ref, f32[3,8192]{1,0:T(4,128)S(1)} %get-tuple-element.9.force_ref), custom_call_target="tpu_custom_call" | custom-call | flops 34359738368 | bytes 4000000 | tf_op jit(solution)/shard_map/pallas_call | solution.py:864
  37.8 43.4 %shard_map.106 = f32[16,32,512]{2,1,0:T(8,128)S(1)} custom-call(f32[16,32,512]{2,1,0:T(8,128)S(1)} %bitcast.5, f32[16,32,512]{2,1,0:T(8,128)} %shift_hbm.1, f32[22,40,640]{2,1,0:T(8,128)S(1)} %get-tuple-element.11.inverse, f32[18,32,384]{2,1,0:T(8,128)S(1)} %get-tuple-element.12.cinverse), custom_call_target="tpu_custom_call" | custom-call | tf_op jit(solution)/shard_map/pallas_call | solution.py:439
  81.2 1.0 %copy.12 = f32[16,32,512]{2,1,0:T(8,128)} copy(f32[16,32,512]{2,1,0:T(8,128)S(1)} %shard_map.106) | data formatting | bytes 2097152

commit v6 on v5

--- a/solution.py
+++ b/solution.py
@@ -274,8 +274,8 @@
 
     along_z = halves(nz, nz // 2, 1)
     along_y = halves(cx * ny // 2, cx * ny, 0)
-    flat = sum(jnp.dot(p, along_z, preferred_element_type=jnp.float32) for p in split3(flat))
-    flat = sum(jnp.dot(along_y, p, preferred_element_type=jnp.float32) for p in split3(flat))
+    flat = sum(jnp.dot(p, along_z, preferred_element_type=jnp.float32) for p in split3(flat)[:2])
+    flat = sum(jnp.dot(along_y, p, preferred_element_type=jnp.float32) for p in split3(flat)[:2])
     out = after(0.5 * flat).reshape(cx, ny // 2, nz // 2)
     into[depth : depth + cx, : ny // 2, : nz // 2] = out
 
@@ -392,9 +392,6 @@
     coarse.finish(FIRST)
     coarse.unpack()
     coarse.start(LAST)
-    field.finish(FIRST)
-    field.unpack()
-    field.start(LAST)
     coarse.finish(LAST)
 
     pairs_of = factors(COARSE_SMOOTH)
@@ -404,13 +401,16 @@
         sweep(
             crhs, cinverse, cbufs[(k - 1) % 2], cbufs[k % 2], cupdate, k, cslabs - k, pairs_of[k]
         )
+    field.finish(FIRST)
+    field.unpack()
+    field.start(LAST)
     fix = cbufs[(COARSE_SMOOTH - 1) % 2]
 
+    flat = fix[low : low + count].reshape(count * cny, cnz)
+
+    tall = sum(jnp.dot(fan_y, p, preferred_element_type=jnp.float32) for p in split3(flat)[:2])
+    full = sum(jnp.dot(p, fan_z, preferred_element_type=jnp.float32) for p in split3(tall)[:2])
     field.finish(LAST)
-    flat = fix[low : low + count].reshape(count * cny, cnz)
-
-    tall = sum(jnp.dot(fan_y, p, preferred_element_type=jnp.float32) for p in split3(flat))
-    full = sum(jnp.dot(p, fan_z, preferred_element_type=jnp.float32) for p in split3(tall))
     for j in range(count):
         part = full[j * fny : (j + 1) * fny]
         for half in range(2):
@@ -457,6 +457,8 @@
 
 
 BIN = 256
+BIN_SHIFT = 16
+BIN_CELLS = 1 << BIN_SHIFT
 AXES = ("gx", "gy", "gz")
 
 
@@ -464,11 +466,23 @@
     return pltpu.with_memory_space_constraint(x, pltpu.HBM)
 
 
-def hot_rows(index, rows, dtype=jnp.bfloat16):
-    r = lax.broadcasted_iota(jnp.int32, (rows, index.shape[1]), 0)
+def levels(rows):
+    level = lax.broadcasted_iota(jnp.int32, (rows, LANES), 0)
     if rows > BIN:
-        return r == index
-    return r.astype(jnp.float32).astype(dtype) == index.astype(jnp.float32).astype(dtype)
+        return level
+    return level.astype(jnp.float32).astype(jnp.bfloat16)
+
+
+def hot_rows(level, index, values=None):
+    if level.dtype != jnp.int32:
+        index = index.astype(jnp.float32).astype(jnp.bfloat16)
+    columns = []
+    for at in range(0, index.shape[1], LANES):
+        here = slice(at, at + LANES)
+        value = jnp.ones((), jnp.bfloat16) if values is None else values[:, here]
+        same = level == index[:, here]
+        columns.append(jnp.where(same, value, jnp.zeros((), jnp.bfloat16)))
+    return jnp.concatenate(columns, axis=1)
 
 
 def place_of(index):
@@ -505,7 +519,8 @@
     per = 2 * split
     npoint = ten_ref.shape[1]
     nx, ny, nz = shift.shape
-    zero, unit = jnp.zeros((), jnp.bfloat16), jnp.ones((), jnp.bfloat16)
+    class_level, slot_level = levels(nbin * ndevice), levels(BIN)
+    row_level = levels(total_ref.shape[0])
     me = lax.axis_index(AXES)
     barrier = pltpu.get_barrier_semaphore()
 
@@ -542,11 +557,11 @@
         )
 
     def classes(here):
-        return own_ref[:, here] + ndevice * jnp.right_shift(cel_ref[:, here], 16)
+        return own_ref[:, here] + ndevice * jnp.right_shift(cel_ref[:, here], BIN_SHIFT)
 
     def count(i, total):
         here = pl.ds(pl.multiple_of(i * chunk, chunk), chunk)
-        hot = jnp.where(hot_rows(classes(here), nbin * ndevice), 1.0, 0.0).astype(jnp.float32)
+        hot = hot_rows(class_level, classes(here)).astype(jnp.float32)
         return total + (
             hot[:, :LANES] + hot[:, LANES : 2 * LANES]
             + (hot[:, 2 * LANES : 3 * LANES] + hot[:, 3 * LANES :])
@@ -569,7 +584,7 @@
 
     def order(i, carry):
         here = pl.ds(pl.multiple_of(i * chunk, chunk), chunk)
-        ones = jnp.where(hot_rows(classes(here), nbin * ndevice), unit, zero)
+        ones = hot_rows(class_level, classes(here))
         earlier = jnp.dot(ones, before, preferred_element_type=jnp.float32) + carry
         wide = ones.astype(jnp.float32)
         rank_ref[:, here] = jnp.sum(wide * earlier, axis=0, keepdims=True).astype(jnp.int32)
@@ -577,10 +592,26 @@
 
     lax.fori_loop(0, npoint // chunk, order, carry_ref[...], unroll=2)
 
+    fetch(7).wait()
+
+    def load(x, carry):
+        inverse[FINE + x, :ny, :nz] = 1.0 / (6.0 + shift[x])
+        return carry
+
+    lax.fori_loop(0, nx, load, 0, unroll=2)
+    pair_up(shift, pairs)
+    pooled(pairs, cinverse, lambda total: 1.0 / (6.0 + total))
+    fine = fine_field(inverse, fine_bufs, (send_sem.at[0], recv_sem.at[0]))
+    coarse = coarse_field(cinverse, coarse_bufs, (send_sem.at[1], recv_sem.at[1]))
+    fine.pack()
+    coarse.pack()
     pl.semaphore_wait(barrier, ndevice - 1)
 
     for side in range(2):
         edge(side, False).start()
+    fine.start(FIRST)
+    coarse.start(FIRST)
+
     def rows_of(device):
         return pl.ds(pl.multiple_of(device * per, per), per)
 
@@ -604,22 +635,23 @@
     def pack(part, pieces):
         total_ref[...] = jnp.zeros_like(total_ref)
 
+        big = npoint // 2
+
         def some(i, carry):
-            here = pl.ds(pl.multiple_of(i * chunk, chunk), chunk)
+            here = pl.ds(pl.multiple_of(i * big, big), big)
             rank = rank_ref[:, here]
-            slots = jnp.where(hot_rows(jnp.bitwise_and(rank, BIN - 1), BIN), unit, zero)
+            slots = hot_rows(slot_level, jnp.bitwise_and(rank, BIN - 1))
             row = own_ref[:, here] * split + jnp.right_shift(rank, 8)
-            hot = hot_rows(row, total_ref.shape[0])
-            total = total_ref[...]
-            for piece in pieces(here):
-                left = jnp.where(hot, piece, zero)
-                total = total + lax.dot_general(
-                    left, slots, (((1,), (1,)), ((), ())), preferred_element_type=jnp.float32
-                )
-            total_ref[...] = total
+            left = [hot_rows(row_level, row, piece) for piece in pieces(here)]
+            both = lax.dot_general(
+                jnp.concatenate(left, axis=0), slots, (((1,), (1,)), ((), ())),
+                preferred_element_type=jnp.float32,
+            )
+            count = total_ref.shape[0]
+            total_ref[...] += sum(both[k * count : k * count + count] for k in range(len(left)))
             return carry
 
-        lax.fori_loop(0, npoint // chunk, some, 0, unroll=2)
+        lax.fori_loop(0, npoint // big, some, 0)
         sub = lax.broadcasted_iota(jnp.int32, (per, LANES), 0)
         for t in range(ndevice // 2):
             one = total_ref[t * per : t * per + per, :LANES]
@@ -638,21 +670,6 @@
 
     pack(1, digits)
     send(1)
-    fetch(7).wait()
-
-    def load(x, carry):
-        inverse[FINE + x, :ny, :nz] = 1.0 / (6.0 + shift[x])
-        return carry
-
-    lax.fori_loop(0, nx, load, 0, unroll=2)
-    pair_up(shift, pairs)
-    pooled(pairs, cinverse, lambda total: 1.0 / (6.0 + total))
-    fine = fine_field(inverse, fine_bufs, (send_sem.at[0], recv_sem.at[0]))
-    coarse = coarse_field(cinverse, coarse_bufs, (send_sem.at[1], recv_sem.at[1]))
-    fine.pack()
-    coarse.pack()
-    fine.start(FIRST)
-    coarse.start(FIRST)
     for k in (4, 3, 2, 1):
         fetch(k).wait()
     for side in range(2):
@@ -690,7 +707,7 @@
             jump_ref[:, here] = jnp.sum(force * nrm_ref[:, here], axis=0, keepdims=True)
         return carry
 
-    lax.fori_loop(0, npoint // (2 * LANES), pull, 0, unroll=2)
+    lax.fori_loop(0, npoint // (2 * LANES), pull, 0, unroll=4)
 
     pack(0, lambda here: split3(jump_ref[:, here])[:2])
     send(0)
@@ -790,7 +807,7 @@
     lane = lax.broadcasted_iota(jnp.int32, (nsource, LANES), 1)
     ends = jnp.zeros((nsource, LANES), jnp.float32)
     for b in range(nbin):
-        inside = jnp.where(used & (got <= float((b + 1) * BIN * BIN)), 1.0, 0.0)
+        inside = jnp.where(used & (got <= float((b + 1) * BIN_CELLS)), 1.0, 0.0)
         total = jnp.sum(jnp.sum(inside, axis=1), axis=1, keepdims=True)
         ends = jnp.where(lane == b + 1, total, ends)
     ends_ref[...] = ends.astype(jnp.int32)
@@ -798,9 +815,8 @@
     copy.start()
     copy.wait()
     fetch.wait()
-    level = lax.broadcasted_iota(jnp.int32, (BIN, LANES), 0).astype(jnp.float32)
-    level = level.astype(jnp.bfloat16)
     zero, unit = jnp.zeros((), jnp.bfloat16), jnp.ones((), jnp.bfloat16)
+    row_level, col_level = levels(2 * rows), levels(BIN)
 
     def quarter(b, carry):
         def span(source):
@@ -820,29 +836,30 @@
                 row = at * per + half * (per // 2) + jnp.right_shift(chunk, 1)
                 value = got_ref[0, pl.ds(row, 1)]
                 cell = got_ref[1, pl.ds(row, 1)].astype(jnp.int32) - 1
-                fits = (jnp.right_shift(cell, 16) == b) & (source < nsource)
+                fits = (jnp.right_shift(cell, BIN_SHIFT) == b) & (source < nsource)
                 half = jnp.bitwise_and(jnp.right_shift(cell, 8), 1)
                 place = half * rows + jnp.bitwise_and(jnp.right_shift(cell, 9), rows - 1)
-                place = jnp.where(fits, place, BIN).astype(jnp.float32).astype(jnp.bfloat16)
+                place = jnp.where(fits, place, 2 * rows).astype(jnp.float32).astype(jnp.bfloat16)
                 col = jnp.bitwise_and(cell, BIN - 1).astype(jnp.float32).astype(jnp.bfloat16)
                 first = value.astype(jnp.bfloat16)
                 second = (value - first.astype(jnp.float32)).astype(jnp.bfloat16)
-                same = level == place
+                same = row_level == place
                 highs.append(jnp.where(same, first, zero))
                 lows.append(jnp.where(same, second, zero))
-                cols.append(jnp.where(level == col, unit, zero))
+                cols.append(jnp.where(col_level == col, unit, zero))
                 over = chunk + 1 >= last
                 source = jnp.where(over, source + 1, source)
                 following = span(source)
                 chunk = jnp.where(over, following[0], chunk + 1)
                 last = jnp.where(over, following[1], last)
-            high = jnp.concatenate(highs, axis=1)
-            low = jnp.concatenate(lows, axis=1)
-            right = jnp.concatenate(cols, axis=1)
-            dims = (((1,), (1,)), ((), ()))
-            acc_ref[...] += lax.dot_general(
-                high, right, dims, preferred_element_type=jnp.float32
-            ) + lax.dot_general(low, right, dims, preferred_element_type=jnp.float32)
+            left = jnp.concatenate(
+                [jnp.concatenate(highs, axis=1), jnp.concatenate(lows, axis=1)], axis=0
+            )
+            both = lax.dot_general(
+                left, jnp.concatenate(cols, axis=1), (((1,), (1,)), ((), ())),
+                preferred_element_type=jnp.float32,
+            )
+            acc_ref[...] += both[: 2 * rows] + both[2 * rows :]
             return source, chunk, last
 
         lax.while_loop(lambda state: state[0] < nsource, work, (jnp.int32(0), *span(0)))
@@ -871,7 +888,7 @@
         ],
         scratch_shapes=[
             pltpu.VMEM((nrow, nz), jnp.float32),
-            pltpu.VMEM((BIN, BIN), jnp.float32),
+            pltpu.VMEM((2 * nrow // nbin, BIN), jnp.float32),
             pltpu.VMEM((nsource, LANES), jnp.int32),
             pltpu.SMEM((nsource, LANES), jnp.int32),
             pltpu.SemaphoreType.DMA((3,)),
@@ -896,7 +913,7 @@
     connectivity,
 ):
     ndevice = lax.axis_size(AXES)
-    nbin = pressure_rhs.size // (BIN * BIN)
+    nbin = pressure_rhs.size // BIN_CELLS
     surface_force, got, inverse, cinverse = front(
         positions, normals, tension, edge_weight, connectivity, owner_map[:, 0], cell_map,
         shift_diag, ndevice, nbin,

time: 82.1 us -> 76.4 us (0.931); the launches traced: 82.2 us -> 75.6 us
  Pallas kernels: 80.6 us -> 74 us
    pallas_call x1, Pallas kernels: 27.4 us -> 22.6 us  [front(): pl.pallas_call(functools.partial(front_kernel, ndevice, nbin), in_specs=[...]
    pallas_call x1, Pallas kernels: 43.4 us -> 40.3 us  [cycle(): pl.pallas_call(cycle_kernel, in_specs=[vmem, pl.BlockSpec(memory_space=pl...]
    pallas_call x1, Pallas kernels: 9.72 us -> 11.1 us  [scatter(): pl.pallas_call(functools.partial(scatter_kernel, nbin), in_specs=[hbm, vm...]
where the time goes in v6:
time: 76.4 us; the launch traced here: 75.6 us
  Pallas kernels  74 us (97%)
  local copies, waits for them, and re-layouts  0.97 us (1%)
    pallas_call x1, Pallas kernels, cycle(): pl.pallas_call(cycle_kernel, in_specs=[vmem, pl.BlockSpec(memory_space=pl...  40.3 us
    pallas_call x1, Pallas kernels, front(): pl.pallas_call(functools.partial(front_kernel, ndevice, nbin), in_specs=[...  22.6 us
    pallas_call x1, Pallas kernels, scatter(): pl.pallas_call(functools.partial(scatter_kernel, nbin), in_specs=[hbm, vm...  11.1 us

profile of v6, /device:TPU:15, one launch (start us, length us, event | category | flops | bytes accessed | tf_op | source)
XLA Modules:
  0.0 75.6 jit_solution(12194330253007863367)
XLA Ops:
  0.6 22.6 %shard_map.104 = (f32[3,8192]{1,0:T(4,128)S(1)}, f32[2,256,128]{2,1,0:T(8,128)S(1)}, f32[22,40,640]{2,1,0:T(8,128)S(1)}, f32[18,32,384]{2,1,0:T(8,128)S(1)}) custom-call(f32[3,8192]{1,0:T(4,128)} %refs_0_.1, f32[3,8192]{1,0:T(4,128)} %refs_1_.1, f32[1,8192]{1,0:T(1,128)} %bitcast.6, f32[6,8192]{1,0:T(8,128)} %refs_3_.1, s32[6,8192]{1,0:T(8,128)} %refs_4_.1, ...), custom_call_target="tpu_custom_call" | custom-call | tf_op jit(solution)/shard_map/pallas_call | solution.py:742
  23.3 11.1 %shard_map.105 = (f32[512,512]{1,0:T(8,128)S(1)}, f32[3,8192]{1,0:T(4,128)}) custom-call(f32[512,512]{1,0:T(8,128)} %bitcast.9, f32[2,256,128]{2,1,0:T(8,128)S(1)} %get-tuple-element.8.got_ref, f32[3,8192]{1,0:T(4,128)S(1)} %get-tuple-element.9.force_ref), custom_call_target="tpu_custom_call" | custom-call | flops 34359738368 | bytes 4000000 | tf_op jit(solution)/shard_map/pallas_call | solution.py:881
  34.3 40.3 %shard_map.106 = f32[16,32,512]{2,1,0:T(8,128)S(1)} custom-call(f32[16,32,512]{2,1,0:T(8,128)S(1)} %bitcast.5, f32[16,32,512]{2,1,0:T(8,128)} %shift_hbm.1, f32[22,40,640]{2,1,0:T(8,128)S(1)} %get-tuple-element.11.inverse, f32[18,32,384]{2,1,0:T(8,128)S(1)} %get-tuple-element.12.cinverse), custom_call_target="tpu_custom_call" | custom-call | tf_op jit(solution)/shard_map/pallas_call | solution.py:439
  74.6 1.0 %copy.12 = f32[16,32,512]{2,1,0:T(8,128)} copy(f32[16,32,512]{2,1,0:T(8,128)S(1)} %shard_map.106) | data formatting | bytes 2097152

commit v7 on v6

--- a/solution.py
+++ b/solution.py
@@ -457,7 +457,7 @@
 
 
 BIN = 256
-BIN_SHIFT = 16
+BIN_SHIFT = 15
 BIN_CELLS = 1 << BIN_SHIFT
 AXES = ("gx", "gy", "gz")
 
@@ -585,12 +585,13 @@
     def order(i, carry):
         here = pl.ds(pl.multiple_of(i * chunk, chunk), chunk)
         ones = hot_rows(class_level, classes(here))
-        earlier = jnp.dot(ones, before, preferred_element_type=jnp.float32) + carry
+        earlier = jnp.dot(ones, before, preferred_element_type=jnp.float32)
         wide = ones.astype(jnp.float32)
-        rank_ref[:, here] = jnp.sum(wide * earlier, axis=0, keepdims=True).astype(jnp.int32)
-        return carry + jnp.sum(wide, axis=1, keepdims=True)
-
-    lax.fori_loop(0, npoint // chunk, order, carry_ref[...], unroll=2)
+        rank = jnp.sum(wide * (earlier + carry), axis=0, keepdims=True)
+        rank_ref[:, here] = rank.astype(jnp.int32)
+        return carry + (earlier[:, chunk - 1 :] + wide[:, chunk - 1 :])
+
+    lax.fori_loop(0, npoint // chunk, order, carry_ref[...], unroll=4)
 
     fetch(7).wait()
 
@@ -786,21 +787,20 @@
     )
 
 
-GROUP = 24
+GROUP = 72
 
 
 def scatter_kernel(
     nbin, rhs_hbm, got_ref, force_ref, out_ref, force_hbm,
-    rhs_ref, acc_ref, ends_ref, bound_ref, sems,
+    rhs_ref, acc_ref, list_ref, chunk_ref, sems,
 ):
     nrow, nz = rhs_ref.shape
     fetch = pltpu.make_async_copy(rhs_hbm, rhs_ref, sems.at[1])
     fetch.start()
     put = pltpu.make_async_copy(force_ref, force_hbm, sems.at[2])
     put.start()
-    nsource = bound_ref.shape[0]
-    per = got_ref.shape[1] // nsource
-    chunks = per
+    per = 8
+    nsource = got_ref.shape[1] // per
     rows = nrow // nbin
     got = got_ref[1].reshape(nsource, per, LANES)
     used = got > 0.0
@@ -810,8 +810,32 @@
         inside = jnp.where(used & (got <= float((b + 1) * BIN_CELLS)), 1.0, 0.0)
         total = jnp.sum(jnp.sum(inside, axis=1), axis=1, keepdims=True)
         ends = jnp.where(lane == b + 1, total, ends)
-    ends_ref[...] = ends.astype(jnp.int32)
-    copy = pltpu.make_async_copy(ends_ref, bound_ref, sems.at[0])
+    ends = ends.astype(jnp.int32)
+    stops = pltpu.roll(ends, LANES - 1, 1)
+    firsts = jnp.right_shift(ends, 7)
+    counts = jnp.where(stops > ends, jnp.right_shift(stops + LANES - 1, 7) - firsts, 0)
+    counts = jnp.where(lane < nbin, counts, 0).astype(jnp.float32)
+    square = (nsource, nsource)
+    before = (
+        lax.broadcasted_iota(jnp.int32, square, 0) > lax.broadcasted_iota(jnp.int32, square, 1)
+    ).astype(jnp.float32).astype(jnp.bfloat16)
+    starts = jnp.dot(before, counts.astype(jnp.bfloat16), preferred_element_type=jnp.float32)
+    sums = jnp.sum(counts, axis=0, keepdims=True)
+    width = list_ref.shape[1]
+    source = lax.broadcasted_iota(jnp.int32, (nsource, width), 0)
+    position = lax.broadcasted_iota(jnp.int32, (nsource, width), 1)
+    for b in range(nbin):
+        pick = slice(b, b + 1)
+        step = position - starts[:, pick].astype(jnp.int32)
+        chunk = firsts[:, pick] + step
+        row = source * per + jnp.bitwise_and(chunk, 1) * (per // 2) + jnp.right_shift(chunk, 1)
+        inside = (step >= 0) & (step < counts[:, pick].astype(jnp.int32))
+        row = jnp.sum(jnp.where(inside, row.astype(jnp.float32), 0.0), axis=0, keepdims=True)
+        list_ref[b : b + 1] = row.astype(jnp.int32)
+        list_ref[nbin + b : nbin + b + 1] = jnp.broadcast_to(sums[:, pick], (1, width)).astype(
+            jnp.int32
+        )
+    copy = pltpu.make_async_copy(list_ref, chunk_ref, sems.at[0])
     copy.start()
     copy.wait()
     fetch.wait()
@@ -819,24 +843,17 @@
     row_level, col_level = levels(2 * rows), levels(BIN)
 
     def quarter(b, carry):
-        def span(source):
-            at = jnp.minimum(source, nsource - 1)
-            first = jnp.minimum(jnp.right_shift(bound_ref[at, b], 7), chunks - 1)
-            last = jnp.right_shift(bound_ref[at, b + 1] + LANES - 1, 7)
-            return first, jnp.maximum(last, first + 1)
-
+        total = chunk_ref[nbin + b, 0]
         acc_ref[...] = jnp.zeros_like(acc_ref)
 
-        def work(state):
-            source, chunk, last = state
+        def work(step, carry):
             highs, lows, cols = [], [], []
-            for _ in range(GROUP):
-                at = jnp.minimum(source, nsource - 1)
-                half = jnp.bitwise_and(chunk, 1)
-                row = at * per + half * (per // 2) + jnp.right_shift(chunk, 1)
+            for k in range(GROUP):
+                at = step * GROUP + k
+                row = chunk_ref[b, jnp.minimum(at, width - 1)]
                 value = got_ref[0, pl.ds(row, 1)]
                 cell = got_ref[1, pl.ds(row, 1)].astype(jnp.int32) - 1
-                fits = (jnp.right_shift(cell, BIN_SHIFT) == b) & (source < nsource)
+                fits = (jnp.right_shift(cell, BIN_SHIFT) == b) & (at < total)
                 half = jnp.bitwise_and(jnp.right_shift(cell, 8), 1)
                 place = half * rows + jnp.bitwise_and(jnp.right_shift(cell, 9), rows - 1)
                 place = jnp.where(fits, place, 2 * rows).astype(jnp.float32).astype(jnp.bfloat16)
@@ -847,11 +864,6 @@
                 highs.append(jnp.where(same, first, zero))
                 lows.append(jnp.where(same, second, zero))
                 cols.append(jnp.where(col_level == col, unit, zero))
-                over = chunk + 1 >= last
-                source = jnp.where(over, source + 1, source)
-                following = span(source)
-                chunk = jnp.where(over, following[0], chunk + 1)
-                last = jnp.where(over, following[1], last)
             left = jnp.concatenate(
                 [jnp.concatenate(highs, axis=1), jnp.concatenate(lows, axis=1)], axis=0
             )
@@ -860,9 +872,9 @@
                 preferred_element_type=jnp.float32,
             )
             acc_ref[...] += both[: 2 * rows] + both[2 * rows :]
-            return source, chunk, last
-
-        lax.while_loop(lambda state: state[0] < nsource, work, (jnp.int32(0), *span(0)))
+            return carry
+
+        lax.fori_loop(0, lax.div(total + GROUP - 1, GROUP), work, 0)
         here = pl.ds(pl.multiple_of(b * rows, rows), rows)
         for half in range(2):
             cols = slice(half * BIN, (half + 1) * BIN)
@@ -889,8 +901,8 @@
         scratch_shapes=[
             pltpu.VMEM((nrow, nz), jnp.float32),
             pltpu.VMEM((2 * nrow // nbin, BIN), jnp.float32),
-            pltpu.VMEM((nsource, LANES), jnp.int32),
-            pltpu.SMEM((nsource, LANES), jnp.int32),
+            pltpu.VMEM((2 * nbin, 8 * nsource), jnp.int32),
+            pltpu.SMEM((2 * nbin, 8 * nsource), jnp.int32),
             pltpu.SemaphoreType.DMA((3,)),
         ],
         compiler_params=pltpu.CompilerParams(vmem_limit_bytes=24 * 2**20),

time: 76.4 us -> 71.7 us (0.938)
  Pallas kernels: 74 us -> 69.9 us
    pallas_call x1, Pallas kernels: 40.3 us -> 32.6 us  [cycle(): pl.pallas_call(cycle_kernel, in_specs=[vmem, pl.BlockSpec(memory_space=pl...]
    pallas_call x1, Pallas kernels: 11.1 us -> 13.5 us  [scatter(): pl.pallas_call(functools.partial(scatter_kernel, nbin), in_specs=[hbm, vm...]
    pallas_call x1, Pallas kernels: 22.6 us -> 23.8 us  [front(): pl.pallas_call(functools.partial(front_kernel, ndevice, nbin), in_specs=[...]
where the time goes in v7:
time: 71.7 us; the launch traced here: 71.5 us
  Pallas kernels  69.9 us (97%)
  local copies, waits for them, and re-layouts  0.97 us (1%)
    pallas_call x1, Pallas kernels, cycle(): pl.pallas_call(cycle_kernel, in_specs=[vmem, pl.BlockSpec(memory_space=pl...  32.6 us
    pallas_call x1, Pallas kernels, front(): pl.pallas_call(functools.partial(front_kernel, ndevice, nbin), in_specs=[...  23.8 us
    pallas_call x1, Pallas kernels, scatter(): pl.pallas_call(functools.partial(scatter_kernel, nbin), in_specs=[hbm, vm...  13.5 us

profile of v7, /device:TPU:15, one launch (start us, length us, event | category | flops | bytes accessed | tf_op | source)
XLA Modules:
  0.0 71.5 jit_solution(11041784396823179825)
XLA Ops:
  0.6 23.8 %shard_map.104 = (f32[3,8192]{1,0:T(4,128)S(1)}, f32[2,256,128]{2,1,0:T(8,128)S(1)}, f32[22,40,640]{2,1,0:T(8,128)S(1)}, f32[18,32,384]{2,1,0:T(8,128)S(1)}) custom-call(f32[3,8192]{1,0:T(4,128)} %refs_0_.1, f32[3,8192]{1,0:T(4,128)} %refs_1_.1, f32[1,8192]{1,0:T(1,128)} %bitcast.6, f32[6,8192]{1,0:T(8,128)} %refs_3_.1, s32[6,8192]{1,0:T(8,128)} %refs_4_.1, ...), custom_call_target="tpu_custom_call" | custom-call | tf_op jit(solution)/shard_map/pallas_call | solution.py:743
  24.5 13.5 %shard_map.105 = (f32[512,512]{1,0:T(8,128)S(1)}, f32[3,8192]{1,0:T(4,128)}) custom-call(f32[512,512]{1,0:T(8,128)} %bitcast.9, f32[2,256,128]{2,1,0:T(8,128)S(1)} %get-tuple-element.8.got_ref, f32[3,8192]{1,0:T(4,128)S(1)} %get-tuple-element.9.force_ref), custom_call_target="tpu_custom_call" | custom-call | flops 34359738368 | bytes 4000000 | tf_op jit(solution)/shard_map/pallas_call | solution.py:893
  37.9 32.6 %shard_map.106 = f32[16,32,512]{2,1,0:T(8,128)S(1)} custom-call(f32[16,32,512]{2,1,0:T(8,128)S(1)} %bitcast.5, f32[16,32,512]{2,1,0:T(8,128)} %shift_hbm.1, f32[22,40,640]{2,1,0:T(8,128)S(1)} %get-tuple-element.11.inverse, f32[18,32,384]{2,1,0:T(8,128)S(1)} %get-tuple-element.12.cinverse), custom_call_target="tpu_custom_call" | custom-call | tf_op jit(solution)/shard_map/pallas_call | solution.py:439
  70.6 1.0 %copy.12 = f32[16,32,512]{2,1,0:T(8,128)} copy(f32[16,32,512]{2,1,0:T(8,128)S(1)} %shard_map.106) | data formatting | bytes 2097152

commit v8 on v7

--- a/solution.py
+++ b/solution.py
@@ -80,14 +80,14 @@
     lax.fori_loop(first, last, slab, 0, unroll=UNROLL)
 
 
-def begin(rhs, inverse, dst, update, slabs):
+def begin(rhs, inverse, dst, update, first, last):
     def slab(x, carry):
         change = inverse[x] * rhs[x] * (1.0 / centre)
         update[x] = change
         dst[x] = change
         return carry
 
-    lax.fori_loop(0, slabs, slab, 0, unroll=2)
+    lax.fori_loop(first, last, slab, 0, unroll=2)
 
 
 def near(axes):
@@ -122,7 +122,7 @@
         def _():
             pl.semaphore_signal(barrier, inc=1, device_id=where, device_id_type=MESH)
 
-    pl.semaphore_wait(barrier, peers)
+    return lambda: pl.semaphore_wait(barrier, peers)
 
 
 class Field:
@@ -323,6 +323,7 @@
     )
     bufs_a, bufs_b, bufs_c = scratch[:5], scratch[5:10], scratch[10:13]
     send_sem, recv_sem = scratch[13:]
+    arrived = greet(LINKS)
     nx, ny, nz = forcing.shape
     sems = [(send_sem.at[k], recv_sem.at[k]) for k in range(3)]
 
@@ -333,18 +334,23 @@
     lax.fori_loop(0, nx, load, 0, unroll=2)
     field = fine_field(rhs, bufs_a, sems[0])
     field.pack()
-    greet(LINKS)
+    arrived()
     field.start(FIRST)
     field.finish(FIRST)
     field.unpack()
     field.start(LAST)
-    field.finish(LAST)
-
     slabs = nx + 2 * FINE
+    low, high = FINE, FINE + nx
     pairs_of = factors(SMOOTH)
     bufs = (one, two)
-    begin(rhs, inverse, one, update, slabs)
-    for k in range(1, SMOOTH):
+    begin(rhs, inverse, one, update, low, high)
+    sweep(rhs, inverse, one, two, update, low + 1, high - 1, pairs_of[1])
+    field.finish(LAST)
+    begin(rhs, inverse, one, update, 0, low)
+    begin(rhs, inverse, one, update, high, slabs)
+    sweep(rhs, inverse, one, two, update, 1, low + 1, pairs_of[1])
+    sweep(rhs, inverse, one, two, update, high - 1, slabs - 1, pairs_of[1])
+    for k in range(2, SMOOTH):
         sweep(rhs, inverse, bufs[(k - 1) % 2], bufs[k % 2], update, k, slabs - k, pairs_of[k])
     smooth = bufs[(SMOOTH - 1) % 2]
     other = bufs[SMOOTH % 2]
@@ -392,12 +398,17 @@
     coarse.finish(FIRST)
     coarse.unpack()
     coarse.start(LAST)
-    coarse.finish(LAST)
-
     pairs_of = factors(COARSE_SMOOTH)
     cbufs = (cone, ctwo)
-    begin(crhs, cinverse, cone, cupdate, cslabs)
-    for k in range(1, COARSE_SMOOTH):
+    inner, outer = COARSE, cslabs - COARSE
+    begin(crhs, cinverse, cone, cupdate, inner, outer)
+    sweep(crhs, cinverse, cone, ctwo, cupdate, inner + 1, outer - 1, pairs_of[1])
+    coarse.finish(LAST)
+    begin(crhs, cinverse, cone, cupdate, 0, inner)
+    begin(crhs, cinverse, cone, cupdate, outer, cslabs)
+    sweep(crhs, cinverse, cone, ctwo, cupdate, 1, inner + 1, pairs_of[1])
+    sweep(crhs, cinverse, cone, ctwo, cupdate, outer - 1, cslabs - 1, pairs_of[1])
+    for k in range(2, COARSE_SMOOTH):
         sweep(
             crhs, cinverse, cbufs[(k - 1) % 2], cbufs[k % 2], cupdate, k, cslabs - k, pairs_of[k]
         )
@@ -593,6 +604,10 @@
 
     lax.fori_loop(0, npoint // chunk, order, carry_ref[...], unroll=4)
 
+    pl.semaphore_wait(barrier, ndevice - 1)
+
+    for side in range(2):
+        edge(side, False).start()
     fetch(7).wait()
 
     def load(x, carry):
@@ -606,10 +621,6 @@
     coarse = coarse_field(cinverse, coarse_bufs, (send_sem.at[1], recv_sem.at[1]))
     fine.pack()
     coarse.pack()
-    pl.semaphore_wait(barrier, ndevice - 1)
-
-    for side in range(2):
-        edge(side, False).start()
     fine.start(FIRST)
     coarse.start(FIRST)
 

time: 71.7 us -> 70 us (0.976)
  Pallas kernels: 69.9 us -> 68.2 us
    pallas_call x1, Pallas kernels: 23.8 us -> 22.8 us  [front(): pl.pallas_call(functools.partial(front_kernel, ndevice, nbin), in_specs=[...]
    pallas_call x1, Pallas kernels: 32.6 us -> 31.9 us  [cycle(): pl.pallas_call(cycle_kernel, in_specs=[vmem, pl.BlockSpec(memory_space=pl...]
where the time goes in v8:
time: 70 us; the launch traced here: 69.8 us
  Pallas kernels  68.2 us (97%)
  local copies, waits for them, and re-layouts  0.97 us (1%)
    pallas_call x1, Pallas kernels, cycle(): pl.pallas_call(cycle_kernel, in_specs=[vmem, pl.BlockSpec(memory_space=pl...  31.9 us
    pallas_call x1, Pallas kernels, front(): pl.pallas_call(functools.partial(front_kernel, ndevice, nbin), in_specs=[...  22.8 us
    pallas_call x1, Pallas kernels, scatter(): pl.pallas_call(functools.partial(scatter_kernel, nbin), in_specs=[hbm, vm...  13.5 us

profile of v8, /device:TPU:15, one launch (start us, length us, event | category | flops | bytes accessed | tf_op | source)
XLA Modules:
  0.0 69.8 jit_solution(788769093107327133)
XLA Ops:
  0.6 22.8 %shard_map.104 = (f32[3,8192]{1,0:T(4,128)S(1)}, f32[2,256,128]{2,1,0:T(8,128)S(1)}, f32[22,40,640]{2,1,0:T(8,128)S(1)}, f32[18,32,384]{2,1,0:T(8,128)S(1)}) custom-call(f32[3,8192]{1,0:T(4,128)} %refs_0_.1, f32[3,8192]{1,0:T(4,128)} %refs_1_.1, f32[1,8192]{1,0:T(1,128)} %bitcast.6, f32[6,8192]{1,0:T(8,128)} %refs_3_.1, s32[6,8192]{1,0:T(8,128)} %refs_4_.1, ...), custom_call_target="tpu_custom_call" | custom-call | tf_op jit(solution)/shard_map/pallas_call | solution.py:754
  23.5 13.5 %shard_map.105 = (f32[512,512]{1,0:T(8,128)S(1)}, f32[3,8192]{1,0:T(4,128)}) custom-call(f32[512,512]{1,0:T(8,128)} %bitcast.9, f32[2,256,128]{2,1,0:T(8,128)S(1)} %get-tuple-element.8.got_ref, f32[3,8192]{1,0:T(4,128)S(1)} %get-tuple-element.9.force_ref), custom_call_target="tpu_custom_call" | custom-call | flops 34359738368 | bytes 4000000 | tf_op jit(solution)/shard_map/pallas_call | solution.py:904
  36.9 31.9 %shard_map.106 = f32[16,32,512]{2,1,0:T(8,128)S(1)} custom-call(f32[16,32,512]{2,1,0:T(8,128)S(1)} %bitcast.5, f32[16,32,512]{2,1,0:T(8,128)} %shift_hbm.1, f32[22,40,640]{2,1,0:T(8,128)S(1)} %get-tuple-element.11.inverse, f32[18,32,384]{2,1,0:T(8,128)S(1)} %get-tuple-element.12.cinverse), custom_call_target="tpu_custom_call" | custom-call | tf_op jit(solution)/shard_map/pallas_call | solution.py:450
  68.8 1.0 %copy.12 = f32[16,32,512]{2,1,0:T(8,128)} copy(f32[16,32,512]{2,1,0:T(8,128)S(1)} %shard_map.106) | data formatting | bytes 2097152

commit v9 on v8

--- a/solution.py
+++ b/solution.py
@@ -602,7 +602,7 @@
         rank_ref[:, here] = rank.astype(jnp.int32)
         return carry + (earlier[:, chunk - 1 :] + wide[:, chunk - 1 :])
 
-    lax.fori_loop(0, npoint // chunk, order, carry_ref[...], unroll=4)
+    lax.fori_loop(0, npoint // chunk, order, carry_ref[...], unroll=8)
 
     pl.semaphore_wait(barrier, ndevice - 1)
 
@@ -719,7 +719,7 @@
             jump_ref[:, here] = jnp.sum(force * nrm_ref[:, here], axis=0, keepdims=True)
         return carry
 
-    lax.fori_loop(0, npoint // (2 * LANES), pull, 0, unroll=4)
+    lax.fori_loop(0, npoint // (2 * LANES), pull, 0, unroll=8)
 
     pack(0, lambda here: split3(jump_ref[:, here])[:2])
     send(0)

time: 70 us -> 69.8 us (level)
    pallas_call x1, Pallas kernels: 22.8 us -> 22 us  [front(): pl.pallas_call(functools.partial(front_kernel, ndevice, nbin), in_specs=[...]
where the time goes in v9:
time: 69.8 us; the launch traced here: 69.6 us
  Pallas kernels  68 us (97%)
  local copies, waits for them, and re-layouts  0.97 us (1%)
    pallas_call x1, Pallas kernels, cycle(): pl.pallas_call(cycle_kernel, in_specs=[vmem, pl.BlockSpec(memory_space=pl...  32.5 us
    pallas_call x1, Pallas kernels, front(): pl.pallas_call(functools.partial(front_kernel, ndevice, nbin), in_specs=[...  22 us
    pallas_call x1, Pallas kernels, scatter(): pl.pallas_call(functools.partial(scatter_kernel, nbin), in_specs=[hbm, vm...  13.5 us

profile of v9, /device:TPU:15, one launch (start us, length us, event | category | flops | bytes accessed | tf_op | source)
XLA Modules:
  0.0 69.6 jit_solution(6047956842561754537)
XLA Ops:
  0.6 22.0 %shard_map.104 = (f32[3,8192]{1,0:T(4,128)S(1)}, f32[2,256,128]{2,1,0:T(8,128)S(1)}, f32[22,40,640]{2,1,0:T(8,128)S(1)}, f32[18,32,384]{2,1,0:T(8,128)S(1)}) custom-call(f32[3,8192]{1,0:T(4,128)} %refs_0_.1, f32[3,8192]{1,0:T(4,128)} %refs_1_.1, f32[1,8192]{1,0:T(1,128)} %bitcast.6, f32[6,8192]{1,0:T(8,128)} %refs_3_.1, s32[6,8192]{1,0:T(8,128)} %refs_4_.1, ...), custom_call_target="tpu_custom_call" | custom-call | tf_op jit(solution)/shard_map/pallas_call | solution.py:754
  22.6 13.5 %shard_map.105 = (f32[512,512]{1,0:T(8,128)S(1)}, f32[3,8192]{1,0:T(4,128)}) custom-call(f32[512,512]{1,0:T(8,128)} %bitcast.9, f32[2,256,128]{2,1,0:T(8,128)S(1)} %get-tuple-element.8.got_ref, f32[3,8192]{1,0:T(4,128)S(1)} %get-tuple-element.9.force_ref), custom_call_target="tpu_custom_call" | custom-call | flops 34359738368 | bytes 4000000 | tf_op jit(solution)/shard_map/pallas_call | solution.py:904
  36.1 32.5 %shard_map.106 = f32[16,32,512]{2,1,0:T(8,128)S(1)} custom-call(f32[16,32,512]{2,1,0:T(8,128)S(1)} %bitcast.5, f32[16,32,512]{2,1,0:T(8,128)} %shift_hbm.1, f32[22,40,640]{2,1,0:T(8,128)S(1)} %get-tuple-element.11.inverse, f32[18,32,384]{2,1,0:T(8,128)S(1)} %get-tuple-element.12.cinverse), custom_call_target="tpu_custom_call" | custom-call | tf_op jit(solution)/shard_map/pallas_call | solution.py:450
  68.6 1.0 %copy.12 = f32[16,32,512]{2,1,0:T(8,128)} copy(f32[16,32,512]{2,1,0:T(8,128)S(1)} %shard_map.106) | data formatting | bytes 2097152
